TPU v7x, 32 devices: a whole 2x2x4 slice. The times are simulated.
32 devices in a mesh: seq: 4 (over y, x), dp: 8 (over z, core).
Axes of the slice: x: 2, y: 2, z: 4, core: 2. Of those that a mesh axis runs over, the one named last changes fastest.
Arguments:
- inputs: bfloat16 [8, 512, 2048], P('dp', 'seq'), may hold values from -6 to 6
- first_gain: bfloat16 [2048], P(('seq', 'dp')), may hold values from 0.099609375 to 1.8984375
- first_shift: bfloat16 [2048], P(('seq', 'dp')), may hold values from -2 to 2
- qkv_weight: bfloat16 [2048, 6144], P(('seq', 'dp')), may hold values from -0.125 to 0.125
- qkv_bias: bfloat16 [6144], P(('seq', 'dp')), may hold values from -3 to 3
- out_weight: bfloat16 [2048, 2048], P(('seq', 'dp')), may hold values from -1 to 1
- second_gain: bfloat16 [2048], P(('seq', 'dp')), may hold values from 0.099609375 to 1.8984375
- second_shift: bfloat16 [2048], P(('seq', 'dp')), may hold values from -2 to 2
- gate_weight: bfloat16 [2048, 5632], P(('seq', 'dp')), may hold values from -0.125 to 0.125
- up_weight: bfloat16 [2048, 5632], P(('seq', 'dp')), may hold values from -0.125 to 0.125
- down_weight: bfloat16 [5632, 2048], P(('seq', 'dp')), may hold values from -0.15625 to 0.15625
- out_cotangent: bfloat16 [8, 512, 2048], P('dp', 'seq'), may hold values from -6 to 6
Outputs:
- outputs: bfloat16 [8, 512, 2048], P('dp', 'seq')
- inputs_grad: bfloat16 [8, 512, 2048], P('dp', 'seq')
- first_gain_grad: float32 [2048], P(('seq', 'dp'))
- first_shift_grad: float32 [2048], P(('seq', 'dp'))
- qkv_weight_grad: float32 [2048, 6144], P(('seq', 'dp'))
- qkv_bias_grad: float32 [6144], P(('seq', 'dp'))
- out_weight_grad: float32 [2048, 2048], P(('seq', 'dp'))
- second_gain_grad: float32 [2048], P(('seq', 'dp'))
- second_shift_grad: float32 [2048], P(('seq', 'dp'))
- gate_weight_grad: float32 [2048, 5632], P(('seq', 'dp'))
- up_weight_grad: float32 [2048, 5632], P(('seq', 'dp'))
- down_weight_grad: float32 [5632, 2048], P(('seq', 'dp'))
All inputs are finite; a program needn't handle non-finite values.
Results may differ from a plain program's by a relative error of at most 0.017.
Values may be sent and summed in bfloat16 or wider, within the bound.
A program may use at most 256 MiB of HBM per device.

v0:
```python
import jax
import jax.numpy as jnp
from jax import lax
from jax.sharding import PartitionSpec as P

HEAD_DIM = 64
ROT = 16


def normalize(values):
    center = values - jnp.mean(values, axis=-1, keepdims=True)
    variance = jnp.mean(center * center, axis=-1, keepdims=True)
    inverse = lax.rsqrt(variance + 1e-05)
    return (center * inverse, inverse)


def norm_back(grad_normed, normed, inverse, gain):
    scaled = grad_normed * gain
    centered = scaled - jnp.mean(scaled, axis=-1, keepdims=True)
    return inverse * (centered - normed * jnp.mean(scaled * normed, axis=-1, keepdims=True))


def contract_rows(left, right):
    return lax.dot_general(
        left, right, (((0,), (0,)), ((), ())), preferred_element_type=jnp.float32
    )


def contract_cols(left, right):
    return lax.dot_general(
        left, right, (((1,), (1,)), ((), ())), preferred_element_type=jnp.float32
    )


def tables(positions):
    half_rot = ROT // 2
    freqs = 10000.0 ** (-(2.0 * jnp.arange(half_rot, dtype=jnp.float32)) / ROT)
    angles = positions[:, None] * freqs[None, :]
    cosine = jnp.cos(angles)
    sine = jnp.sin(angles)
    return (jnp.concatenate([cosine, cosine], -1), jnp.concatenate([sine, sine], -1))


def rotate(heads_in, cosine, sine):
    half_rot = ROT // 2
    rotary = heads_in[..., :ROT]
    turned = jnp.concatenate([-rotary[..., half_rot:], rotary[..., :half_rot]], -1)
    moved = rotary * cosine[:, None, :] + turned * sine[:, None, :]
    return jnp.concatenate([moved, heads_in[..., ROT:]], -1)


def shards(
    inputs,
    first_gain,
    first_shift,
    qkv_weight,
    qkv_bias,
    out_weight,
    second_gain,
    second_shift,
    gate_weight,
    up_weight,
    down_weight,
    out_cotangent,
):
    width = inputs.shape[2]
    local_rows = inputs.shape[1]
    hidden_in = inputs[0].astype(jnp.float32)
    qkv_full, qkv_shift, gain_one, shift_one, out_full, gain_two, shift_two = (
        lax.all_gather(qkv_weight, ("seq", "dp"), axis=0, tiled=True),
        lax.all_gather(qkv_bias, ("seq", "dp"), axis=0, tiled=True),
        lax.all_gather(first_gain, ("seq", "dp"), axis=0, tiled=True),
        lax.all_gather(first_shift, ("seq", "dp"), axis=0, tiled=True),
        lax.all_gather(out_weight, ("seq", "dp"), axis=0, tiled=True),
        lax.all_gather(second_gain, ("seq", "dp"), axis=0, tiled=True),
        lax.all_gather(second_shift, ("seq", "dp"), axis=0, tiled=True),
    )
    gain_one = gain_one.astype(jnp.float32)
    shift_one = shift_one.astype(jnp.float32)
    gain_two = gain_two.astype(jnp.float32)
    shift_two = shift_two.astype(jnp.float32)
    normed_one, inverse_one = normalize(hidden_in)
    attn_input = (normed_one * gain_one + shift_one).astype(jnp.bfloat16)
    projected = jnp.dot(
        attn_input, qkv_full, preferred_element_type=jnp.float32
    ) + qkv_shift.astype(jnp.float32)
    first_row = lax.axis_index("seq") * local_rows
    positions = (first_row + jnp.arange(local_rows, dtype=jnp.int32)).astype(jnp.float32)
    cosine, sine = tables(positions)

    def to_heads(flat_part):
        return flat_part.reshape(local_rows, width // HEAD_DIM, HEAD_DIM)

    queries = (
        rotate(to_heads(projected[:, :width]), cosine, sine)
        .reshape(local_rows, width)
        .astype(jnp.bfloat16)
    )
    keys_local = (
        rotate(to_heads(projected[:, width : 2 * width]), cosine, sine)
        .reshape(local_rows, width)
        .astype(jnp.bfloat16)
    )
    values_local = projected[:, 2 * width :].astype(jnp.bfloat16)
    head_queries, head_keys, head_values = (
        lax.all_to_all(queries, "seq", split_axis=1, concat_axis=0, tiled=True),
        lax.all_to_all(keys_local, "seq", split_axis=1, concat_axis=0, tiled=True),
        lax.all_to_all(values_local, "seq", split_axis=1, concat_axis=0, tiled=True),
    )
    seq_length = head_queries.shape[0]
    local_heads = head_queries.shape[1] // HEAD_DIM
    queries_heads = head_queries.reshape(seq_length, local_heads, HEAD_DIM)
    keys_heads = head_keys.reshape(seq_length, local_heads, HEAD_DIM)
    values_heads = head_values.reshape(seq_length, local_heads, HEAD_DIM)
    block_rows = min(512, seq_length)
    blocks = seq_length // block_rows
    scale = HEAD_DIM ** (-0.5)
    key_index = jnp.arange(seq_length, dtype=jnp.int32)

    def scores_of(block_index):
        first_query = block_index * block_rows
        query_block = lax.dynamic_slice_in_dim(queries_heads, first_query, block_rows, 0)
        scores = (
            jnp.einsum("qhd,khd->hqk", query_block, keys_heads, preferred_element_type=jnp.float32)
            * scale
        )
        query_index = first_query + jnp.arange(block_rows, dtype=jnp.int32)
        allowed = key_index[None, None, :] <= query_index[None, :, None]
        return (query_block, jnp.where(allowed, scores, -jnp.inf))

    def forward_block(block_index):
        query_block, scores = scores_of(block_index)
        largest = jnp.max(scores, axis=-1, keepdims=True)
        exponent = jnp.exp(scores - largest)
        totals = jnp.sum(exponent, axis=-1, keepdims=True)
        probs_low = (exponent / totals).astype(jnp.bfloat16)
        mixed = jnp.einsum(
            "hqk,khd->qhd", probs_low, values_heads, preferred_element_type=jnp.float32
        )
        return (mixed, (largest + jnp.log(totals))[..., 0])

    block_ids = jnp.arange(blocks, dtype=jnp.int32)
    mixed_blocks, log_totals = lax.map(forward_block, block_ids)
    attended_heads = mixed_blocks.reshape(seq_length, local_heads * HEAD_DIM).astype(jnp.bfloat16)
    attended = lax.all_to_all(attended_heads, "seq", split_axis=0, concat_axis=1, tiled=True)
    residual = hidden_in + jnp.dot(attended, out_full, preferred_element_type=jnp.float32)
    normed_two, inverse_two = normalize(residual)
    mlp_input = (normed_two * gain_two + shift_two).astype(jnp.bfloat16)
    gate_full, up_full, down_full = (
        lax.all_gather(gate_weight, ("seq", "dp"), axis=0, tiled=True),
        lax.all_gather(up_weight, ("seq", "dp"), axis=0, tiled=True),
        lax.all_gather(down_weight, ("seq", "dp"), axis=0, tiled=True),
    )
    gate_value = jnp.dot(mlp_input, gate_full, preferred_element_type=jnp.float32)
    up_value = jnp.dot(mlp_input, up_full, preferred_element_type=jnp.float32)
    activated = jax.nn.silu(gate_value)
    hidden = (activated * up_value).astype(jnp.bfloat16)
    layer_out = residual + jnp.dot(hidden, down_full, preferred_element_type=jnp.float32)
    grad_out = out_cotangent[0]
    gate_back, up_back, down_back = (gate_full, up_full, down_full)
    hidden_grad = contract_cols(grad_out, down_back)
    sigmoid_gate = jax.nn.sigmoid(gate_value)
    gate_grad_act = (
        hidden_grad * up_value * (sigmoid_gate * (1.0 + gate_value * (1.0 - sigmoid_gate)))
    ).astype(jnp.bfloat16)
    up_grad_act = (hidden_grad * activated).astype(jnp.bfloat16)
    mlp_input_grad = contract_cols(gate_grad_act, gate_back) + contract_cols(up_grad_act, up_back)
    gain_two_grad = jnp.sum(mlp_input_grad * normed_two, axis=0)
    shift_two_grad = jnp.sum(mlp_input_grad, axis=0)
    residual_grad = grad_out.astype(jnp.float32) + norm_back(
        mlp_input_grad, normed_two, inverse_two, gain_two
    )
    branch_grad = residual_grad.astype(jnp.bfloat16)
    qkv_back, out_back = (qkv_full, out_full)
    attended_grad = contract_cols(branch_grad, out_back).astype(jnp.bfloat16)
    head_grad = lax.all_to_all(
        attended_grad, "seq", split_axis=1, concat_axis=0, tiled=True
    ).reshape(seq_length, local_heads, HEAD_DIM)

    def backward_block(carry, item):
        keys_grad, values_grad = carry
        block_index, log_total = item
        query_block, scores = scores_of(block_index)
        probs = jnp.exp(scores - log_total[..., None])
        grad_block = lax.dynamic_slice_in_dim(head_grad, block_index * block_rows, block_rows, 0)
        values_grad = values_grad + jnp.einsum(
            "hqk,qhd->khd",
            probs.astype(jnp.bfloat16),
            grad_block,
            preferred_element_type=jnp.float32,
        )
        probs_grad = jnp.einsum(
            "qhd,khd->hqk", grad_block, values_heads, preferred_element_type=jnp.float32
        )
        scores_grad = (
            probs * (probs_grad - jnp.sum(probs * probs_grad, axis=-1, keepdims=True))
        ).astype(jnp.bfloat16)
        query_grad = (
            jnp.einsum("hqk,khd->qhd", scores_grad, keys_heads, preferred_element_type=jnp.float32)
            * scale
        )
        keys_grad = (
            keys_grad
            + jnp.einsum(
                "hqk,qhd->khd", scores_grad, query_block, preferred_element_type=jnp.float32
            )
            * scale
        )
        return ((keys_grad, values_grad), query_grad)

    zero_heads = jnp.zeros((seq_length, local_heads, HEAD_DIM), jnp.float32)
    (keys_grad, values_grad), query_blocks = lax.scan(
        backward_block, (zero_heads, zero_heads), (block_ids, log_totals)
    )
    flat_shape = (seq_length, local_heads * HEAD_DIM)
    query_back, key_back, value_back = (
        lax.all_to_all(
            query_blocks.reshape(flat_shape).astype(jnp.bfloat16),
            "seq",
            split_axis=0,
            concat_axis=1,
            tiled=True,
        ),
        lax.all_to_all(
            keys_grad.reshape(flat_shape).astype(jnp.bfloat16),
            "seq",
            split_axis=0,
            concat_axis=1,
            tiled=True,
        ),
        lax.all_to_all(
            values_grad.reshape(flat_shape).astype(jnp.bfloat16),
            "seq",
            split_axis=0,
            concat_axis=1,
            tiled=True,
        ),
    )
    query_plain = rotate(to_heads(query_back.astype(jnp.float32)), cosine, -sine).reshape(
        local_rows, width
    )
    key_plain = rotate(to_heads(key_back.astype(jnp.float32)), cosine, -sine).reshape(
        local_rows, width
    )
    projected_grad = jnp.concatenate(
        [query_plain, key_plain, value_back.astype(jnp.float32)], axis=1
    ).astype(jnp.bfloat16)
    qkv_bias_term = jnp.sum(projected_grad.astype(jnp.float32), axis=0)
    attn_input_grad = contract_cols(projected_grad, qkv_back)
    gain_one_grad = jnp.sum(attn_input_grad * normed_one, axis=0)
    shift_one_grad = jnp.sum(attn_input_grad, axis=0)
    input_grad = residual_grad + norm_back(attn_input_grad, normed_one, inverse_one, gain_one)
    cols_attn, cols_attended, cols_mlp, cols_hidden = (
        lax.all_to_all(attn_input, "seq", split_axis=1, concat_axis=0, tiled=True),
        lax.all_to_all(attended, "seq", split_axis=1, concat_axis=0, tiled=True),
        lax.all_to_all(mlp_input, "seq", split_axis=1, concat_axis=0, tiled=True),
        lax.all_to_all(hidden, "seq", split_axis=1, concat_axis=0, tiled=True),
    )
    rows_grad_out, rows_gate, rows_up, rows_proj, rows_branch = (
        lax.all_gather(grad_out, "seq", axis=0, tiled=True),
        lax.all_gather(gate_grad_act, "seq", axis=0, tiled=True),
        lax.all_gather(up_grad_act, "seq", axis=0, tiled=True),
        lax.all_gather(projected_grad, "seq", axis=0, tiled=True),
        lax.all_gather(branch_grad, "seq", axis=0, tiled=True),
    )
    gate_rows = contract_rows(cols_mlp, rows_gate)
    up_rows = contract_rows(cols_mlp, rows_up)
    down_rows = contract_rows(cols_hidden, rows_grad_out)
    qkv_rows = contract_rows(cols_attn, rows_proj)
    out_rows = contract_rows(cols_attended, rows_branch)
    gate_shard, up_shard, down_shard, qkv_shard, out_shard = (
        lax.psum_scatter(
            gate_rows.astype(jnp.bfloat16), "dp", scatter_dimension=0, tiled=True
        ).astype(jnp.float32),
        lax.psum_scatter(
            up_rows.astype(jnp.bfloat16), "dp", scatter_dimension=0, tiled=True
        ).astype(jnp.float32),
        lax.psum_scatter(
            down_rows.astype(jnp.bfloat16), "dp", scatter_dimension=0, tiled=True
        ).astype(jnp.float32),
        lax.psum_scatter(
            qkv_rows.astype(jnp.bfloat16), "dp", scatter_dimension=0, tiled=True
        ).astype(jnp.float32),
        lax.psum_scatter(
            out_rows.astype(jnp.bfloat16), "dp", scatter_dimension=0, tiled=True
        ).astype(jnp.float32),
    )
    gain_one_shard, shift_one_shard, qkv_bias_shard, gain_two_shard, shift_two_shard = (
        lax.psum_scatter(gain_one_grad, ("seq", "dp"), scatter_dimension=0, tiled=True),
        lax.psum_scatter(shift_one_grad, ("seq", "dp"), scatter_dimension=0, tiled=True),
        lax.psum_scatter(qkv_bias_term, ("seq", "dp"), scatter_dimension=0, tiled=True),
        lax.psum_scatter(gain_two_grad, ("seq", "dp"), scatter_dimension=0, tiled=True),
        lax.psum_scatter(shift_two_grad, ("seq", "dp"), scatter_dimension=0, tiled=True),
    )
    return (
        layer_out.astype(jnp.bfloat16)[None],
        input_grad.astype(jnp.bfloat16)[None],
        gain_one_shard,
        shift_one_shard,
        qkv_shard,
        qkv_bias_shard,
        out_shard,
        gain_two_shard,
        shift_two_shard,
        gate_shard,
        up_shard,
        down_shard,
    )


def solution(mesh):
    in_specs = (
        P("dp", "seq", None),
        P(("seq", "dp")),
        P(("seq", "dp")),
        P(("seq", "dp"), None),
        P(("seq", "dp")),
        P(("seq", "dp"), None),
        P(("seq", "dp")),
        P(("seq", "dp")),
        P(("seq", "dp"), None),
        P(("seq", "dp"), None),
        P(("seq", "dp"), None),
        P("dp", "seq", None),
    )
    out_specs = (
        P("dp", "seq", None),
        P("dp", "seq", None),
        P(("seq", "dp")),
        P(("seq", "dp")),
        P(("seq", "dp"), None),
        P(("seq", "dp")),
        P(("seq", "dp"), None),
        P(("seq", "dp")),
        P(("seq", "dp")),
        P(("seq", "dp"), None),
        P(("seq", "dp"), None),
        P(("seq", "dp"), None),
    )
    return jax.shard_map(shards, mesh=mesh, in_specs=in_specs, out_specs=out_specs, check_vma=False)
```

profile of v0, /device:TPU:0, one launch (start us, length us, event | category | flops | bytes accessed | tf_op | source)
XLA Modules:
  0.0 1366.9 jit_solution(5567357706465428928)
XLA Ops:
  14.8 44.0 %all-reduce.11 = (bf16[6144]{0:T(1024)(128)(2,1)S(1)}, bf16[2048]{0:T(1024)(128)(2,1)S(1)}, bf16[2048]{0:T(1024)(128)(2,1)S(1)}, bf16[2048]{0:T(1024)(128)(2,1)S(1)}, bf16[2048]{0:T(1024)(128)(2,1)S(1)}) all-reduce(bf16[6144]{0:T(1024)(128)(2,1)S(1)} %dynamic-update-slice.2, ...), channel_id=1, replica_groups=mesh['seq'=4,'dp'=8] {'seq','dp'}, use_global_device_ids=true, to_apply=%add.2 | all-reduce | flops 14336 | bytes 57344
  62.2 107.0 %all-gather.12.cloned.1.call-done = bf16[2048,6144]{1,0:T(8,128)(2,1)} async-done(((bf16[64,6144]{1,0:T(8,128)(2,1)}), bf16[2048,6144]{1,0:T(8,128)(2,1)}) %all-gather.12.cloned.1.call-update) | async-done | bytes 25165840 | tf_op jit(solution)/shard_map/all_gather | solution.py:70
  169.2 10.3 convolution_add_fusion
  181.0 2.5 copy.71
  183.5 2.5 copy.73
  190.4 4.1 all-to-all-start.2
  196.6 11.7 all-to-all-done.2
  208.4 4.1 all-to-all-start.1
  213.4 5.7 all-to-all-done.1
  219.2 4.1 all-to-all-start
  226.8 10.0 all-to-all-done
  240.1 2.1 copy-done
  244.8 3.5 all-to-all-start.3
  248.5 7.0 all-gather.14.cloned.1.call-done
  255.5 4.9 fusion.46
  261.0 140.7 %all-gather.16.cloned.1.call-done = bf16[2048,5632]{1,0:T(8,128)(2,1)} async-done(((bf16[64,5632]{1,0:T(8,128)(2,1)}), bf16[2048,5632]{1,0:T(8,128)(2,1)}) %all-gather.16.cloned.1.call-update) | async-done | bytes 23068688 | tf_op jit(solution)/shard_map/all_gather | solution.py:150
  401.7 12.4 fusion.47
  414.1 132.4 %all-gather.18.cloned.1.call-done = bf16[2048,5632]{1,0:T(8,128)(2,1)} async-done(((bf16[64,5632]{1,0:T(8,128)(2,1)}), bf16[2048,5632]{1,0:T(8,128)(2,1)}) %all-gather.18.cloned.1.call-update) | async-done | bytes 23068688 | tf_op jit(solution)/shard_map/all_gather | solution.py:151
  546.5 12.3 fusion.48
  558.8 132.5 %all-gather.20.cloned.1.call-done = bf16[5632,2048]{1,0:T(8,128)(2,1)} async-done(((bf16[176,2048]{1,0:T(8,128)(2,1)}), bf16[5632,2048]{1,0:T(8,128)(2,1)}) %all-gather.20.cloned.1.call-update) | async-done | bytes 23068688 | tf_op jit(solution)/shard_map/all_gather | solution.py:152
  691.3 15.1 %multiply_convert_fusion.1 = (bf16[128,5632]{1,0:T(8,128)(2,1)S(1)}, bf16[128,5632]{1,0:T(8,128)(2,1)}, bf16[128,5632]{1,0:T(8,128)(2,1)}) fusion(f32[128,5632]{1,0:T(8,128)} %fusion.47, f32[128,5632]{1,0:T(8,128)} %fusion.48, bf16[5632,2048]{1,0:T(8,128)(2,1)} %all-gather.20.cloned.1.call-done, bf16[1,128,2048]{2,1,0:T(8,128)(2,1)} %param.23), kind=kOutput, calls=%fused_computation.18 | convolution fusion | flops 2963603456 | bytes 33685504 | tf_op jit(solution)/shard_map/dot_general | solution.py:30
  706.4 13.5 fusion.49
  719.9 13.4 multiply_reduce_fusion.1
  737.9 6.8 convolution_convert_fusion.5
  745.5 3.7 all-to-all-start.4
  749.3 9.0 all-to-all-done.4
  760.6 5.5 multiply_reduce_fusion
  766.1 4.5 multiply_convert_fusion
  770.6 1.9 copy-done.1
  774.1 2.0 convert_element_type.217
  776.1 1.9 copy.80
  778.0 4.1 all-to-all-start.5
  782.2 4.4 fusion.16
  788.6 4.2 all-to-all-done.5
  792.8 3.5 all-to-all-start.6
  796.3 5.9 fusion.18
  804.3 2.1 convert_element_type.220
  809.4 3.5 all-to-all-start.7
  820.9 3.4 convert_reduce_fusion
  824.4 17.7 %all_to_all.174 = bf16[128,4,512]{0,2,1:T(8,128)(2,1)} all-to-all(bf16[128,4,512]{0,2,1:T(8,128)(2,1)S(1)} %bitcast.144), channel_id=1, replica_groups=mesh['seq'=4,'dp'=8] {'seq'}, dimensions={1} | all-to-all | bytes 1048576 | tf_op jit(solution)/shard_map/all_to_all | solution.py:255
  842.1 2.2 copy.86
  844.2 4.4 convolution_convert_fusion.4
  849.9 3.5 all-to-all-start.11
  854.0 28.6 %all-to-all-done.11 = bf16[128,4,1408]{2,0,1:T(8,128)(2,1)S(1)} async-done(((bf16[128,4,1408]{2,0,1:T(8,128)(2,1)}), bf16[128,4,1408]{2,0,1:T(8,128)(2,1)S(1)}, u32[]{:S(2)}, u32[]{:S(2)}) %all-to-all-start.11) | async-done | bytes 1441824 | tf_op jit(solution)/shard_map/all_to_all | solution.py:257
  882.5 7.3 convolution_convert_fusion.3
  889.9 14.7 %all_to_all.175 = bf16[128,4,512]{2,0,1:T(8,128)(2,1)S(1)} all-to-all(bf16[128,4,512]{2,0,1:T(8,128)(2,1)S(1)} %bitcast.166), channel_id=1, replica_groups=mesh['seq'=4,'dp'=8] {'seq'}, dimensions={1} | all-to-all | bytes 1048576 | tf_op jit(solution)/shard_map/all_to_all | solution.py:256
  904.8 7.6 convolution_convert_fusion.1
  912.5 61.1 %all-gather.28.cloned.1.call-done = bf16[512,5632]{1,0:T(8,128)(2,1)} async-done(((bf16[128,5632]{1,0:T(8,128)(2,1)}), bf16[512,5632]{1,0:T(8,128)(2,1)}) %all-gather.28.cloned.1.call-update) | async-done | bytes 5767184 | tf_op jit(solution)/shard_map/all_gather | solution.py:262
  973.6 7.6 convolution_convert_fusion
  983.2 17.2 %all_to_all.176 = bf16[128,4,512]{2,0,1:T(8,128)(2,1)S(1)} all-to-all(bf16[128,4,512]{2,0,1:T(8,128)(2,1)S(1)} %fusion.25), channel_id=1, replica_groups=mesh['seq'=4,'dp'=8] {'seq'}, dimensions={1} | all-to-all | bytes 1048576 | tf_op jit(solution)/shard_map/all_to_all | solution.py:254
  1000.4 50.9 %all-gather.22.cloned.1.call-done = bf16[512,6144]{0,1:T(8,128)(2,1)} async-done(((bf16[128,6144]{0,1:T(8,128)(2,1)}), bf16[512,6144]{0,1:T(8,128)(2,1)}) %all-gather.22.cloned.1.call-update) | async-done | bytes 6291472 | tf_op jit(solution)/shard_map/all_gather | solution.py:263
  1051.4 8.2 convolution_convert_fusion.2
  1059.6 12.2 fusion.8
  1071.8 13.5 multiply_reduce_fusion.2
  1085.4 42.1 %all-reduce.10 = (f32[2048]{0:T(1024)S(1)}, f32[2048]{0:T(1024)S(1)}, f32[6144]{0:T(1024)S(1)}, f32[2048]{0:T(1024)S(1)}, f32[2048]{0:T(1024)S(1)}) all-reduce(f32[2048]{0:T(1024)S(1)} %get-tuple-element.55, f32[2048]{0:T(1024)S(1)} %get-tuple-element.70, ...), channel_id=3, replica_groups=mesh['seq'=4,'dp'=8] {'seq','dp'}, use_global_device_ids=true, to_apply=%region_12.13.clone | all-reduce | flops 14336 | bytes 114688
  1130.4 2.5 fusion.27
  1134.7 21.7 %reduce-scatter.14.cloned.1.call-done = bf16[176,2048]{1,0:T(8,128)(2,1)} async-done(((bf16[1408,2048]{1,0:T(8,128)(2,1)}), bf16[176,2048]{1,0:T(8,128)(2,1)}) %reduce-scatter.14.cloned.1.call-update) | async-done | bytes 720912 | tf_op jit(solution)/shard_map/reduce_scatter | solution.py:278
  1156.4 2.4 convert_element_type.247
  1158.8 63.2 %reduce-scatter.10.cloned.1.call-done = bf16[64,5632]{1,0:T(8,128)(2,1)} async-done(((bf16[512,5632]{1,0:T(8,128)(2,1)}), bf16[64,5632]{1,0:T(8,128)(2,1)}) %reduce-scatter.10.cloned.1.call-update) | async-done | bytes 720912 | tf_op jit(solution)/shard_map/reduce_scatter | solution.py:272
  1222.0 2.3 convert_element_type.243
  1224.3 63.1 %reduce-scatter.12.cloned.1.call-done = bf16[64,5632]{1,0:T(8,128)(2,1)} async-done(((bf16[512,5632]{1,0:T(8,128)(2,1)}), bf16[64,5632]{1,0:T(8,128)(2,1)}) %reduce-scatter.12.cloned.1.call-update) | async-done | bytes 720912 | tf_op jit(solution)/shard_map/reduce_scatter | solution.py:275
  1287.4 2.3 convert_element_type.245
  1289.7 68.1 %reduce-scatter.6.cloned.1.call-done = bf16[64,6144]{1,0:T(8,128)(2,1)} async-done(((bf16[512,6144]{1,0:T(8,128)(2,1)}), bf16[64,6144]{1,0:T(8,128)(2,1)}) %reduce-scatter.6.cloned.1.call-update) | async-done | bytes 786448 | tf_op jit(solution)/shard_map/reduce_scatter | solution.py:281
  1357.8 2.4 convert_element_type.238
  (197 shorter events, 63.0 us)
Async XLA Ops:
  7.2 162.1 %all-gather.12.cloned.1.call-start = ((), (), s32[]{:S(2)}) async-start(), calls=%async_computation.17 | async-start | bytes 25952256 | tf_op jit(solution)/shard_map/all_gather | solution.py:70
  7.9 247.6 %all-gather.14.cloned.1.call-start = ((), (), s32[]{:S(2)}) async-start(), calls=%async_computation.18 | async-start | bytes 8650752 | tf_op jit(solution)/shard_map/all_gather | solution.py:74
  8.7 393.0 %all-gather.16.cloned.1.call-start = ((), (), s32[]{:S(2)}) async-start(), calls=%async_computation.19 | async-start | bytes 23789568 | tf_op jit(solution)/shard_map/all_gather | solution.py:150
  9.4 537.1 %all-gather.18.cloned.1.call-start = ((), (), s32[]{:S(2)}) async-start(), calls=%async_computation.20 | async-start | bytes 23789568 | tf_op jit(solution)/shard_map/all_gather | solution.py:151
  10.0 681.3 %all-gather.20.cloned.1.call-start = ((), (), s32[]{:S(2)}) async-start(), calls=%async_computation.21 | async-start | bytes 23789568 | tf_op jit(solution)/shard_map/all_gather | solution.py:152
  58.8 0.8 copy-start.31
  58.8 3.3 copy-start.29
  59.6 128.8 %copy-start.21 = (f32[128,16]{0,1:T(8,128)}, f32[128,16]{0,1:T(8,128)S(1)}, u32[]{:S(2)}) copy-start(f32[128,16]{0,1:T(8,128)S(1)} %get-tuple-element.110) | copy-start | bytes 24580
  60.8 118.7 %copy-start.27 = (f32[128]{0:T(128)}, f32[128]{0:T(128)S(1)}, u32[]{:S(2)}) copy-start(f32[128]{0:T(128)S(1)} %broadcast_multiply_fusion.5) | copy-start | bytes 1540
  62.2 117.4 %copy-start.33 = (f32[128]{0:T(128)}, f32[128]{0:T(128)S(1)}, u32[]{:S(2)}) copy-start(f32[128]{0:T(128)S(1)} %add_rsqrt_fusion.1) | copy-start | bytes 1540
  190.4 18.0 %all-to-all-start.2 = ((bf16[128,4,512]{0,2,1:T(8,128)(2,1)}), bf16[128,4,512]{0,2,1:T(8,128)(2,1)}, u32[]{:S(2)}, u32[]{:S(2)}) async-start(bf16[128,4,512]{0,2,1:T(8,128)(2,1)} %bitcast.161), calls=%async_computation.2 | async-start | bytes 1048576 | tf_op jit(solution)/shard_map/all_to_all | solution.py:107
  208.4 10.8 all-to-all-start.1
  219.2 17.7 %all-to-all-start = ((bf16[128,4,512]{2,0,1:T(8,128)(2,1)}), bf16[128,4,512]{2,0,1:T(8,128)(2,1)S(1)}, u32[]{:S(2)}, u32[]{:S(2)}) async-start(bf16[128,4,512]{2,0,1:T(8,128)(2,1)} %bitcast.141), calls=%async_computation | async-start | bytes 1048576 | tf_op jit(solution)/shard_map/all_to_all | solution.py:108
  225.0 13.9 %copy-start.10 = (bf16[512,8,64]{0,2,1:T(8,128)(2,1)}, bf16[512,8,64]{0,2,1:T(8,128)(2,1)S(1)}, u32[]{:S(2)}) copy-start(bf16[512,8,64]{0,2,1:T(8,128)(2,1)S(1)} %reshape.270) | copy-start | bytes 1572868
  226.8 12.0 copy-start.8
  237.3 2.7 copy-start.15
  238.9 3.4 copy-start
  238.9 4.9 copy-start.18
  242.2 1.6 copy-start.23
  242.2 13.3 copy-start.2
  244.8 10.7 all-to-all-start.3
  248.3 595.9 %all-gather.24.cloned.1.call-start = ((), (), s32[]{:S(2)}) async-start(), calls=%async_computation.24 | async-start | bytes 2621440 | tf_op jit(solution)/shard_map/all_gather | solution.py:264
  255.5 4.9 copy-start.5
  260.5 153.6 %copy-start.35 = (f32[128]{0:T(128)}, f32[128]{0:T(128)S(1)}, u32[]{:S(2)}) copy-start(f32[128]{0:T(128)S(1)} %broadcast_multiply_fusion.4) | copy-start | bytes 1540
  260.7 153.3 %copy-start.37 = (f32[128]{0:T(128)}, f32[128]{0:T(128)S(1)}, u32[]{:S(2)}) copy-start(f32[128]{0:T(128)S(1)} %add_rsqrt_fusion) | copy-start | bytes 1540
  706.4 13.5 copy-start.4
  719.9 14.0 %copy-start.17 = (bf16[1,128,2048]{2,1,0:T(8,128)(2,1)S(1)}, bf16[1,128,2048]{2,1,0:T(8,128)(2,1)}, u32[]{:S(2)}) copy-start(bf16[1,128,2048]{2,1,0:T(8,128)(2,1)} %param.23) | copy-start | bytes 1572868
  719.9 14.0 %copy-start.36 = (f32[128]{0:T(128)S(1)}, f32[128]{0:T(128)}, u32[]{:S(2)}) copy-start(f32[128]{0:T(128)} %copy-done.35) | copy-start | bytes 1540
  719.9 14.0 %copy-start.38 = (f32[128]{0:T(128)S(1)}, f32[128]{0:T(128)}, u32[]{:S(2)}) copy-start(f32[128]{0:T(128)} %copy-done.37) | copy-start | bytes 1540
  735.6 118.3 %all-gather.30.cloned.1.call-start = ((), (), s32[]{:S(2)}) async-start(), calls=%async_computation.31 | async-start | bytes 2621440 | tf_op jit(solution)/shard_map/all_gather | solution.py:260
  736.4 168.4 %all-gather.26.cloned.1.call-start = ((), (), s32[]{:S(2)}) async-start(), calls=%async_computation.26 | async-start | bytes 7208960 | tf_op jit(solution)/shard_map/all_gather | solution.py:261
  737.1 236.4 %all-gather.28.cloned.1.call-start = ((), (), s32[]{:S(2)}) async-start(), calls=%async_computation.28 | async-start | bytes 7208960 | tf_op jit(solution)/shard_map/all_gather | solution.py:262
  737.9 11.4 copy-start.19
  737.9 11.4 copy-start.24
  737.9 22.7 %copy-start.16 = (bf16[512,8,64]{0,2,1:T(8,128)(2,1)S(1)}, bf16[512,8,64]{0,2,1:T(8,128)(2,1)}, u32[]{:S(2)}) copy-start(bf16[512,8,64]{0,2,1:T(8,128)(2,1)} %copy-done.15) | copy-start | bytes 1572868
  745.5 12.7 all-to-all-start.4
  760.6 5.5 copy-start.12
  766.1 6.5 copy-start.11
  770.6 1.9 copy-start.1
  772.5 9.7 copy-start.9
  774.1 22.2 %copy-start.13 = (bf16[512,8,64]{0,2,1:T(8,128)(2,1)S(1)}, bf16[512,8,64]{0,2,1:T(8,128)(2,1)}, u32[]{:S(2)}) copy-start(bf16[512,8,64]{0,2,1:T(8,128)(2,1)} %copy-done.12) | copy-start | bytes 1572868
  778.0 14.8 %all-to-all-start.5 = ((bf16[4,128,512]{1,2,0:T(8,128)(2,1)}), bf16[4,128,512]{1,2,0:T(8,128)(2,1)}, u32[]{:S(2)}, u32[]{:S(2)}) async-start(bf16[4,128,512]{1,2,0:T(8,128)(2,1)} %copy.80), calls=%async_computation.5 | async-start | bytes 1048576 | tf_op jit(solution)/shard_map/all_to_all | solution.py:217
  792.8 16.5 %all-to-all-start.6 = ((bf16[4,128,512]{1,2,0:T(8,128)(2,1)}), bf16[4,128,512]{1,2,0:T(8,128)(2,1)S(1)}, u32[]{:S(2)}, u32[]{:S(2)}) async-start(bf16[4,128,512]{1,2,0:T(8,128)(2,1)} %copy.82), calls=%async_computation.6 | async-start | bytes 1048576 | tf_op jit(solution)/shard_map/all_to_all | solution.py:224
  802.2 15.7 %copy-start.22 = (f32[128,16]{0,1:T(8,128)S(1)}, f32[128,16]{0,1:T(8,128)}, u32[]{:S(2)}) copy-start(f32[128,16]{0,1:T(8,128)} %copy-done.21) | copy-start | bytes 24580
  809.4 3.5 copy-start.14
  809.4 11.5 all-to-all-start.7
  812.8 238.5 %all-gather.22.cloned.1.call-start = ((), (), s32[]{:S(2)}) async-start(), calls=%async_computation.22 | async-start | bytes 7864320 | tf_op jit(solution)/shard_map/all_gather | solution.py:263
  812.9 11.5 copy-start.6
  824.3 308.6 %reduce-scatter.8.cloned.1.call-start = ((), (), s32[]{:S(2)}) async-start(), calls=%async_computation.25 | async-start | bytes 2359296 | tf_op jit(solution)/shard_map/reduce_scatter | solution.py:284
  842.1 6.6 copy-start.7
  849.9 32.7 %all-to-all-start.11 = ((bf16[128,4,1408]{2,0,1:T(8,128)(2,1)}), bf16[128,4,1408]{2,0,1:T(8,128)(2,1)S(1)}, u32[]{:S(2)}, u32[]{:S(2)}) async-start(bf16[128,4,1408]{2,0,1:T(8,128)(2,1)} %bitcast.146), calls=%async_computation.15 | async-start | bytes 2883584 | tf_op jit(solution)/shard_map/all_to_all | solution.py:257
  853.4 303.0 %reduce-scatter.14.cloned.1.call-start = ((), (), s32[]{:S(2)}) async-start(), calls=%async_computation.30 | async-start | bytes 6488064 | tf_op jit(solution)/shard_map/reduce_scatter | solution.py:278
  889.8 332.2 %reduce-scatter.10.cloned.1.call-start = ((), (), s32[]{:S(2)}) async-start(), calls=%async_computation.27 | async-start | bytes 6488064 | tf_op jit(solution)/shard_map/reduce_scatter | solution.py:272
  912.5 374.9 %reduce-scatter.12.cloned.1.call-start = ((), (), s32[]{:S(2)}) async-start(), calls=%async_computation.29 | async-start | bytes 6488064 | tf_op jit(solution)/shard_map/reduce_scatter | solution.py:275
  981.2 0.7 copy-start.32
  981.2 0.7 copy-start.30
  981.2 1.5 copy-start.28
  981.2 1.5 copy-start.34
  981.2 376.6 %reduce-scatter.6.cloned.1.call-start = ((), (), s32[]{:S(2)}) async-start(), calls=%async_computation.23 | async-start | bytes 7077888 | tf_op jit(solution)/shard_map/reduce_scatter | solution.py:281
  1059.6 12.2 copy-start.3
  1071.8 13.5 copy-start.20
  1071.8 13.5 copy-start.25
  1071.8 13.6 copy-start.26
Sparse Core Ops, SparseCore 0:
  11.0 158.1 all-gather.11
  172.2 83.2 all-gather.13
  258.4 143.2 all-gather.15
  404.4 142.0 all-gather.17
  549.2 142.0 all-gather.19
  735.8 33.5 all-gather.23
  771.2 45.8 all-gather.29
  819.5 85.2 all-gather.25
  907.3 66.2 all-gather.27
  975.8 75.4 all-gather.21
  1053.7 36.0 reduce-scatter.7
  1091.9 64.4 reduce-scatter.13
  1158.7 63.2 reduce-scatter.9
  1224.2 63.2 reduce-scatter.11
  1289.6 68.1 reduce-scatter.5
where the time goes:
time: 1370 us
  waiting for transfers between devices  924 us (67%)
  matrix products  170 us (12%)
  blocking collectives  136 us (10%)
  local copies, waits for them, and re-layouts  46.6 us (3%)
  other arithmetic  40.5 us (3%)
  starting transfers between devices  35.4 us (3%)
  between operations  14.9 us (1%)
    all_gather x1, waiting for transfers between devices, shards(): lax.all_gather(gate_weight, ('seq', 'dp'), axis=0, tiled=True)  141 us
    all_gather x1, waiting for transfers between devices, shards(): lax.all_gather(down_weight, ('seq', 'dp'), axis=0, tiled=True)  133 us
    all_gather x1, waiting for transfers between devices, shards(): lax.all_gather(up_weight, ('seq', 'dp'), axis=0, tiled=True)  132 us
    all_gather x1, waiting for transfers between devices, shards(): lax.all_gather(qkv_weight, ('seq', 'dp'), axis=0, tiled=True)  107 us
    unnamed x2, blocking collectives  86.1 us
    reduce_scatter x1, waiting for transfers between devices, shards(): lax.psum_scatter(qkv_rows.astype(jnp.bfloat16), 'dp', scatter_dimension=0...  68.1 us
    reduce_scatter x1, waiting for transfers between devices, shards(): lax.psum_scatter(gate_rows.astype(jnp.bfloat16), 'dp', scatter_dimension=...  63.2 us
    reduce_scatter x1, waiting for transfers between devices, shards(): lax.psum_scatter(up_rows.astype(jnp.bfloat16), 'dp', scatter_dimension=0,...  63.1 us
  transfers between devices with their start and end apart: 24, of which 20 were waited for; matrix products, arithmetic and copies ran while one was open for 15% of the time, Pallas kernels for 0%

commit v1 on v0

v1 whole, which is shorter than its diff:
```python
import jax
import jax.numpy as jnp
from jax import lax
from jax.sharding import PartitionSpec as P

HEAD_DIM = 64
ROT = 16
F32 = jnp.float32
BF16 = jnp.bfloat16


def normalize(values):
    center = values - jnp.mean(values, axis=-1, keepdims=True)
    variance = jnp.mean(center * center, axis=-1, keepdims=True)
    inverse = lax.rsqrt(variance + 1e-05)
    return (center * inverse, inverse)


def norm_back(grad_normed, normed, inverse, gain):
    scaled = grad_normed * gain
    centered = scaled - jnp.mean(scaled, axis=-1, keepdims=True)
    return inverse * (centered - normed * jnp.mean(scaled * normed, axis=-1, keepdims=True))


def dot(left, right):
    return jnp.dot(left, right, preferred_element_type=F32)


def contract_rows(left, right):
    return lax.dot_general(left, right, (((0,), (0,)), ((), ())), preferred_element_type=F32)


def contract_cols(left, right):
    return lax.dot_general(left, right, (((1,), (1,)), ((), ())), preferred_element_type=F32)


def tables(positions):
    half_rot = ROT // 2
    freqs = 10000.0 ** (-(2.0 * jnp.arange(half_rot, dtype=F32)) / ROT)
    angles = positions[:, None] * freqs[None, :]
    cosine = jnp.cos(angles)
    sine = jnp.sin(angles)
    return (jnp.concatenate([cosine, cosine], -1), jnp.concatenate([sine, sine], -1))


def rotate(heads_in, cosine, sine):
    half_rot = ROT // 2
    rotary = heads_in[..., :ROT]
    turned = jnp.concatenate([-rotary[..., half_rot:], rotary[..., :half_rot]], -1)
    moved = rotary * cosine[:, None, :] + turned * sine[:, None, :]
    return jnp.concatenate([moved, heads_in[..., ROT:]], -1)


def gather(value, axis):
    return lax.all_gather(value, axis, axis=0, tiled=True)


def scatter_sum(value, axis):
    return lax.psum_scatter(value, axis, scatter_dimension=0, tiled=True)


def swap(value, axis, split, concat):
    return lax.all_to_all(value, axis, split_axis=split, concat_axis=concat, tiled=True)


def attention_forward(queries, keys, values):
    length = queries.shape[0]
    scale = HEAD_DIM ** (-0.5)
    index = jnp.arange(length, dtype=jnp.int32)
    allowed = index[None, :] <= index[:, None]
    scores = jnp.einsum("qhd,khd->hqk", queries, keys, preferred_element_type=F32) * scale
    scores = jnp.where(allowed[None], scores, -jnp.inf)
    largest = jnp.max(scores, axis=-1, keepdims=True)
    exponent = jnp.exp(scores - largest)
    totals = jnp.sum(exponent, axis=-1, keepdims=True)
    probs = exponent / totals
    mixed = jnp.einsum("hqk,khd->qhd", probs.astype(BF16), values, preferred_element_type=F32)
    return mixed.astype(BF16), (largest + jnp.log(totals))


def attention_backward(queries, keys, values, log_total, grad):
    length = queries.shape[0]
    scale = HEAD_DIM ** (-0.5)
    index = jnp.arange(length, dtype=jnp.int32)
    allowed = index[None, :] <= index[:, None]
    scores = jnp.einsum("qhd,khd->hqk", queries, keys, preferred_element_type=F32) * scale
    scores = jnp.where(allowed[None], scores, -jnp.inf)
    probs = jnp.exp(scores - log_total)
    values_grad = jnp.einsum("hqk,qhd->khd", probs.astype(BF16), grad, preferred_element_type=F32)
    probs_grad = jnp.einsum("qhd,khd->hqk", grad, values, preferred_element_type=F32)
    scores_grad = (
        probs * (probs_grad - jnp.sum(probs * probs_grad, axis=-1, keepdims=True))
    ).astype(BF16)
    query_grad = jnp.einsum("hqk,khd->qhd", scores_grad, keys, preferred_element_type=F32) * scale
    keys_grad = jnp.einsum("hqk,qhd->khd", scores_grad, queries, preferred_element_type=F32) * scale
    return query_grad.astype(BF16), keys_grad.astype(BF16), values_grad.astype(BF16)


def shards(
    ways,
    inputs,
    first_gain,
    first_shift,
    qkv_weight,
    qkv_bias,
    out_weight,
    second_gain,
    second_shift,
    gate_weight,
    up_weight,
    down_weight,
    out_cotangent,
):
    seqs, dps = ways
    width = inputs.shape[2]
    rows = inputs.shape[1]
    length = rows * seqs
    part = width // (seqs * dps)
    units = down_weight.shape[0]
    group = width // seqs
    heads = group // HEAD_DIM
    me_seq = lax.axis_index("seq")
    grad_out = out_cotangent[0]
    hidden_in = inputs[0].astype(F32)

    small = gather(
        jnp.concatenate([first_gain, first_shift, second_gain, second_shift, qkv_bias])[None],
        ("seq", "dp"),
    ).astype(F32)
    gain_one = small[:, :part].reshape(-1)
    shift_one = small[:, part : 2 * part].reshape(-1)
    gain_two = small[:, 2 * part : 3 * part].reshape(-1)
    shift_two = small[:, 3 * part : 4 * part].reshape(-1)
    bias = small[:, 4 * part :].reshape(3, seqs, group)
    bias = lax.dynamic_index_in_dim(bias, me_seq, 1, keepdims=False).reshape(3 * group)

    qkv_cut = qkv_weight.reshape(part, 3, seqs, group).transpose(2, 0, 1, 3)
    qkv_cut = swap(qkv_cut.reshape(seqs * part, 3 * group), "seq", 0, 0)
    qkv_full = gather(qkv_cut, "dp")
    out_full = gather(out_weight, "dp")

    def cut_units(weight):
        cut = weight.reshape(part, seqs, dps, units).transpose(2, 0, 1, 3)
        return cut.reshape(dps * part, seqs * units)

    gate_cut = jnp.concatenate([cut_units(gate_weight), cut_units(up_weight)], 1)
    gate_up = gather(swap(gate_cut, "dp", 0, 0), "seq")
    down_full = gather(down_weight, "seq")
    wide = seqs * units

    def to_mixed(value):
        return value.reshape(rows, seqs, dps, part).swapaxes(1, 2).reshape(rows, width)

    def from_mixed(value):
        return value.reshape(rows, dps, seqs, part).swapaxes(1, 2).reshape(rows, width)

    normed_one, inverse_one = normalize(hidden_in)
    attn_input = (normed_one * gain_one + shift_one).astype(BF16)
    attn_all = gather(to_mixed(attn_input), "seq")
    projected = dot(attn_all, qkv_full) + bias
    cosine, sine = tables(jnp.arange(length, dtype=jnp.int32).astype(F32))

    def to_heads(flat):
        return flat.reshape(length, heads, HEAD_DIM)

    queries = rotate(to_heads(projected[:, :group]), cosine, sine).astype(BF16)
    keys = rotate(to_heads(projected[:, group : 2 * group]), cosine, sine).astype(BF16)
    values = to_heads(projected[:, 2 * group :]).astype(BF16)
    attended, log_total = attention_forward(queries, keys, values)
    attended = attended.reshape(length, group)
    branch = scatter_sum(dot(attended, out_full).astype(BF16), "seq").astype(F32)
    residual = hidden_in + branch

    normed_two, inverse_two = normalize(residual)
    mlp_input = (normed_two * gain_two + shift_two).astype(BF16)
    mlp_all = gather(mlp_input, "dp")
    grad_all = gather(grad_out, "dp")
    both = dot(mlp_all, gate_up)
    gate_value = both[:, :wide]
    up_value = both[:, wide:]
    sigmoid_gate = jax.nn.sigmoid(gate_value)
    activated = gate_value * sigmoid_gate
    hidden = (activated * up_value).astype(BF16)
    layer_out = residual + scatter_sum(dot(hidden, down_full).astype(BF16), "dp").astype(F32)

    hidden_grad = contract_cols(grad_all, down_full)
    gate_grad = (
        hidden_grad * up_value * (sigmoid_gate * (1.0 + gate_value * (1.0 - sigmoid_gate)))
    ).astype(BF16)
    up_grad = (hidden_grad * activated).astype(BF16)
    both_grad = jnp.concatenate([gate_grad, up_grad], 1)
    mlp_grad = scatter_sum(contract_cols(both_grad, gate_up).astype(BF16), "dp").astype(F32)
    gain_two_grad = jnp.sum(mlp_grad * normed_two, axis=0)
    shift_two_grad = jnp.sum(mlp_grad, axis=0)
    residual_grad = grad_out.astype(F32) + norm_back(mlp_grad, normed_two, inverse_two, gain_two)
    branch_grad = residual_grad.astype(BF16)

    branch_all = gather(branch_grad, "seq")
    attended_grad = contract_cols(branch_all, out_full).astype(BF16)
    query_grad, keys_grad, values_grad = attention_backward(
        queries, keys, values, log_total, to_heads(attended_grad)
    )
    query_plain = rotate(query_grad.astype(F32), cosine, -sine).astype(BF16)
    keys_plain = rotate(keys_grad.astype(F32), cosine, -sine).astype(BF16)
    projected_grad = jnp.concatenate(
        [item.reshape(length, group) for item in (query_plain, keys_plain, values_grad)], 1
    )
    attn_grad = scatter_sum(contract_cols(projected_grad, qkv_full).astype(BF16), "seq")
    attn_grad = from_mixed(attn_grad).astype(F32)
    gain_one_grad = jnp.sum(attn_grad * normed_one, axis=0)
    shift_one_grad = jnp.sum(attn_grad, axis=0)
    input_grad = residual_grad + norm_back(attn_grad, normed_one, inverse_one, gain_one)

    down_shard = scatter_sum(contract_rows(hidden, grad_all).astype(BF16), "seq").astype(F32)
    both_rows = scatter_sum(contract_rows(mlp_all, both_grad).astype(BF16), "seq")
    both_rows = swap(both_rows, "dp", 0, 0).reshape(dps, part, 2, seqs, units)
    both_rows = both_rows.transpose(2, 1, 3, 0, 4).reshape(2, part, seqs * dps * units).astype(F32)
    out_shard = scatter_sum(contract_rows(attended, branch_all).astype(BF16), "dp").astype(F32)
    qkv_rows = scatter_sum(contract_rows(attn_all, projected_grad).astype(BF16), "dp")
    qkv_rows = swap(qkv_rows, "seq", 0, 0).reshape(seqs, part, 3, group)
    qkv_shard = qkv_rows.transpose(1, 2, 0, 3).reshape(part, 3 * width).astype(F32)

    bias_term = jnp.sum(projected_grad.astype(F32), axis=0).reshape(3, 1, group)
    here = (jnp.arange(seqs, dtype=jnp.int32) == me_seq).astype(F32)[None, :, None]
    bias_term = (bias_term * here).reshape(seqs * dps, 3 * part)
    terms = [gain_one_grad, shift_one_grad, gain_two_grad, shift_two_grad]
    terms = [item.reshape(seqs * dps, part) for item in terms] + [bias_term]
    tiny = scatter_sum(jnp.concatenate(terms, 1), ("seq", "dp"))[0]
    return (
        layer_out.astype(BF16)[None],
        input_grad.astype(BF16)[None],
        tiny[:part],
        tiny[part : 2 * part],
        qkv_shard,
        tiny[4 * part :],
        out_shard,
        tiny[2 * part : 3 * part],
        tiny[3 * part : 4 * part],
        both_rows[0],
        both_rows[1],
        down_shard,
    )


def solution(mesh):
    split = ("seq", "dp")
    tokens = P("dp", "seq", None)
    in_specs = (
        tokens,
        P(split),
        P(split),
        P(split, None),
        P(split),
        P(split, None),
        P(split),
        P(split),
        P(split, None),
        P(split, None),
        P(split, None),
        tokens,
    )
    out_specs = (
        tokens,
        tokens,
        P(split),
        P(split),
        P(split, None),
        P(split),
        P(split, None),
        P(split),
        P(split),
        P(split, None),
        P(split, None),
        P(split, None),
    )
    ways = (mesh.shape["seq"], mesh.shape["dp"])

    def local(*args):
        return shards(ways, *args)

    return jax.shard_map(local, mesh=mesh, in_specs=in_specs, out_specs=out_specs, check_vma=False)
```

time: 1370 us -> 895 us (0.65)
  waiting for transfers between devices: 924 us -> 521 us
  matrix products: 170 us -> 102 us
  starting transfers between devices: 35.4 us -> 11.3 us
  local copies, waits for them, and re-layouts: 46.6 us -> 66 us
    all_gather x10 -> x8, waiting for transfers between devices: 632 us -> 289 us  [gather(): return lax.all_gather(value, axis, axis=0, tiled=True)]
    all_to_all x9 -> x2, waiting for transfers between devices: 70.7 us -> 0.01 us  [swap(): lax.all_to_all(value, axis, split_axis=split, concat_axis=concat, tiled=T...]
    dot_general x5 -> x4, matrix products: 62.2 us -> 28.2 us  [contract_cols(): lax.dot_general(left, right, (((1,), (1,)), ((), ())), preferred_element_...]
    dot_general x11 -> x10, matrix products: 72.5 us -> 43.3 us  [the longest x4 30.2 us: dot(): return jnp.dot(left, right, preferred_element_type=F32)]
    all_to_all x9 -> x2, starting transfers between devices: 34.2 us -> 9.19 us  [swap(): lax.all_to_all(value, axis, split_axis=split, concat_axis=concat, tiled=T...]
    convert_element_type x9 -> x10, local copies, waits for them, and re-layouts: 9.8 us -> 25.6 us  [the longest x2 12.2 us: shards(): both_rows.transpose(2, 1, 3, 0, 4).reshape(2, part, seqs * dps * units)]
    reduce_scatter x5 -> x8, waiting for transfers between devices: 216 us -> 230 us  [scatter_sum(): return lax.psum_scatter(value, axis, scatter_dimension=0, tiled=True)]
    all_to_all x3 -> x2, blocking collectives: 49.6 us -> 57.8 us  [swap(): lax.all_to_all(value, axis, split_axis=split, concat_axis=concat, tiled=T...]
  transfers between devices with their start and end apart: 24 -> 18, of which waited for: 20 -> 15; matrix products, arithmetic and copies ran while one was open for 15% -> 16% of each run, Pallas kernels for 0% -> 0%
where the time goes in v1:
time: 895 us; the launch traced here: 889 us
  waiting for transfers between devices  521 us (58%)
  blocking collectives  141 us (16%)
  matrix products  102 us (11%)
  local copies, waits for them, and re-layouts  66 us (7%)
  other arithmetic  32.6 us (4%)
  between operations  15.2 us (2%)
  starting transfers between devices  11.3 us (1%)
    all_gather x8, waiting for transfers between devices, gather(): return lax.all_gather(value, axis, axis=0, tiled=True)  289 us
    reduce_scatter x8, waiting for transfers between devices, scatter_sum(): return lax.psum_scatter(value, axis, scatter_dimension=0, tiled=True)  230 us
    unnamed x2, blocking collectives  83.4 us
    all_to_all x2, blocking collectives, swap(): lax.all_to_all(value, axis, split_axis=split, concat_axis=concat, tiled=T...  57.8 us
    dot_general x4, matrix products, contract_rows(): lax.dot_general(left, right, (((0,), (0,)), ((), ())), preferred_element_...  30.3 us
    dot_general x4, matrix products, dot(): return jnp.dot(left, right, preferred_element_type=F32)  30.2 us
    dot_general x4, matrix products, contract_cols(): lax.dot_general(left, right, (((1,), (1,)), ((), ())), preferred_element_...  28.2 us
  transfers between devices with their start and end apart: 18, of which 15 were waited for; matrix products, arithmetic and copies ran while one was open for 16% of the time, Pallas kernels for 0%

profile of v1, /device:TPU:0, one launch (start us, length us, event | category | flops | bytes accessed | tf_op | source)
XLA Modules:
  0.0 889.3 jit_solution(8843745862194956889)
XLA Ops:
  9.8 1.7 multiply_reduce_fusion.3
  11.5 3.4 concatenate.58
  15.2 42.3 %all-reduce = bf16[14336]{0:T(1024)(128)(2,1)S(1)} all-reduce(bf16[14336]{0:T(1024)(128)(2,1)S(1)} %dynamic-update-slice), channel_id=2, replica_groups=mesh['seq'=4,'dp'=8] {'seq','dp'}, use_global_device_ids=true, to_apply=%add | all-reduce | flops 14336 | bytes 57344
  61.8 19.7 %all_to_all.39 = bf16[4,64,1536]{2,1,0:T(8,128)(2,1)} all-to-all(bf16[4,64,1536]{2,1,0:T(8,128)(2,1)S(1)} %all_to_all.26), channel_id=1, replica_groups=mesh['seq'=4,'dp'=8] {'seq'}, dimensions={0} | all-to-all | bytes 1572864 | tf_op jit(solution)/shard_map/all_to_all | solution.py:63
  84.2 14.6 %all-gather.11.cloned.1.call-done = bf16[512,2048]{0,1:T(8,128)(2,1)} async-done(((bf16[128,2048]{0,1:T(8,128)(2,1)}), bf16[512,2048]{0,1:T(8,128)(2,1)}) %all-gather.11.cloned.1.call-update) | async-done | bytes 2097168 | tf_op jit(solution)/shard_map/all_gather | solution.py:55
  98.8 66.4 %all-gather.13.cloned.1.call-done = bf16[2048,1536]{1,0:T(8,128)(2,1)} async-done(((bf16[256,1536]{1,0:T(8,128)(2,1)}), bf16[2048,1536]{1,0:T(8,128)(2,1)}) %all-gather.13.cloned.1.call-update) | async-done | bytes 6291472 | tf_op jit(solution)/shard_map/all_gather | solution.py:55
  165.2 6.3 convolution_add_fusion
  171.7 1.3 copy.84
  173.2 1.5 slice.234
  179.6 2.5 fusion.54
  183.4 2.0 copy-done
  185.5 1.6 fusion.17
  187.1 7.5 all-gather.15.cloned.1.call-done
  194.6 4.3 convolution_convert_fusion.6
  199.2 2.0 reshape.307
  202.6 3.0 reshape.308
  207.4 38.1 %all_to_all.40 = bf16[8,64,1408]{2,1,0:T(8,128)(2,1)} all-to-all(bf16[8,64,1408]{2,1,0:T(8,128)(2,1)S(1)} %pad_maximum_fusion.4), channel_id=1, replica_groups=mesh['seq'=4,'dp'=8] {'dp'}, dimensions={0} | all-to-all | bytes 2883584 | tf_op jit(solution)/shard_map/all_to_all | solution.py:63
  247.0 1.3 multiply_reduce_fusion.2
  248.4 2.1 add_convert_fusion.2
  252.3 57.9 %all-gather.19.cloned.1.call-done = bf16[2048,1408]{1,0:T(8,128)(2,1)} async-done(((bf16[512,1408]{1,0:T(8,128)(2,1)}), bf16[2048,1408]{1,0:T(8,128)(2,1)}) %all-gather.19.cloned.1.call-update) | async-done | bytes 5767184 | tf_op jit(solution)/shard_map/all_gather | solution.py:55
  310.2 48.9 %all-gather.17.cloned.1.call-done = bf16[1024,2048]{1,0:T(8,128)(2,1)} async-done(((bf16[128,2048]{1,0:T(8,128)(2,1)}), bf16[1024,2048]{1,0:T(8,128)(2,1)}) %all-gather.17.cloned.1.call-update) | async-done | bytes 4194320 | tf_op jit(solution)/shard_map/all_gather | solution.py:55
  359.2 11.7 %fusion.57 = f32[1024,1408]{1,0:T(8,128)} fusion(bf16[1024,2048]{1,0:T(8,128)(2,1)} %all-gather.17.cloned.1.call-done, bf16[2048,1408]{1,0:T(8,128)(2,1)} %all-gather.19.cloned.1.call-done), kind=kOutput, calls=%fused_computation.143 | convolution fusion | flops 5905580032 | bytes 15728640 | tf_op jit(solution)/shard_map/dot_general | solution.py:26
  370.9 30.6 %all-gather.21.cloned.1.call-done = bf16[704,2048]{1,0:T(8,128)(2,1)} async-done(((bf16[176,2048]{1,0:T(8,128)(2,1)}), bf16[704,2048]{1,0:T(8,128)(2,1)}) %all-gather.21.cloned.1.call-update) | async-done | bytes 2883600 | tf_op jit(solution)/shard_map/all_gather | solution.py:55
  401.5 48.5 %all-gather.25.cloned.1.call-done = bf16[1,1024,2048]{2,1,0:T(8,128)(2,1)} async-done(((bf16[1,128,2048]{2,1,0:T(8,128)(2,1)}), bf16[1,1024,2048]{2,1,0:T(8,128)(2,1)}) %all-gather.25.cloned.1.call-update) | async-done | bytes 4194320 | tf_op jit(solution)/shard_map/all_gather | solution.py:55
  450.0 9.0 %multiply_convert_fusion.2 = (bf16[1024,704]{1,0:T(8,128)(2,1)S(1)}, bf16[1024,704]{1,0:T(8,128)(2,1)S(1)}, bf16[1024,704]{1,0:T(8,128)(2,1)S(1)}) fusion(f32[1024,1408]{1,0:T(8,128)} %fusion.57, bf16[704,2048]{1,0:T(8,128)(2,1)} %all-gather.21.cloned.1.call-done, bf16[1,1024,2048]{2,1,0:T(8,128)(2,1)} %all-gather.25.cloned.1.call-done), kind=kOutput, calls=%fused_computation.24 | convolution fusion | flops 2963603456 | bytes 17170432 | tf_op jit(solution)/shard_map/dot_general | solution.py:34
  460.7 11.0 %convolution_convert_fusion.2 = bf16[1024,2048]{1,0:T(8,128)(2,1)} fusion(bf16[2048,1408]{1,0:T(8,128)(2,1)} %all-gather.19.cloned.1.call-done, bf16[1024,704]{1,0:T(8,128)(2,1)S(1)} %get-tuple-element.21, bf16[1024,704]{1,0:T(8,128)(2,1)S(1)} %get-tuple-element.20), kind=kOutput, calls=%fused_computation.18 | convolution fusion | flops 5913444352 | bytes 12845056 | tf_op jit(solution)/shard_map/dot_general | solution.py:34
  471.8 48.8 %reduce-scatter.13.cloned.1.call-done = bf16[128,2048]{1,0:T(8,128)(2,1)} async-done(((bf16[1024,2048]{1,0:T(8,128)(2,1)}), bf16[128,2048]{1,0:T(8,128)(2,1)}) %reduce-scatter.13.cloned.1.call-update) | async-done | bytes 524304 | tf_op jit(solution)/shard_map/reduce_scatter | solution.py:59
  520.6 2.2 fusion.29
  522.8 2.5 fusion.50
  525.9 11.2 %convolution_convert_fusion = bf16[2048,1408]{1,0:T(8,128)(2,1)} fusion(bf16[1024,2048]{1,0:T(8,128)(2,1)} %all-gather.17.cloned.1.call-done, bf16[1024,704]{1,0:T(8,128)(2,1)} %copy-done.50, bf16[1024,704]{1,0:T(8,128)(2,1)} %copy-done.49), kind=kOutput, calls=%fused_computation.6 | convolution fusion | flops 5914230784 | bytes 12845056 | tf_op jit(solution)/shard_map/dot_general | solution.py:30
  537.2 7.0 fusion.10
  544.4 14.7 %all-gather.23.cloned.1.call-done = bf16[512,2048]{1,0:T(8,128)(2,1)} async-done(((bf16[128,2048]{1,0:T(8,128)(2,1)}), bf16[512,2048]{1,0:T(8,128)(2,1)}) %all-gather.23.cloned.1.call-update) | async-done | bytes 2097168 | tf_op jit(solution)/shard_map/all_gather | solution.py:55
  559.1 3.5 convolution_convert_fusion.7
  562.7 5.4 multiply_reduce_fusion
  568.5 2.5 multiply_convert_fusion
  571.1 1.4 fusion.56
  573.8 1.4 fusion.18
  576.5 4.8 convolution_convert_fusion.5
  581.3 7.9 convolution_convert_fusion.1
  590.3 4.2 convolution_convert_fusion.4
  594.8 7.9 convolution_convert_fusion.3
  602.7 25.1 %reduce-scatter.21.cloned.1.call-done = bf16[512,1408]{1,0:T(8,128)(2,1)} async-done(((bf16[2048,1408]{1,0:T(8,128)(2,1)}), bf16[512,1408]{1,0:T(8,128)(2,1)}) %reduce-scatter.21.cloned.1.call-update) | async-done | bytes 1441808 | tf_op jit(solution)/shard_map/reduce_scatter | solution.py:59
  627.8 4.6 all-to-all-start.3
  633.6 38.9 %reduce-scatter.23.cloned.1.call-done = bf16[176,2048]{1,0:T(8,128)(2,1)} async-done(((bf16[704,2048]{1,0:T(8,128)(2,1)}), bf16[176,2048]{1,0:T(8,128)(2,1)}) %reduce-scatter.23.cloned.1.call-update) | async-done | bytes 720912 | tf_op jit(solution)/shard_map/reduce_scatter | solution.py:59
  672.5 2.4 convert_element_type.267
  675.6 1.4 reshape.314
  677.0 1.9 convert_reduce_fusion
  680.5 7.5 reshape.318
  687.9 4.8 copy.112
  692.7 1.8 fusion.51
  694.5 2.6 squeeze.15
  697.2 3.4 squeeze.14
  700.5 10.1 %reduce-scatter.15.cloned.1.call-done = bf16[128,2048]{1,0:T(8,128)(2,1)} async-done(((bf16[512,2048]{1,0:T(8,128)(2,1)}), bf16[128,2048]{1,0:T(8,128)(2,1)}) %reduce-scatter.15.cloned.1.call-update) | async-done | bytes 524304 | tf_op jit(solution)/shard_map/reduce_scatter | solution.py:59
  713.0 41.2 %all-reduce.1 = f32[32,448]{1,0:T(8,128)S(1)} all-reduce(f32[32,448]{1,0:T(8,128)S(1)} %concatenate.74), channel_id=8, replica_groups=mesh['seq'=4,'dp'=8] {'seq','dp'}, use_global_device_ids=true, to_apply=%region_20.21.clone | all-reduce | flops 14336 | bytes 114688
  754.2 29.5 %reduce-scatter.17.cloned.1.call-done = bf16[256,1536]{1,0:T(8,128)(2,1)} async-done(((bf16[2048,1536]{1,0:T(8,128)(2,1)}), bf16[256,1536]{1,0:T(8,128)(2,1)}) %reduce-scatter.17.cloned.1.call-update) | async-done | bytes 786448 | tf_op jit(solution)/shard_map/reduce_scatter | solution.py:59
  783.7 4.6 all-to-all-start.2
  789.9 1.6 copy.96
  792.2 28.3 %reduce-scatter.19.cloned.1.call-done = bf16[64,2048]{1,0:T(8,128)(2,1)} async-done(((bf16[512,2048]{1,0:T(8,128)(2,1)}), bf16[64,2048]{1,0:T(8,128)(2,1)}) %reduce-scatter.19.cloned.1.call-update) | async-done | bytes 262160 | tf_op jit(solution)/shard_map/reduce_scatter | solution.py:59
  820.4 1.8 convert_element_type.261
  822.2 49.0 %reduce-scatter.11.cloned.1.call-done = bf16[128,2048]{1,0:T(8,128)(2,1)} async-done(((bf16[1024,2048]{1,0:T(8,128)(2,1)}), bf16[128,2048]{1,0:T(8,128)(2,1)}) %reduce-scatter.11.cloned.1.call-update) | async-done | bytes 524304 | tf_op jit(solution)/shard_map/reduce_scatter | solution.py:59
  871.3 3.1 fusion.35
  874.4 2.7 reshape.321
  877.1 2.2 copy.97
  879.3 3.2 reshape.317
  (213 shorter events, 37.7 us)
Async XLA Ops:
  7.2 52.5 %copy-start.16 = (bf16[64,6144]{1,0:T(8,128)(2,1)S(1)}, bf16[64,6144]{1,0:T(8,128)(2,1)}, u32[]{:S(2)}) copy-start(bf16[64,6144]{1,0:T(8,128)(2,1)} %param.15) | copy-start | bytes 2359300
  7.2 91.6 %all-gather.11.cloned.1.call-start = ((), (), s32[]{:S(2)}) async-start(), calls=%async_computation.12 | async-start | bytes 2621440 | tf_op jit(solution)/shard_map/all_gather | solution.py:55
  9.7 50.9 %copy-start.3 = (f32[1,128,2048]{1,2,0:T(8,128)}, f32[1,128,2048]{1,2,0:T(8,128)S(1)}, u32[]{:S(2)}) copy-start(f32[1,128,2048]{1,2,0:T(8,128)S(1)} %copy.80) | copy-start | bytes 3145732
  9.8 50.9 %copy-start.38 = (f32[128]{0:T(128)}, f32[128]{0:T(128)S(1)}, u32[]{:S(2)}) copy-start(f32[128]{0:T(128)S(1)} %broadcast_multiply_fusion.6) | copy-start | bytes 1540
  11.5 49.2 %copy-start.40 = (f32[128]{0:T(128)}, f32[128]{0:T(128)S(1)}, u32[]{:S(2)}) copy-start(f32[128]{0:T(128)S(1)} %add_rsqrt_fusion.1) | copy-start | bytes 1540
  59.6 105.5 %all-gather.13.cloned.1.call-start = ((), (), s32[]{:S(2)}) async-start(), calls=%async_computation.13 | async-start | bytes 7077888 | tf_op jit(solution)/shard_map/all_gather | solution.py:55
  81.5 113.1 %all-gather.15.cloned.1.call-start = ((), (), s32[]{:S(2)}) async-start(), calls=%async_computation.14 | async-start | bytes 2359296 | tf_op jit(solution)/shard_map/all_gather | solution.py:55
  82.2 163.5 %reduce-scatter.9.cloned.1.call-start = ((), (), s32[]{:S(2)}) async-start(), calls=%async_computation.15 | async-start | bytes 2621440 | tf_op jit(solution)/shard_map/reduce_scatter | solution.py:59
  173.0 4.3 copy-start.8
  173.2 10.1 %copy-start.9 = (bf16[512,512]{0,1:T(8,128)(2,1)}, bf16[512,512]{0,1:T(8,128)(2,1)S(1)}, u32[]{:S(2)}) copy-start(bf16[512,512]{0,1:T(8,128)(2,1)S(1)} %copy.83) | copy-start | bytes 1572868
  174.8 7.3 copy-start.14
  177.3 4.8 copy-start.12
  182.1 3.3 copy-start
  182.2 3.3 copy-start.26
  183.4 3.7 copy-start.28
  187.1 11.8 %copy-start.46 = (bf16[8,64,512]{2,1,0:T(8,128)(2,1)}, bf16[8,64,512]{2,1,0:T(8,128)(2,1)S(1)}, u32[]{:S(2)}) copy-start(bf16[8,64,512]{2,1,0:T(8,128)(2,1)S(1)} %fusion.17) | copy-start | bytes 1572868
  194.6 4.6 copy-start.17
  198.9 111.3 %all-gather.19.cloned.1.call-start = ((), (), s32[]{:S(2)}) async-start(), calls=%async_computation.17 | async-start | bytes 7208960 | tf_op jit(solution)/shard_map/all_gather | solution.py:55
  206.9 38.7 %copy-start.31 = (f32[32,64]{1,0:T(8,128)S(1)}, f32[32,64]{1,0:T(8,128)}, u32[]{:S(2)}) copy-start(f32[32,64]{1,0:T(8,128)} %get-tuple-element.40) | copy-start | bytes 24580
  206.9 38.8 %copy-start.1 = (bf16[1,128,2048]{2,1,0:T(8,128)(2,1)S(1)}, bf16[1,128,2048]{2,1,0:T(8,128)(2,1)}, u32[]{:S(2)}) copy-start(bf16[1,128,2048]{2,1,0:T(8,128)(2,1)} %param.12) | copy-start | bytes 1572868
  245.5 113.6 %all-gather.17.cloned.1.call-start = ((), (), s32[]{:S(2)}) async-start(), calls=%async_computation.16 | async-start | bytes 4718592 | tf_op jit(solution)/shard_map/all_gather | solution.py:55
  245.7 277.1 %copy-start.21 = (f32[2048]{0:T(1024)}, f32[2048]{0:T(1024)S(1)}, u32[]{:S(2)}) copy-start(f32[2048]{0:T(1024)S(1)} %mul.291) | copy-start | bytes 24580
  247.0 275.8 %copy-start.34 = (f32[128]{0:T(128)}, f32[128]{0:T(128)S(1)}, u32[]{:S(2)}) copy-start(f32[128]{0:T(128)S(1)} %broadcast_multiply_fusion.5) | copy-start | bytes 1540
  248.4 274.4 %copy-start.36 = (f32[128]{0:T(128)}, f32[128]{0:T(128)S(1)}, u32[]{:S(2)}) copy-start(f32[128]{0:T(128)S(1)} %add_rsqrt_fusion) | copy-start | bytes 1540
  250.5 151.0 %all-gather.21.cloned.1.call-start = ((), (), s32[]{:S(2)}) async-start(), calls=%async_computation.18 | async-start | bytes 3604480 | tf_op jit(solution)/shard_map/all_gather | solution.py:55
  251.3 198.7 %all-gather.25.cloned.1.call-start = ((), (), s32[]{:S(2)}) async-start(), calls=%async_computation.27 | async-start | bytes 4718592 | tf_op jit(solution)/shard_map/all_gather | solution.py:55
  252.0 268.5 %reduce-scatter.13.cloned.1.call-start = ((), (), s32[]{:S(2)}) async-start(), calls=%async_computation.20 | async-start | bytes 4718592 | tf_op jit(solution)/shard_map/reduce_scatter | solution.py:59
  459.0 78.1 %copy-start.48 = (bf16[1024,704]{1,0:T(8,128)(2,1)}, bf16[1024,704]{1,0:T(8,128)(2,1)S(1)}, u32[]{:S(2)}) copy-start(bf16[1024,704]{1,0:T(8,128)(2,1)S(1)} %get-tuple-element.22) | copy-start | bytes 4325380
  471.7 48.9 %copy-start.2 = (bf16[128,2048]{1,0:T(8,128)(2,1)S(1)}, bf16[128,2048]{1,0:T(8,128)(2,1)}, u32[]{:S(2)}) copy-start(bf16[128,2048]{1,0:T(8,128)(2,1)} %reduce-scatter.9.cloned.1.call-done) | copy-start | bytes 1572868
  471.7 51.1 %copy-start.5 = (bf16[1,128,2048]{2,1,0:T(8,128)(2,1)S(1)}, bf16[1,128,2048]{2,1,0:T(8,128)(2,1)}, u32[]{:S(2)}) copy-start(bf16[1,128,2048]{2,1,0:T(8,128)(2,1)} %param.23) | copy-start | bytes 1572868
  471.7 87.4 %all-gather.23.cloned.1.call-start = ((), (), s32[]{:S(2)}) async-start(), calls=%async_computation.21 | async-start | bytes 2621440 | tf_op jit(solution)/shard_map/all_gather | solution.py:55
  522.8 14.3 %copy-start.42 = (f32[128]{0:T(128)}, f32[128]{0:T(128)S(1)}, u32[]{:S(2)}) copy-start(f32[128]{0:T(128)S(1)} %broadcast_multiply_fusion.3) | copy-start | bytes 1540
  522.8 14.3 %copy-start.44 = (f32[128]{0:T(128)}, f32[128]{0:T(128)S(1)}, u32[]{:S(2)}) copy-start(f32[128]{0:T(128)S(1)} %broadcast_multiply_fusion.4) | copy-start | bytes 1540
  525.3 102.5 %reduce-scatter.21.cloned.1.call-start = ((), (), s32[]{:S(2)}) async-start(), calls=%async_computation.25 | async-start | bytes 7208960 | tf_op jit(solution)/shard_map/reduce_scatter | solution.py:59
  537.1 135.4 %reduce-scatter.23.cloned.1.call-start = ((), (), s32[]{:S(2)}) async-start(), calls=%async_computation.26 | async-start | bytes 3604480 | tf_op jit(solution)/shard_map/reduce_scatter | solution.py:59
  537.2 7.2 copy-start.27
  537.2 7.2 copy-start.29
  544.2 166.5 %reduce-scatter.15.cloned.1.call-start = ((), (), s32[]{:S(2)}) async-start(), calls=%async_computation.22 | async-start | bytes 2621440 | tf_op jit(solution)/shard_map/reduce_scatter | solution.py:59
  544.4 18.2 %copy-start.10 = (bf16[512,512]{0,1:T(8,128)(2,1)S(1)}, bf16[512,512]{0,1:T(8,128)(2,1)}, u32[]{:S(2)}) copy-start(bf16[512,512]{0,1:T(8,128)(2,1)} %copy-done.9) | copy-start | bytes 1572868
  562.6 5.5 slice-start
  562.7 5.8 slice-start.1
  568.5 2.6 copy-start.15
  568.5 2.6 copy-start.19
  573.7 7.6 copy-start.11
  573.7 2.7 slice-start.3
  581.3 202.4 %reduce-scatter.17.cloned.1.call-start = ((), (), s32[]{:S(2)}) async-start(), calls=%async_computation.23 | async-start | bytes 7077888 | tf_op jit(solution)/shard_map/reduce_scatter | solution.py:59
  589.3 231.2 %reduce-scatter.19.cloned.1.call-start = ((), (), s32[]{:S(2)}) async-start(), calls=%async_computation.24 | async-start | bytes 2359296 | tf_op jit(solution)/shard_map/reduce_scatter | solution.py:59
  594.5 276.7 %reduce-scatter.11.cloned.1.call-start = ((), (), s32[]{:S(2)}) async-start(), calls=%async_computation.19 | async-start | bytes 4718592 | tf_op jit(solution)/shard_map/reduce_scatter | solution.py:59
  602.7 29.8 %copy-start.30 = (f32[32,64]{1,0:T(8,128)S(1)}, f32[32,64]{1,0:T(8,128)}, u32[]{:S(2)}) copy-start(f32[32,64]{1,0:T(8,128)} %get-tuple-element.37) | copy-start | bytes 24580
  627.8 52.6 %all-to-all-start.3 = ((bf16[8,64,1408]{2,1,0:T(8,128)(2,1)}), bf16[8,64,1408]{2,1,0:T(8,128)(2,1)S(1)}, u32[]{:S(2)}, u32[]{:S(2)}) async-start(bf16[8,64,1408]{2,1,0:T(8,128)(2,1)} %bitcast.176), calls=%async_computation.10 | async-start | bytes 2883584 | tf_op jit(solution)/shard_map/all_to_all | solution.py:63
  697.2 14.8 %copy-start.4 = (f32[1,128,2048]{1,2,0:T(8,128)S(1)}, f32[1,128,2048]{1,2,0:T(8,128)}, u32[]{:S(2)}) copy-start(f32[1,128,2048]{1,2,0:T(8,128)} %copy-done.3) | copy-start | bytes 3145732
  697.2 14.8 %copy-start.24 = (f32[4,8,64]{2,1,0:T(8,128)S(1)}, f32[4,8,64]{2,1,0:T(8,128)}, u32[]{:S(2)}) copy-start(f32[4,8,64]{2,1,0:T(8,128)} %copy-done.23) | copy-start | bytes 24580
  697.2 14.8 %copy-start.39 = (f32[128]{0:T(128)S(1)}, f32[128]{0:T(128)}, u32[]{:S(2)}) copy-start(f32[128]{0:T(128)} %copy-done.38) | copy-start | bytes 1540
  697.2 14.8 %copy-start.41 = (f32[128]{0:T(128)S(1)}, f32[128]{0:T(128)}, u32[]{:S(2)}) copy-start(f32[128]{0:T(128)} %copy-done.40) | copy-start | bytes 1540
  697.2 15.7 %copy-start.32 = (f32[32,64]{1,0:T(8,128)S(1)}, f32[32,64]{1,0:T(8,128)}, u32[]{:S(2)}) copy-start(f32[32,64]{1,0:T(8,128)} %reshape.314) | copy-start | bytes 24580
  783.7 87.5 %copy-start.6 = (bf16[1,128,2048]{2,1,0:T(8,128)(2,1)S(1)}, bf16[1,128,2048]{2,1,0:T(8,128)(2,1)}, u32[]{:S(2)}) copy-start(bf16[1,128,2048]{2,1,0:T(8,128)(2,1)} %param.23) | copy-start | bytes 1572868
  783.7 87.5 %copy-start.7 = (bf16[128,2048]{1,0:T(8,128)(2,1)S(1)}, bf16[128,2048]{1,0:T(8,128)(2,1)}, u32[]{:S(2)}) copy-start(bf16[128,2048]{1,0:T(8,128)(2,1)} %reduce-scatter.13.cloned.1.call-done) | copy-start | bytes 1572868
  783.7 87.6 %copy-start.22 = (f32[2048]{0:T(1024)S(1)}, f32[2048]{0:T(1024)}, u32[]{:S(2)}) copy-start(f32[2048]{0:T(1024)} %copy-done.21) | copy-start | bytes 24580
  783.7 87.6 %copy-start.33 = (f32[2048]{0:T(1024)S(1)}, f32[2048]{0:T(1024)}, u32[]{:S(2)}) copy-start(f32[2048]{0:T(1024)} %mul.316) | copy-start | bytes 24580
  783.7 87.6 %copy-start.35 = (f32[128]{0:T(128)S(1)}, f32[128]{0:T(128)}, u32[]{:S(2)}) copy-start(f32[128]{0:T(128)} %copy-done.34) | copy-start | bytes 1540
  783.7 87.6 %copy-start.37 = (f32[128]{0:T(128)S(1)}, f32[128]{0:T(128)}, u32[]{:S(2)}) copy-start(f32[128]{0:T(128)} %copy-done.36) | copy-start | bytes 1540
  783.7 87.6 %copy-start.43 = (f32[128]{0:T(128)S(1)}, f32[128]{0:T(128)}, u32[]{:S(2)}) copy-start(f32[128]{0:T(128)} %copy-done.42) | copy-start | bytes 1540
  783.7 87.6 %copy-start.45 = (f32[128]{0:T(128)S(1)}, f32[128]{0:T(128)}, u32[]{:S(2)}) copy-start(f32[128]{0:T(128)} %copy-done.44) | copy-start | bytes 1540
  783.7 90.7 %all-to-all-start.2 = ((bf16[4,64,1536]{2,1,0:T(8,128)(2,1)}), bf16[4,64,1536]{2,1,0:T(8,128)(2,1)}, u32[]{:S(2)}, u32[]{:S(2)}) async-start(bf16[4,64,1536]{2,1,0:T(8,128)(2,1)} %bitcast.177), calls=%async_computation.7 | async-start | bytes 1572864 | tf_op jit(solution)/shard_map/all_to_all | solution.py:63
  (9 other events, 13.2 us)
Sparse Core Ops, SparseCore 0:
  59.7 39.0 all-gather.10
  100.4 64.6 all-gather.12
  166.8 27.7 all-gather.14
  199.0 34.5 reduce-scatter.8
  245.7 64.5 all-gather.18
  312.3 46.8 all-gather.16
  361.0 40.4 all-gather.20
  403.1 46.8 all-gather.24
  471.8 48.7 reduce-scatter.12
  525.5 33.6 all-gather.22
  562.1 65.6 reduce-scatter.20
  630.7 41.7 reduce-scatter.22
  675.5 35.1 reduce-scatter.14
  712.8 70.7 reduce-scatter.16
  785.8 34.5 reduce-scatter.18
  822.6 48.5 reduce-scatter.10

commit v2 on v1

--- a/solution.py
+++ b/solution.py
@@ -1,6 +1,10 @@
+import functools
+
 import jax
 import jax.numpy as jnp
 from jax import lax
+from jax.experimental import pallas as pl
+from jax.experimental.pallas import tpu as pltpu
 from jax.sharding import PartitionSpec as P
 
 HEAD_DIM = 64
@@ -61,6 +65,215 @@
 
 def swap(value, axis, split, concat):
     return lax.all_to_all(value, axis, split_axis=split, concat_axis=concat, tiled=True)
+
+
+MESH = pl.DeviceIdType.MESH
+
+
+def meet(peers):
+    barrier = pltpu.get_barrier_semaphore()
+    for peer in peers:
+        pl.semaphore_signal(barrier, inc=1, device_id=peer, device_id_type=MESH)
+    pl.semaphore_wait(barrier, len(peers))
+
+
+def push(source, target, send, recv, at, peer):
+    copy = pltpu.make_async_remote_copy(
+        src_ref=source,
+        dst_ref=target,
+        send_sem=send.at[at],
+        recv_sem=recv.at[at],
+        device_id=peer,
+        device_id_type=MESH,
+    )
+    copy.start()
+    return copy
+
+
+def corners():
+    me = lax.axis_index("seq")
+    high, low = me // 2, lax.rem(me, 2)
+    across = high * 2 + (1 - low)
+    along = (1 - high) * 2 + low
+    return me, across, along, 3 - me
+
+
+def gather_square(x_ref, o_ref, send, recv, local):
+    me, across, along, far = corners()
+    to_across, to_along = {"seq": across}, {"seq": along}
+    half = x_ref.shape[0] // 2
+    top, low = pl.ds(0, half), pl.ds(half, half)
+    meet([to_across, to_along])
+    copies = [
+        push(x_ref.at[top], o_ref.at[me, top], send, recv, 0, to_across),
+        push(x_ref.at[low], o_ref.at[me, low], send, recv, 1, to_along),
+        push(x_ref.at[low], o_ref.at[me, low], send, recv, 2, to_across),
+        push(x_ref.at[top], o_ref.at[me, top], send, recv, 3, to_along),
+    ]
+    own = pltpu.make_async_copy(x_ref, o_ref.at[me], local)
+    own.start()
+    copies[0].wait_recv()
+    copies.append(push(o_ref.at[across, top], o_ref.at[across, top], send, recv, 4, to_along))
+    copies[1].wait_recv()
+    copies.append(push(o_ref.at[along, low], o_ref.at[along, low], send, recv, 5, to_across))
+    for at, copy in enumerate(copies):
+        copy.wait_send()
+        if at > 1:
+            copy.wait_recv()
+    own.wait()
+
+
+def gather_direct(count, x_ref, o_ref, send, recv, local):
+    me = lax.axis_index("seq")
+    peers = [{"seq": lax.rem(me + step, count)} for step in range(1, count)]
+    meet(peers)
+    copies = [push(x_ref, o_ref.at[me], send, recv, at, peer) for at, peer in enumerate(peers)]
+    own = pltpu.make_async_copy(x_ref, o_ref.at[me], local)
+    own.start()
+    for copy in copies:
+        copy.wait()
+    own.wait()
+
+
+def gather_seq(value, count, tag):
+    square = count == 4
+    body = gather_square if square else functools.partial(gather_direct, count)
+    slots = 6 if square else count - 1
+    out = pl.pallas_call(
+        body,
+        out_shape=jax.ShapeDtypeStruct((count,) + value.shape, value.dtype),
+        in_specs=[pl.BlockSpec(memory_space=pltpu.VMEM)],
+        out_specs=pl.BlockSpec(memory_space=pl.ANY),
+        scratch_shapes=[
+            pltpu.SemaphoreType.DMA((slots,)),
+            pltpu.SemaphoreType.DMA((slots,)),
+            pltpu.SemaphoreType.DMA,
+        ],
+        compiler_params=pltpu.CompilerParams(collective_id=tag, has_side_effects=True),
+    )(value)
+    return out.reshape(count * value.shape[0], value.shape[1])
+
+
+def reduce_square(x_ref, o_ref, pair, got, send, recv):
+    me, across, along, far = corners()
+    to_across, to_along = {"seq": across}, {"seq": along}
+    half = x_ref.shape[1] // 2
+    top, low = pl.ds(0, half), pl.ds(half, half)
+    meet([to_across, to_along])
+    copies = [
+        push(x_ref.at[far, top], pair.at[0], send, recv, 0, to_across),
+        push(x_ref.at[far, low], pair.at[1], send, recv, 1, to_along),
+        push(x_ref.at[across, top], got.at[0, top], send, recv, 2, to_across),
+        push(x_ref.at[along, low], got.at[1, low], send, recv, 3, to_along),
+    ]
+    copies[0].wait_recv()
+    pair[2] = (pair[0].astype(F32) + x_ref[along, top].astype(F32)).astype(pair.dtype)
+    copies.append(push(pair.at[2], got.at[1, top], send, recv, 4, to_along))
+    copies[1].wait_recv()
+    pair[3] = (pair[1].astype(F32) + x_ref[across, low].astype(F32)).astype(pair.dtype)
+    copies.append(push(pair.at[3], got.at[0, low], send, recv, 5, to_across))
+    for at, copy in enumerate(copies):
+        copy.wait_send()
+        if at > 1:
+            copy.wait_recv()
+    o_ref[...] = x_ref[me].astype(F32) + (got[0].astype(F32) + got[1].astype(F32))
+
+
+def reduce_direct(count, x_ref, o_ref, got, send, recv):
+    me = lax.axis_index("seq")
+    targets = [lax.rem(me + step, count) for step in range(1, count)]
+    peers = [{"seq": target} for target in targets]
+    meet(peers)
+    copies = [
+        push(x_ref.at[target], got.at[at], send, recv, at, peer)
+        for at, (target, peer) in enumerate(zip(targets, peers))
+    ]
+    for copy in copies:
+        copy.wait()
+    total = x_ref[me].astype(F32)
+    for at in range(count - 1):
+        total = total + got[at].astype(F32)
+    o_ref[...] = total
+
+
+def reduce_seq(value, count, tag):
+    rows, wide = value.shape[0] // count, value.shape[1]
+    square = count == 4
+    if square:
+        body, slots = reduce_square, 6
+        held = [
+            pltpu.VMEM((4, rows // 2, wide), value.dtype),
+            pltpu.VMEM((2, rows, wide), value.dtype),
+        ]
+    else:
+        body, slots = functools.partial(reduce_direct, count), count - 1
+        held = [pltpu.VMEM((count - 1, rows, wide), value.dtype)]
+    return pl.pallas_call(
+        body,
+        out_shape=jax.ShapeDtypeStruct((rows, wide), F32),
+        in_specs=[pl.BlockSpec(memory_space=pltpu.VMEM)],
+        out_specs=pl.BlockSpec(memory_space=pltpu.VMEM),
+        scratch_shapes=held
+        + [pltpu.SemaphoreType.DMA((slots,)), pltpu.SemaphoreType.DMA((slots,))],
+        compiler_params=pltpu.CompilerParams(collective_id=tag, has_side_effects=True),
+    )(value.reshape(count, rows, wide))
+
+
+def exchange(ways, shared, x_ref, o_ref, got, send, recv):
+    seqs, dps = ways
+    count = seqs * dps
+    me = lax.axis_index("seq") * dps + lax.axis_index("dp")
+    barrier = pltpu.get_barrier_semaphore()
+
+    def peer_of(step):
+        other = lax.rem(me + step, count)
+        return other, {"seq": other // dps, "dp": lax.rem(other, dps)}
+
+    def copy_of(step):
+        other, peer = peer_of(step)
+        return pltpu.make_async_remote_copy(
+            src_ref=x_ref if shared else x_ref.at[other],
+            dst_ref=got.at[me],
+            send_sem=send.at[step - 1],
+            recv_sem=recv.at[step - 1],
+            device_id=peer,
+            device_id_type=MESH,
+        )
+
+    @pl.loop(1, count)
+    def _(step):
+        pl.semaphore_signal(barrier, inc=1, device_id=peer_of(step)[1], device_id_type=MESH)
+
+    pl.semaphore_wait(barrier, count - 1)
+
+    @pl.loop(1, count)
+    def _(step):
+        copy_of(step).start()
+
+    got[me] = x_ref[...] if shared else x_ref[me]
+
+    @pl.loop(1, count)
+    def _(step):
+        copy_of(step).wait()
+
+    o_ref[...] = got[...] if shared else jnp.sum(got[...], axis=0)
+
+
+def exchange_all(value, ways, shared, tag):
+    count = ways[0] * ways[1]
+    block = value.shape if shared else value.shape[1:]
+    return pl.pallas_call(
+        functools.partial(exchange, ways, shared),
+        out_shape=jax.ShapeDtypeStruct(((count,) if shared else ()) + block, value.dtype),
+        in_specs=[pl.BlockSpec(memory_space=pltpu.VMEM)],
+        out_specs=pl.BlockSpec(memory_space=pltpu.VMEM),
+        scratch_shapes=[
+            pltpu.VMEM((count,) + block, value.dtype),
+            pltpu.SemaphoreType.DMA((count - 1,)),
+            pltpu.SemaphoreType.DMA((count - 1,)),
+        ],
+        compiler_params=pltpu.CompilerParams(collective_id=tag, has_side_effects=True),
+    )(value)
 
 
 def attention_forward(queries, keys, values):
@@ -123,10 +336,11 @@
     grad_out = out_cotangent[0]
     hidden_in = inputs[0].astype(F32)
 
-    small = gather(
-        jnp.concatenate([first_gain, first_shift, second_gain, second_shift, qkv_bias])[None],
-        ("seq", "dp"),
-    ).astype(F32)
+    small = jnp.concatenate([first_gain, first_shift, second_gain, second_shift, qkv_bias])
+    total = small.shape[0]
+    padded = -(-total // 2048) * 2048
+    small = jnp.pad(small, (0, padded - total)).reshape(padded // 128, 128)
+    small = exchange_all(small, ways, True, 4).reshape(seqs * dps, padded)[:, :total].astype(F32)
     gain_one = small[:, :part].reshape(-1)
     shift_one = small[:, part : 2 * part].reshape(-1)
     gain_two = small[:, 2 * part : 3 * part].reshape(-1)
@@ -156,7 +370,7 @@
 
     normed_one, inverse_one = normalize(hidden_in)
     attn_input = (normed_one * gain_one + shift_one).astype(BF16)
-    attn_all = gather(to_mixed(attn_input), "seq")
+    attn_all = gather_seq(to_mixed(attn_input), seqs, 0)
     projected = dot(attn_all, qkv_full) + bias
     cosine, sine = tables(jnp.arange(length, dtype=jnp.int32).astype(F32))
 
@@ -168,7 +382,7 @@
     values = to_heads(projected[:, 2 * group :]).astype(BF16)
     attended, log_total = attention_forward(queries, keys, values)
     attended = attended.reshape(length, group)
-    branch = scatter_sum(dot(attended, out_full).astype(BF16), "seq").astype(F32)
+    branch = reduce_seq(dot(attended, out_full).astype(BF16), seqs, 1)
     residual = hidden_in + branch
 
     normed_two, inverse_two = normalize(residual)
@@ -195,7 +409,7 @@
     residual_grad = grad_out.astype(F32) + norm_back(mlp_grad, normed_two, inverse_two, gain_two)
     branch_grad = residual_grad.astype(BF16)
 
-    branch_all = gather(branch_grad, "seq")
+    branch_all = gather_seq(branch_grad, seqs, 2)
     attended_grad = contract_cols(branch_all, out_full).astype(BF16)
     query_grad, keys_grad, values_grad = attention_backward(
         queries, keys, values, log_total, to_heads(attended_grad)
@@ -205,8 +419,8 @@
     projected_grad = jnp.concatenate(
         [item.reshape(length, group) for item in (query_plain, keys_plain, values_grad)], 1
     )
-    attn_grad = scatter_sum(contract_cols(projected_grad, qkv_full).astype(BF16), "seq")
-    attn_grad = from_mixed(attn_grad).astype(F32)
+    attn_grad = reduce_seq(contract_cols(projected_grad, qkv_full).astype(BF16), seqs, 3)
+    attn_grad = from_mixed(attn_grad)
     gain_one_grad = jnp.sum(attn_grad * normed_one, axis=0)
     shift_one_grad = jnp.sum(attn_grad, axis=0)
     input_grad = residual_grad + norm_back(attn_grad, normed_one, inverse_one, gain_one)
@@ -225,14 +439,17 @@
     bias_term = (bias_term * here).reshape(seqs * dps, 3 * part)
     terms = [gain_one_grad, shift_one_grad, gain_two_grad, shift_two_grad]
     terms = [item.reshape(seqs * dps, part) for item in terms] + [bias_term]
-    tiny = scatter_sum(jnp.concatenate(terms, 1), ("seq", "dp"))[0]
+    terms = jnp.concatenate(terms, 1)
+    padded = -(-total // 1024) * 1024
+    terms = jnp.pad(terms, ((0, 0), (0, padded - total))).reshape(seqs * dps, padded // 128, 128)
+    tiny = exchange_all(terms, ways, False, 5).reshape(padded)
     return (
         layer_out.astype(BF16)[None],
         input_grad.astype(BF16)[None],
         tiny[:part],
         tiny[part : 2 * part],
         qkv_shard,
-        tiny[4 * part :],
+        tiny[4 * part : total],
         out_shard,
         tiny[2 * part : 3 * part],
         tiny[3 * part : 4 * part],

time: 895 us -> 775 us (0.87)
  waiting for transfers between devices: 521 us -> 296 us
  Pallas kernels: 0 us -> 139 us
  blocking collectives: 141 us -> 93.9 us
  starting transfers between devices: 11.3 us -> 21.4 us
    all_gather x8 -> x6, waiting for transfers between devices: 289 us -> 124 us  [gather(): return lax.all_gather(value, axis, axis=0, tiled=True)]
    pallas_call x0 -> x6, Pallas kernels: none -> 139 us  [the longest x2 59.8 us: reduce_seq(): pl.pallas_call(body, out_shape=jax.ShapeDtypeStruct((rows, wide), F32), i...]
    unnamed x2 -> x0, blocking collectives: 83.4 us -> none
    reduce_scatter x8 -> x6, waiting for transfers between devices: 230 us -> 170 us  [scatter_sum(): return lax.psum_scatter(value, axis, scatter_dimension=0, tiled=True)]
    all_to_all x2, blocking collectives: 57.8 us -> 93.9 us  [swap(): lax.all_to_all(value, axis, split_axis=split, concat_axis=concat, tiled=T...]
    reduce_scatter x8 -> x6, starting transfers between devices: 1.6 us -> 12.5 us  [scatter_sum(): return lax.psum_scatter(value, axis, scatter_dimension=0, tiled=True)]
  transfers between devices with their start and end apart: 18 -> 14, of which waited for: 15 -> 9; matrix products, arithmetic and copies ran while one was open for 16% -> 21% of each run, Pallas kernels for 0% -> 18%
where the time goes in v2:
time: 775 us; the launch traced here: 767 us
  waiting for transfers between devices  296 us (38%)
  Pallas kernels  139 us (18%)
  matrix products  105 us (14%)
  blocking collectives  93.9 us (12%)
  local copies, waits for them, and re-layouts  67.6 us (9%)
  other arithmetic  28 us (4%)
  starting transfers between devices  21.4 us (3%)
  between operations  15.3 us (2%)
    reduce_scatter x6, waiting for transfers between devices, scatter_sum(): return lax.psum_scatter(value, axis, scatter_dimension=0, tiled=True)  170 us
    all_gather x6, waiting for transfers between devices, gather(): return lax.all_gather(value, axis, axis=0, tiled=True)  124 us
    all_to_all x2, blocking collectives, swap(): lax.all_to_all(value, axis, split_axis=split, concat_axis=concat, tiled=T...  93.9 us
    pallas_call x2, Pallas kernels, reduce_seq(): pl.pallas_call(body, out_shape=jax.ShapeDtypeStruct((rows, wide), F32), i...  59.8 us
    pallas_call x2, Pallas kernels, gather_seq(): pl.pallas_call(body, out_shape=jax.ShapeDtypeStruct((count,) + value.shap...  56.4 us
    dot_general x4, matrix products, contract_cols(): lax.dot_general(left, right, (((1,), (1,)), ((), ())), preferred_element_...  32.5 us
    dot_general x4, matrix products, dot(): return jnp.dot(left, right, preferred_element_type=F32)  30 us
    dot_general x4, matrix products, contract_rows(): lax.dot_general(left, right, (((0,), (0,)), ((), ())), preferred_element_...  29.5 us
  transfers between devices with their start and end apart: 14, of which 9 were waited for; matrix products, arithmetic and copies ran while one was open for 21% of the time, Pallas kernels for 18%

profile of v2, /device:TPU:0, one launch (start us, length us, event | category | flops | bytes accessed | tf_op | source)
XLA Modules:
  0.0 766.8 jit_solution(2293680304763560924)
XLA Ops:
  7.2 2.3 reshape.322
  11.1 16.4 %all_to_all.39 = bf16[4,64,1536]{2,1,0:T(8,128)(2,1)} all-to-all(bf16[4,64,1536]{2,1,0:T(8,128)(2,1)S(1)} %all_to_all.26), channel_id=1, replica_groups=mesh['seq'=4,'dp'=8] {'seq'}, dimensions={0} | all-to-all | bytes 1572864 | tf_op jit(solution)/shard_map/all_to_all | solution.py:67
  28.3 2.0 reshape.328
  31.7 3.0 reshape.329
  36.6 77.4 %all_to_all.40 = bf16[8,64,1408]{2,1,0:T(8,128)(2,1)} all-to-all(bf16[8,64,1408]{2,1,0:T(8,128)(2,1)S(1)} %pad_maximum_fusion.4), channel_id=1, replica_groups=mesh['seq'=4,'dp'=8] {'dp'}, dimensions={0} | all-to-all | bytes 2883584 | tf_op jit(solution)/shard_map/all_to_all | solution.py:67
  115.1 10.5 %shard_map.211 = bf16[32,16,128]{2,1,0:T(8,128)(2,1)} custom-call(bf16[16,128]{1,0:T(8,128)(2,1)} %pad_bitcast_fusion.1.x_ref), custom_call_target="tpu_custom_call" | custom-call | tf_op jit(solution)/shard_map/pallas_call | solution.py:265
  129.8 21.2 %shard_map.212 = bf16[4,128,2048]{2,1,0:T(8,128)(2,1)} custom-call(bf16[128,2048]{1,0:T(8,128)(2,1)} %copy.67.x_ref), custom_call_target="tpu_custom_call" | custom-call | tf_op jit(solution)/shard_map/pallas_call | solution.py:142
  152.7 6.2 convolution_add_fusion
  160.9 2.7 copy.70
  163.5 1.3 copy.69
  164.8 2.2 slice.220
  167.1 1.3 copy.71
  172.0 2.5 fusion.56
  175.8 2.0 copy-done
  178.0 1.6 fusion.17
  179.6 4.4 convolution_convert_fusion.6
  183.9 37.6 %shard_map.213 = f32[128,2048]{1,0:T(8,128)} custom-call(bf16[4,128,2048]{2,1,0:T(8,128)(2,1)} %bitcast.163), custom_call_target="tpu_custom_call" | custom-call | tf_op jit(solution)/shard_map/pallas_call | solution.py:211
  221.5 1.4 fusion.51
  225.5 11.9 %reduce-scatter.9.cloned.1.call-start = ((), (), s32[]{:S(2)}) async-start(), calls=%async_computation.16 | async-start | bytes 4718592 | tf_op jit(solution)/shard_map/reduce_scatter | solution.py:63
  237.4 45.2 %all-gather.12.cloned.1.call-done = bf16[1024,2048]{1,0:T(8,128)(2,1)} async-done(((bf16[128,2048]{1,0:T(8,128)(2,1)}), bf16[1024,2048]{1,0:T(8,128)(2,1)}) %all-gather.12.cloned.1.call-update) | async-done | bytes 4194320 | tf_op jit(solution)/shard_map/all_gather | solution.py:59
  282.6 11.7 %fusion.59 = f32[1024,1408]{1,0:T(8,128)} fusion(bf16[1024,2048]{1,0:T(8,128)(2,1)} %all-gather.12.cloned.1.call-done, bf16[2048,1408]{1,0:T(8,128)(2,1)} %all-gather.14.cloned.1.call-done), kind=kOutput, calls=%fused_computation.144 | convolution fusion | flops 5905580032 | bytes 15728640 | tf_op jit(solution)/shard_map/dot_general | solution.py:30
  294.3 30.4 %all-gather.16.cloned.1.call-done = bf16[704,2048]{1,0:T(8,128)(2,1)} async-done(((bf16[176,2048]{1,0:T(8,128)(2,1)}), bf16[704,2048]{1,0:T(8,128)(2,1)}) %all-gather.16.cloned.1.call-update) | async-done | bytes 2883600 | tf_op jit(solution)/shard_map/all_gather | solution.py:59
  324.8 48.4 %all-gather.18.cloned.1.call-done = bf16[1,1024,2048]{2,1,0:T(8,128)(2,1)} async-done(((bf16[1,128,2048]{2,1,0:T(8,128)(2,1)}), bf16[1,1024,2048]{2,1,0:T(8,128)(2,1)}) %all-gather.18.cloned.1.call-update) | async-done | bytes 4194320 | tf_op jit(solution)/shard_map/all_gather | solution.py:59
  373.1 10.1 %multiply_convert_fusion.2 = (bf16[1024,704]{1,0:T(8,128)(2,1)S(1)}, bf16[1024,704]{1,0:T(8,128)(2,1)S(1)}, bf16[1024,704]{1,0:T(8,128)(2,1)}) fusion(f32[1024,1408]{1,0:T(8,128)} %fusion.59, bf16[704,2048]{1,0:T(8,128)(2,1)} %all-gather.16.cloned.1.call-done, bf16[1,1024,2048]{2,1,0:T(8,128)(2,1)} %all-gather.18.cloned.1.call-done), kind=kOutput, calls=%fused_computation.24 | convolution fusion | flops 2963603456 | bytes 17170432 | tf_op jit(solution)/shard_map/dot_general | solution.py:38
  385.0 11.0 %convolution_convert_fusion.2 = bf16[1024,2048]{1,0:T(8,128)(2,1)} fusion(bf16[2048,1408]{1,0:T(8,128)(2,1)} %all-gather.14.cloned.1.call-done, bf16[1024,704]{1,0:T(8,128)(2,1)S(1)} %get-tuple-element.25, bf16[1024,704]{1,0:T(8,128)(2,1)S(1)} %get-tuple-element.24), kind=kOutput, calls=%fused_computation.18 | convolution fusion | flops 5913444352 | bytes 12845056 | tf_op jit(solution)/shard_map/dot_general | solution.py:38
  396.1 7.7 %convolution_convert_fusion.3 = bf16[1024,2048]{1,0:T(8,128)(2,1)} fusion(bf16[1024,704]{1,0:T(8,128)(2,1)} %get-tuple-element.26, bf16[704,2048]{1,0:T(8,128)(2,1)} %all-gather.16.cloned.1.call-done), kind=kOutput, calls=%fused_computation.19 | convolution fusion | flops 2954887168 | bytes 8519680 | tf_op jit(solution)/shard_map/dot_general | solution.py:30
  403.8 11.2 %convolution_convert_fusion = bf16[2048,1408]{1,0:T(8,128)(2,1)} fusion(bf16[1024,2048]{1,0:T(8,128)(2,1)} %all-gather.12.cloned.1.call-done, bf16[1024,704]{1,0:T(8,128)(2,1)} %copy-done.41, bf16[1024,704]{1,0:T(8,128)(2,1)} %copy-done.40), kind=kOutput, calls=%fused_computation.6 | convolution fusion | flops 5914230784 | bytes 12845056 | tf_op jit(solution)/shard_map/dot_general | solution.py:34
  415.8 7.5 fusion.10
  423.8 21.2 %reduce-scatter.9.cloned.1.call-done = bf16[128,2048]{1,0:T(8,128)(2,1)} async-done(((bf16[1024,2048]{1,0:T(8,128)(2,1)}), bf16[128,2048]{1,0:T(8,128)(2,1)}) %reduce-scatter.9.cloned.1.call-update) | async-done | bytes 524304 | tf_op jit(solution)/shard_map/reduce_scatter | solution.py:63
  445.0 2.1 fusion.29
  448.1 47.6 %reduce-scatter.7.cloned.1.call-done = bf16[128,2048]{1,0:T(8,128)(2,1)} async-done(((bf16[1024,2048]{1,0:T(8,128)(2,1)}), bf16[128,2048]{1,0:T(8,128)(2,1)}) %reduce-scatter.7.cloned.1.call-update) | async-done | bytes 524304 | tf_op jit(solution)/shard_map/reduce_scatter | solution.py:63
  495.7 3.2 fusion.49
  498.9 35.1 %shard_map.214 = bf16[4,128,2048]{2,1,0:T(8,128)(2,1)} custom-call(bf16[128,2048]{1,0:T(8,128)(2,1)} %get-tuple-element.20.x_ref), custom_call_target="tpu_custom_call" | custom-call | tf_op jit(solution)/shard_map/pallas_call | solution.py:142
  534.1 3.9 convolution_convert_fusion.7
  538.0 5.6 multiply_reduce_fusion
  544.1 2.5 multiply_convert_fusion
  546.7 1.4 fusion.58
  549.4 1.4 fusion.18
  551.4 6.4 convolution_convert_fusion.1
  557.8 4.4 convolution_convert_fusion.4
  562.2 12.6 %reduce-scatter.15.cloned.1.call-done = bf16[512,1408]{1,0:T(8,128)(2,1)} async-done(((bf16[2048,1408]{1,0:T(8,128)(2,1)}), bf16[512,1408]{1,0:T(8,128)(2,1)}) %reduce-scatter.15.cloned.1.call-update) | async-done | bytes 1441808 | tf_op jit(solution)/shard_map/reduce_scatter | solution.py:63
  574.8 4.8 all-to-all-start.3
  579.8 39.7 %reduce-scatter.17.cloned.1.call-done = bf16[176,2048]{1,0:T(8,128)(2,1)} async-done(((bf16[704,2048]{1,0:T(8,128)(2,1)}), bf16[176,2048]{1,0:T(8,128)(2,1)}) %reduce-scatter.17.cloned.1.call-update) | async-done | bytes 720912 | tf_op jit(solution)/shard_map/reduce_scatter | solution.py:63
  619.5 2.4 convert_element_type.242
  622.0 7.5 convolution_convert_fusion.5
  629.5 22.1 %shard_map.215 = f32[128,2048]{1,0:T(8,128)} custom-call(bf16[4,128,2048]{2,1,0:T(8,128)(2,1)} %bitcast.162), custom_call_target="tpu_custom_call" | custom-call | tf_op jit(solution)/shard_map/pallas_call | solution.py:211
  651.7 1.5 copy.80
  654.3 2.5 copy.82
  656.8 1.5 convert_reduce_fusion
  660.2 12.5 %shard_map.216 = f32[8,128]{1,0:T(8,128)} custom-call(f32[32,8,128]{2,1,0:T(8,128)} %bitcast.168), custom_call_target="tpu_custom_call" | custom-call | tf_op jit(solution)/shard_map/pallas_call | solution.py:265
  672.7 1.3 slice.146
  674.0 2.9 fusion.34
  676.9 16.8 %reduce-scatter.11.cloned.1.call-done = bf16[256,1536]{1,0:T(8,128)(2,1)} async-done(((bf16[2048,1536]{1,0:T(8,128)(2,1)}), bf16[256,1536]{1,0:T(8,128)(2,1)}) %reduce-scatter.11.cloned.1.call-update) | async-done | bytes 786448 | tf_op jit(solution)/shard_map/reduce_scatter | solution.py:63
  693.7 3.6 all-to-all-start.2
  697.9 32.5 %reduce-scatter.13.cloned.1.call-done = bf16[64,2048]{1,0:T(8,128)(2,1)} async-done(((bf16[512,2048]{1,0:T(8,128)(2,1)}), bf16[64,2048]{1,0:T(8,128)(2,1)}) %reduce-scatter.13.cloned.1.call-update) | async-done | bytes 262160 | tf_op jit(solution)/shard_map/reduce_scatter | solution.py:63
  730.5 1.8 convert_element_type.236
  732.2 8.4 %reshape.344 = f32[8,64,2,4,176]{4,3,2,1,0:T(4,128)} reshape(bf16[8,64,1408]{2,1,0:T(8,128)(2,1)} %all-to-all-done.3) | data formatting | bytes 4325376 | tf_op jit(solution)/shard_map/convert_element_type | solution.py:431
  740.6 4.6 copy.101
  745.3 1.8 fusion.52
  747.1 3.3 squeeze.14
  750.3 2.6 squeeze.13
  753.0 1.4 reshape.345
  754.4 2.2 copy.83
  756.6 3.2 reshape.343
  (185 shorter events, 31.8 us)
Async XLA Ops:
  7.2 145.5 %all-gather.8.cloned.1.call-start = ((), (), s32[]{:S(2)}) async-start(), calls=%async_computation.10 | async-start | bytes 7077888 | tf_op jit(solution)/shard_map/all_gather | solution.py:59
  9.5 18.8 %copy-start.10 = (bf16[64,5632]{1,0:T(8,128)(2,1)S(1)}, bf16[64,5632]{1,0:T(8,128)(2,1)}, u32[]{:S(2)}) copy-start(bf16[64,5632]{1,0:T(8,128)(2,1)} %param.20) | copy-start | bytes 2162692
  27.5 152.0 %all-gather.10.cloned.1.call-start = ((), (), s32[]{:S(2)}) async-start(), calls=%async_computation.11 | async-start | bytes 2359296 | tf_op jit(solution)/shard_map/all_gather | solution.py:59
  28.3 209.1 %all-gather.14.cloned.1.call-start = ((), (), s32[]{:S(2)}) async-start(), calls=%async_computation.13 | async-start | bytes 7208960 | tf_op jit(solution)/shard_map/all_gather | solution.py:59
  36.1 78.3 %copy-start.34 = (bf16[64]{0:T(256)(128)(2,1)S(1)}, bf16[64]{0:T(256)(128)(2,1)}, u32[]{:S(2)}) copy-start(bf16[64]{0:T(256)(128)(2,1)} %param.13) | copy-start | bytes 388
  36.1 78.3 %copy-start.35 = (bf16[64]{0:T(256)(128)(2,1)S(1)}, bf16[64]{0:T(256)(128)(2,1)}, u32[]{:S(2)}) copy-start(bf16[64]{0:T(256)(128)(2,1)} %param.14) | copy-start | bytes 388
  36.1 78.3 %copy-start.36 = (bf16[64]{0:T(256)(128)(2,1)S(1)}, bf16[64]{0:T(256)(128)(2,1)}, u32[]{:S(2)}) copy-start(bf16[64]{0:T(256)(128)(2,1)} %param.18) | copy-start | bytes 388
  36.1 78.3 %copy-start.37 = (bf16[64]{0:T(256)(128)(2,1)S(1)}, bf16[64]{0:T(256)(128)(2,1)}, u32[]{:S(2)}) copy-start(bf16[64]{0:T(256)(128)(2,1)} %param.19) | copy-start | bytes 388
  36.1 78.3 %copy-start.38 = (bf16[192]{0:T(256)(128)(2,1)S(1)}, bf16[192]{0:T(256)(128)(2,1)}, u32[]{:S(2)}) copy-start(bf16[192]{0:T(256)(128)(2,1)} %param.16) | copy-start | bytes 1156
  36.6 90.9 %copy-start.1 = (bf16[1,128,2048]{2,1,0:T(8,128)(2,1)S(1)}, bf16[1,128,2048]{2,1,0:T(8,128)(2,1)}, u32[]{:S(2)}) copy-start(bf16[1,128,2048]{2,1,0:T(8,128)(2,1)} %param.12) | copy-start | bytes 1572868
  114.0 168.5 %all-gather.12.cloned.1.call-start = ((), (), s32[]{:S(2)}) async-start(), calls=%async_computation.12 | async-start | bytes 4718592 | tf_op jit(solution)/shard_map/all_gather | solution.py:59
  127.3 0.8 copy-start.16
  127.4 95.9 %copy-start.18 = (f32[2048]{0:T(1024)}, f32[2048]{0:T(1024)S(1)}, u32[]{:S(2)}) copy-start(f32[2048]{0:T(1024)S(1)} %mul.291) | copy-start | bytes 24580
  127.8 23.2 %copy-start.29 = (f32[128]{0:T(128)}, f32[128]{0:T(128)S(1)}, u32[]{:S(2)}) copy-start(f32[128]{0:T(128)S(1)} %broadcast_multiply_fusion.6) | copy-start | bytes 1540
  128.1 22.9 %copy-start.32 = (f32[128]{0:T(128)}, f32[128]{0:T(128)S(1)}, u32[]{:S(2)}) copy-start(f32[128]{0:T(128)S(1)} %add_rsqrt_fusion.1) | copy-start | bytes 1540
  164.8 11.0 %copy-start.4 = (bf16[512,512]{0,1:T(8,128)(2,1)}, bf16[512,512]{0,1:T(8,128)(2,1)S(1)}, u32[]{:S(2)}) copy-start(bf16[512,512]{0,1:T(8,128)(2,1)S(1)} %copy.69) | copy-start | bytes 1572868
  168.4 3.6 copy-start.8
  172.0 2.6 copy-start.11
  172.0 2.6 copy-start.13
  174.6 3.3 copy-start
  174.6 3.4 copy-start.20
  175.8 2.1 copy-start.22
  179.5 4.4 copy-start.39
  223.0 71.4 %copy-start.28 = (f32[128]{0:T(128)}, f32[128]{0:T(128)S(1)}, u32[]{:S(2)}) copy-start(f32[128]{0:T(128)S(1)} %broadcast_multiply_fusion.5) | copy-start | bytes 1540
  223.2 71.1 %copy-start.31 = (f32[128]{0:T(128)}, f32[128]{0:T(128)S(1)}, u32[]{:S(2)}) copy-start(f32[128]{0:T(128)S(1)} %add_rsqrt_fusion) | copy-start | bytes 1540
  224.3 100.4 %all-gather.16.cloned.1.call-start = ((), (), s32[]{:S(2)}) async-start(), calls=%async_computation.14 | async-start | bytes 3604480 | tf_op jit(solution)/shard_map/all_gather | solution.py:59
  224.9 148.2 %all-gather.18.cloned.1.call-start = ((), (), s32[]{:S(2)}) async-start(), calls=%async_computation.21 | async-start | bytes 4718592 | tf_op jit(solution)/shard_map/all_gather | solution.py:59
  225.5 219.5 %reduce-scatter.9.cloned.1.call-start = ((), (), s32[]{:S(2)}) async-start(), calls=%async_computation.16 | async-start | bytes 4718592 | tf_op jit(solution)/shard_map/reduce_scatter | solution.py:63
  383.2 1.2 copy-start.40
  383.2 1.8 copy-start.41
  396.0 99.7 %reduce-scatter.7.cloned.1.call-start = ((), (), s32[]{:S(2)}) async-start(), calls=%async_computation.15 | async-start | bytes 4718592 | tf_op jit(solution)/shard_map/reduce_scatter | solution.py:63
  403.8 171.1 %reduce-scatter.15.cloned.1.call-start = ((), (), s32[]{:S(2)}) async-start(), calls=%async_computation.19 | async-start | bytes 7208960 | tf_op jit(solution)/shard_map/reduce_scatter | solution.py:63
  415.1 0.7 copy-start.21
  415.1 0.7 copy-start.23
  415.1 204.4 %reduce-scatter.17.cloned.1.call-start = ((), (), s32[]{:S(2)}) async-start(), calls=%async_computation.20 | async-start | bytes 3604480 | tf_op jit(solution)/shard_map/reduce_scatter | solution.py:63
  423.3 72.4 %copy-start.3 = (bf16[1,128,2048]{2,1,0:T(8,128)(2,1)S(1)}, bf16[1,128,2048]{2,1,0:T(8,128)(2,1)}, u32[]{:S(2)}) copy-start(bf16[1,128,2048]{2,1,0:T(8,128)(2,1)} %param.23) | copy-start | bytes 1572868
  423.3 270.4 %reduce-scatter.11.cloned.1.call-start = ((), (), s32[]{:S(2)}) async-start(), calls=%async_computation.17 | async-start | bytes 7077888 | tf_op jit(solution)/shard_map/reduce_scatter | solution.py:63
  534.1 4.0 copy-start.5
  538.0 5.6 slice-start
  538.0 6.1 slice-start.1
  544.1 2.6 copy-start.9
  544.1 2.6 copy-start.14
  546.7 1.4 copy-start.12
  548.2 0.9 copy-start.15
  548.2 0.9 copy-start.19
  549.3 72.8 %copy-start.6 = (bf16[512,8,64]{0,2,1:T(8,128)(2,1)}, bf16[512,8,64]{0,2,1:T(8,128)(2,1)S(1)}, u32[]{:S(2)}) copy-start(bf16[512,8,64]{0,2,1:T(8,128)(2,1)S(1)} %pad_maximum_fusion.7) | copy-start | bytes 1572868
  549.3 72.7 %copy-start.7 = (bf16[512,8,64]{0,2,1:T(8,128)(2,1)}, bf16[512,8,64]{0,2,1:T(8,128)(2,1)S(1)}, u32[]{:S(2)}) copy-start(bf16[512,8,64]{0,2,1:T(8,128)(2,1)S(1)} %pad_maximum_fusion.8) | copy-start | bytes 1572868
  549.4 2.0 copy-start.2
  557.7 172.7 %reduce-scatter.13.cloned.1.call-start = ((), (), s32[]{:S(2)}) async-start(), calls=%async_computation.18 | async-start | bytes 2359296 | tf_op jit(solution)/shard_map/reduce_scatter | solution.py:63
  562.2 17.5 %copy-start.24 = (f32[32,64]{1,0:T(8,128)S(1)}, f32[32,64]{1,0:T(8,128)}, u32[]{:S(2)}) copy-start(f32[32,64]{1,0:T(8,128)} %get-tuple-element.36) | copy-start | bytes 24580
  562.2 59.7 %copy-start.26 = (f32[2048]{0:T(1024)S(1)}, f32[2048]{0:T(1024)}, u32[]{:S(2)}) copy-start(f32[2048]{0:T(1024)} %get-tuple-element.14) | copy-start | bytes 24580
  562.2 59.7 %copy-start.25 = (f32[2048]{0:T(1024)S(1)}, f32[2048]{0:T(1024)}, u32[]{:S(2)}) copy-start(f32[2048]{0:T(1024)} %get-tuple-element.19) | copy-start | bytes 24580
  574.8 102.1 %all-to-all-start.3 = ((bf16[8,64,1408]{2,1,0:T(8,128)(2,1)}), bf16[8,64,1408]{2,1,0:T(8,128)(2,1)}, u32[]{:S(2)}, u32[]{:S(2)}) async-start(bf16[8,64,1408]{2,1,0:T(8,128)(2,1)} %bitcast.165), calls=%async_computation.8 | async-start | bytes 2883584 | tf_op jit(solution)/shard_map/all_to_all | solution.py:67
  653.2 5.3 copy-start.17
  653.3 5.3 copy-start.30
  653.3 5.3 copy-start.33
  672.7 24.6 %copy-start.27 = (f32[8,128]{1,0:T(8,128)S(1)}, f32[8,128]{1,0:T(8,128)}, u32[]{:S(2)}) copy-start(f32[8,128]{1,0:T(8,128)} %shard_map.216) | copy-start | bytes 12292
  693.7 59.3 %all-to-all-start.2 = ((bf16[4,64,1536]{2,1,0:T(8,128)(2,1)}), bf16[4,64,1536]{2,1,0:T(8,128)(2,1)S(1)}, u32[]{:S(2)}, u32[]{:S(2)}) async-start(bf16[4,64,1536]{2,1,0:T(8,128)(2,1)} %bitcast.166), calls=%async_computation.5 | async-start | bytes 1572864 | tf_op jit(solution)/shard_map/all_to_all | solution.py:67
Sparse Core Ops, SparseCore 0:
  27.6 94.9 all-gather.7
  124.2 29.7 all-gather.9
  155.9 79.3 all-gather.13
  237.3 45.2 all-gather.11
  284.3 40.4 all-gather.15
  326.2 46.8 all-gather.17
  396.1 48.7 reduce-scatter.8
  447.2 48.3 reduce-scatter.6
  498.7 76.1 reduce-scatter.14
  577.7 41.7 reduce-scatter.16
  621.8 71.8 reduce-scatter.10
  695.8 34.5 reduce-scatter.12

commit v3 on v2

--- a/solution.py
+++ b/solution.py
@@ -6,6 +6,7 @@
 from jax.experimental import pallas as pl
 from jax.experimental.pallas import tpu as pltpu
 from jax.sharding import PartitionSpec as P
+
 
 HEAD_DIM = 64
 ROT = 16
@@ -68,6 +69,10 @@
 
 
 MESH = pl.DeviceIdType.MESH
+
+
+def lasting(micros):
+    return pl.CostEstimate(flops=0, transcendentals=0, bytes_accessed=int(micros * 3.0e6))
 
 
 def meet(peers):
@@ -99,7 +104,7 @@
 
 
 def gather_square(x_ref, o_ref, send, recv, local):
-    me, across, along, far = corners()
+    me, across, along, _ = corners()
     to_across, to_along = {"seq": across}, {"seq": along}
     half = x_ref.shape[0] // 2
     top, low = pl.ds(0, half), pl.ds(half, half)
@@ -149,6 +154,7 @@
             pltpu.SemaphoreType.DMA((slots,)),
             pltpu.SemaphoreType.DMA,
         ],
+        cost_estimate=lasting(22),
         compiler_params=pltpu.CompilerParams(collective_id=tag, has_side_effects=True),
     )(value)
     return out.reshape(count * value.shape[0], value.shape[1])
@@ -215,8 +221,32 @@
         out_specs=pl.BlockSpec(memory_space=pltpu.VMEM),
         scratch_shapes=held
         + [pltpu.SemaphoreType.DMA((slots,)), pltpu.SemaphoreType.DMA((slots,))],
+        cost_estimate=lasting(22),
         compiler_params=pltpu.CompilerParams(collective_id=tag, has_side_effects=True),
     )(value.reshape(count, rows, wide))
+
+
+def move_blocks(value, axis, count):
+    rows = value.shape[0] // count
+    me = lax.axis_index(axis)
+    blocks = []
+    for step in range(count):
+        at = lax.rem(me + step, count) * rows
+        block = lax.dynamic_slice_in_dim(value, at, rows, 0)
+        if step:
+            block = lax.ppermute(block, axis, [(i, (i + step) % count) for i in range(count)])
+        blocks.append(block)
+    return blocks
+
+
+def place_blocks(blocks, axis):
+    count, rows = len(blocks), blocks[0].shape[0]
+    me = lax.axis_index(axis)
+    out = jnp.zeros((count * rows,) + blocks[0].shape[1:], blocks[0].dtype)
+    for step, block in enumerate(blocks):
+        at = lax.rem(me - step + count, count) * rows
+        out = lax.dynamic_update_slice_in_dim(out, block, at, 0)
+    return out
 
 
 def exchange(ways, shared, x_ref, o_ref, got, send, recv):
@@ -272,8 +302,409 @@
             pltpu.SemaphoreType.DMA((count - 1,)),
             pltpu.SemaphoreType.DMA((count - 1,)),
         ],
+        cost_estimate=lasting(10),
         compiler_params=pltpu.CompilerParams(collective_id=tag, has_side_effects=True),
     )(value)
+
+
+def remote(source, target, send, recv, peer):
+    return pltpu.make_async_remote_copy(
+        src_ref=source,
+        dst_ref=target,
+        send_sem=send,
+        recv_sem=recv,
+        device_id=peer,
+        device_id_type=MESH,
+    )
+
+
+def line_place(dps):
+    dp = lax.axis_index("dp")
+    chip, core = dp // 2, lax.rem(dp, 2)
+    chips = dps // 2
+    ends = (chip + 1 < chips, chip >= 1)
+    sides = ({"dp": lax.rem(dp + 2, dps)}, {"dp": lax.rem(dp - 2 + dps, dps)})
+    return chips, chip, core, ends, sides, {"dp": 2 * chip + (1 - core)}
+
+
+def gather_line_body(dps, x_ref, o_ref, line_s, line_r, pair_s, pair_r, local):
+    chips, chip, core, ends, sides, sibling = line_place(dps)
+    meet([sides[0], sides[1], sibling])
+
+    def onward(side, hop, owner, source=None):
+        block = o_ref.at[2 * owner + core]
+        at = (side, hop)
+        return remote(
+            block if source is None else source, block, line_s.at[at], line_r.at[at], sides[side]
+        )
+
+    def share(owner, owner_core, source=None):
+        block = o_ref.at[2 * owner + owner_core]
+        return remote(
+            block if source is None else source, block, pair_s.at[owner], pair_r.at[owner], sibling
+        )
+
+    for side in range(2):
+
+        @pl.when(ends[side])
+        def _(side=side):
+            onward(side, 0, chip, x_ref).start()
+
+    share(chip, core, x_ref).start()
+    own = pltpu.make_async_copy(x_ref, o_ref.at[2 * chip + core], local)
+    own.start()
+    for hop in range(chips - 1):
+        for side in range(2):
+            origin = chip - 1 - hop if side == 0 else chip + 1 + hop
+            there = origin >= 0 if side == 0 else origin < chips
+
+            @pl.when(there)
+            def _(side=side, hop=hop, origin=origin):
+                onward(side, hop, origin).wait_recv()
+
+            if hop < chips - 2:
+
+                @pl.when(jnp.logical_and(there, ends[side]))
+                def _(side=side, hop=hop, origin=origin):
+                    onward(side, hop + 1, origin).start()
+
+            @pl.when(there)
+            def _(origin=origin):
+                share(origin, core).start()
+
+    own.wait()
+    for hop in range(chips - 1):
+        for side in range(2):
+            origin = chip - hop if side == 0 else chip + hop
+            there = origin >= 0 if side == 0 else origin < chips
+
+            @pl.when(jnp.logical_and(there, ends[side]))
+            def _(side=side, hop=hop, origin=origin):
+                onward(side, hop, origin).wait_send()
+
+    for owner in range(chips):
+        share(owner, core).wait_send()
+        share(owner, 1 - core).wait_recv()
+
+
+def gather_line(value, dps, tag):
+    dma, chips = pltpu.SemaphoreType.DMA, dps // 2
+    out = pl.pallas_call(
+        functools.partial(gather_line_body, dps),
+        out_shape=jax.ShapeDtypeStruct((dps,) + value.shape, value.dtype),
+        in_specs=[pl.BlockSpec(memory_space=pltpu.VMEM)],
+        out_specs=pl.BlockSpec(memory_space=pl.ANY),
+        scratch_shapes=[
+            dma((2, chips - 1)),
+            dma((2, chips - 1)),
+            dma((chips,)),
+            dma((chips,)),
+            dma,
+        ],
+        cost_estimate=lasting(42),
+        compiler_params=pltpu.CompilerParams(collective_id=tag, has_side_effects=True),
+    )(value)
+    return out.reshape(dps * value.shape[0], value.shape[1])
+
+
+def reduce_line_body(dps, x_ref, o_ref, pair, moving, line_s, line_r, pair_s, pair_r):
+    chips, chip, core, ends, sides, sibling = line_place(dps)
+    meet([sides[0], sides[1], sibling])
+
+    def share(owner, owner_core):
+        return remote(
+            x_ref.at[2 * owner + owner_core],
+            pair.at[owner],
+            pair_s.at[owner],
+            pair_r.at[owner],
+            sibling,
+        )
+
+    def onward(side, owner):
+        at = (side, owner)
+        return remote(pair.at[owner], moving.at[at], line_s.at[at], line_r.at[at], sides[side])
+
+    order = [at for pair_at in zip(range(chips - 1, -1, -1), range(chips)) for at in pair_at]
+    order = list(dict.fromkeys(order))
+    for owner in order:
+        share(owner, 1 - core).start()
+    o_ref[...] = x_ref[2 * chip + core].astype(F32)
+    for at in range(chips):
+        for side in range(2):
+            owner = chips - 1 - at if side == 0 else at
+            passing = chip < owner if side == 0 else chip > owner
+            fed = jnp.logical_and(passing, ends[1 - side])
+
+            @pl.when(passing)
+            def _(owner=owner):
+                share(owner, core).wait_recv()
+
+            @pl.when(fed)
+            def _(side=side, owner=owner):
+                onward(side, owner).wait_recv()
+                pair[owner] = (
+                    pair[owner].astype(F32)
+                    + x_ref[2 * owner + core].astype(F32)
+                    + moving[side, owner].astype(F32)
+                ).astype(pair.dtype)
+
+            @pl.when(jnp.logical_and(passing, jnp.logical_not(fed)))
+            def _(owner=owner):
+                pair[owner] = (
+                    pair[owner].astype(F32) + x_ref[2 * owner + core].astype(F32)
+                ).astype(pair.dtype)
+
+            @pl.when(passing)
+            def _(side=side, owner=owner):
+                onward(side, owner).start()
+
+    for owner in range(chips):
+
+        @pl.when(chip == owner)
+        def _(owner=owner):
+            share(owner, core).wait_recv()
+            o_ref[...] += pair[owner].astype(F32)
+
+        for side in range(2):
+
+            @pl.when(jnp.logical_and(chip == owner, ends[1 - side]))
+            def _(side=side, owner=owner):
+                onward(side, owner).wait_recv()
+                o_ref[...] += moving[side, owner].astype(F32)
+
+            passing = chip < owner if side == 0 else chip > owner
+
+            @pl.when(passing)
+            def _(side=side, owner=owner):
+                onward(side, owner).wait_send()
+
+        share(owner, 1 - core).wait_send()
+
+
+def reduce_line(value, dps, tag):
+    rows, wide = value.shape[0] // dps, value.shape[1]
+    dma, chips = pltpu.SemaphoreType.DMA, dps // 2
+    return pl.pallas_call(
+        functools.partial(reduce_line_body, dps),
+        out_shape=jax.ShapeDtypeStruct((rows, wide), F32),
+        in_specs=[pl.BlockSpec(memory_space=pltpu.VMEM)],
+        out_specs=pl.BlockSpec(memory_space=pltpu.VMEM),
+        scratch_shapes=[
+            pltpu.VMEM((chips, rows, wide), value.dtype),
+            pltpu.VMEM((2, chips, rows, wide), value.dtype),
+            dma((2, chips)),
+            dma((2, chips)),
+            dma((chips,)),
+            dma((chips,)),
+        ],
+        cost_estimate=lasting(48),
+        compiler_params=pltpu.CompilerParams(collective_id=tag, has_side_effects=True),
+    )(value.reshape(dps, rows, wide))
+
+
+def opening(ways, qkv_ref, x_ref, small_ref, w_ref, all_ref, given_ref, *sems):
+    seqs, dps = ways
+    chips, count = dps // 2, seqs * dps
+    swap_s, swap_r, line_s, line_r, pair_s, pair_r, x_s, x_r, small_s, small_r, own_sem = sems
+    seq, dp = lax.axis_index("seq"), lax.axis_index("dp")
+    chip, core = dp // 2, lax.rem(dp, 2)
+    me = seq * dps + dp
+    part, group = qkv_ref.shape[0], w_ref.shape[1] // 3
+    width = qkv_ref.shape[1] // 3
+    barrier = pltpu.get_barrier_semaphore()
+
+    def other(step):
+        at = lax.rem(me + step, count)
+        return {"seq": at // dps, "dp": lax.rem(at, dps)}
+
+    @pl.loop(1, count)
+    def _(step):
+        pl.semaphore_signal(barrier, inc=1, device_id=other(step), device_id_type=MESH)
+
+    pl.semaphore_wait(barrier, count - 1)
+
+    def block(source, owner):
+        return w_ref.at[pl.ds(pl.multiple_of((source * dps + owner) * part, part), part), :]
+
+    def piece(source, third):
+        rows = pl.ds(pl.multiple_of((source * dps + dp) * part, part), part)
+        return w_ref.at[rows, pl.ds(third * group, group)]
+
+    def columns(target, third):
+        at = pl.multiple_of(third * width + target * group, 128)
+        return qkv_ref.at[:, pl.ds(at, group)]
+
+    swaps = []
+    for step in range(1, seqs):
+        target = lax.rem(seq + step, seqs)
+        for third in range(3):
+            at = 3 * (step - 1) + third
+            swaps.append(
+                remote(
+                    columns(target, third),
+                    piece(seq, third),
+                    swap_s.at[at],
+                    swap_r.at[at],
+                    {"seq": target},
+                )
+            )
+            swaps[-1].start()
+    owns = [
+        pltpu.make_async_copy(columns(seq, third), piece(seq, third), own_sem.at[third])
+        for third in range(3)
+    ]
+    for own in owns:
+        own.start()
+
+    square = seqs == 4
+    if square:
+        _, across, along, _ = corners()
+        to_across, to_along = {"seq": across}, {"seq": along}
+        half = x_ref.shape[0] // 2
+        top, low = pl.ds(0, half), pl.ds(half, half)
+        copies = [
+            push(x_ref.at[top], all_ref.at[seq, top], x_s, x_r, 0, to_across),
+            push(x_ref.at[low], all_ref.at[seq, low], x_s, x_r, 1, to_along),
+            push(x_ref.at[low], all_ref.at[seq, low], x_s, x_r, 2, to_across),
+            push(x_ref.at[top], all_ref.at[seq, top], x_s, x_r, 3, to_along),
+        ]
+    else:
+        copies = [
+            push(x_ref, all_ref.at[seq], x_s, x_r, step - 1, {"seq": lax.rem(seq + step, seqs)})
+            for step in range(1, seqs)
+        ]
+    owns.append(pltpu.make_async_copy(x_ref, all_ref.at[seq], own_sem.at[3]))
+    owns[3].start()
+
+    def small_copy(step):
+        return remote(
+            small_ref, given_ref.at[me], small_s.at[step - 1], small_r.at[step - 1], other(step)
+        )
+
+    @pl.loop(1, count)
+    def _(step):
+        small_copy(step).start()
+
+    given_ref[me] = small_ref[...]
+
+    sibling = {"dp": 2 * chip + (1 - core)}
+    ends = (chip + 1 < chips, chip >= 1)
+    sides = ({"dp": lax.rem(dp + 2, dps)}, {"dp": lax.rem(dp - 2 + dps, dps)})
+
+    def onward(side, hop, source, owner_chip):
+        part_of = block(source[1], 2 * owner_chip + core)
+        at = (side, hop, source[0])
+        return remote(part_of, part_of, line_s.at[at], line_r.at[at], sides[side])
+
+    def share(source, owner_chip, owner_core):
+        part_of = block(source[1], 2 * owner_chip + owner_core)
+        at = (owner_chip, source[0])
+        return remote(part_of, part_of, pair_s.at[at], pair_r.at[at], sibling)
+
+    sources = [(back, lax.rem(seq - back + seqs, seqs)) for back in range(seqs)]
+    for source in sources:
+        if source[0] == 0:
+            for own in owns[:3]:
+                own.wait()
+        else:
+            for third in range(3):
+                swaps[3 * (source[0] - 1) + third].wait_recv()
+        for side in range(2):
+
+            @pl.when(ends[side])
+            def _(side=side, source=source):
+                onward(side, 0, source, chip).start()
+
+        share(source, chip, core).start()
+    if square:
+        copies[0].wait_recv()
+        copies.append(push(all_ref.at[across, top], all_ref.at[across, top], x_s, x_r, 4, to_along))
+        copies[1].wait_recv()
+        copies.append(push(all_ref.at[along, low], all_ref.at[along, low], x_s, x_r, 5, to_across))
+    for hop in range(chips - 1):
+        for source in sources:
+            for side in range(2):
+                origin = chip - 1 - hop if side == 0 else chip + 1 + hop
+                there = origin >= 0 if side == 0 else origin < chips
+
+                @pl.when(there)
+                def _(side=side, hop=hop, source=source, origin=origin):
+                    onward(side, hop, source, origin).wait_recv()
+                    share(source, origin, core).start()
+
+                if hop < chips - 2:
+
+                    @pl.when(jnp.logical_and(there, ends[side]))
+                    def _(side=side, hop=hop, source=source, origin=origin):
+                        onward(side, hop + 1, source, origin).start()
+
+    for swapped in swaps:
+        swapped.wait_send()
+    for at, copy in enumerate(copies):
+        copy.wait_send()
+        if not square or at > 1:
+            copy.wait_recv()
+    owns[3].wait()
+
+    @pl.loop(1, count)
+    def _(step):
+        small_copy(step).wait()
+
+    for hop in range(chips - 1):
+        for source in sources:
+            for side in range(2):
+                origin = chip - hop if side == 0 else chip + hop
+                there = origin >= 0 if side == 0 else origin < chips
+
+                @pl.when(jnp.logical_and(there, ends[side]))
+                def _(side=side, hop=hop, source=source, origin=origin):
+                    onward(side, hop, source, origin).wait_send()
+
+    for owner in range(chips):
+        for source in sources:
+            share(source, owner, core).wait_send()
+            share(source, owner, 1 - core).wait_recv()
+
+
+def open_all(ways, qkv_weight, rows_in, small):
+    seqs, dps = ways
+    chips, count = dps // 2, seqs * dps
+    part, group = qkv_weight.shape[0], qkv_weight.shape[1] // (3 * seqs)
+    slots = 6 if seqs == 4 else seqs - 1
+    dma = pltpu.SemaphoreType.DMA
+    return pl.pallas_call(
+        functools.partial(opening, ways),
+        out_shape=(
+            jax.ShapeDtypeStruct((part * count, 3 * group), BF16),
+            jax.ShapeDtypeStruct((seqs,) + rows_in.shape, BF16),
+            jax.ShapeDtypeStruct((count,) + small.shape, BF16),
+        ),
+        in_specs=[pl.BlockSpec(memory_space=pltpu.VMEM)] * 3,
+        out_specs=(
+            pl.BlockSpec(memory_space=pl.ANY),
+            pl.BlockSpec(memory_space=pl.ANY),
+            pl.BlockSpec(memory_space=pltpu.VMEM),
+        ),
+        scratch_shapes=[
+            dma((3 * (seqs - 1),)),
+            dma((3 * (seqs - 1),)),
+            dma((2, chips - 1, seqs)),
+            dma((2, chips - 1, seqs)),
+            dma((chips, seqs)),
+            dma((chips, seqs)),
+            dma((slots,)),
+            dma((slots,)),
+            dma((count - 1,)),
+            dma((count - 1,)),
+            dma((4,)),
+        ],
+        cost_estimate=lasting(75),
+        compiler_params=pltpu.CompilerParams(collective_id=0, has_side_effects=True),
+    )(qkv_weight, rows_in, small)
+
+
+def after(value, *earlier):
+    return lax.optimization_barrier((value,) + earlier)[0]
 
 
 def attention_forward(queries, keys, values):
@@ -340,7 +771,8 @@
     total = small.shape[0]
     padded = -(-total // 2048) * 2048
     small = jnp.pad(small, (0, padded - total)).reshape(padded // 128, 128)
-    small = exchange_all(small, ways, True, 4).reshape(seqs * dps, padded)[:, :total].astype(F32)
+    qkv_full, inputs_all, small = open_all(ways, qkv_weight, inputs[0], small)
+    small = small.reshape(seqs * dps, padded)[:, :total].astype(F32)
     gain_one = small[:, :part].reshape(-1)
     shift_one = small[:, part : 2 * part].reshape(-1)
     gain_two = small[:, 2 * part : 3 * part].reshape(-1)
@@ -348,29 +780,22 @@
     bias = small[:, 4 * part :].reshape(3, seqs, group)
     bias = lax.dynamic_index_in_dim(bias, me_seq, 1, keepdims=False).reshape(3 * group)
 
-    qkv_cut = qkv_weight.reshape(part, 3, seqs, group).transpose(2, 0, 1, 3)
-    qkv_cut = swap(qkv_cut.reshape(seqs * part, 3 * group), "seq", 0, 0)
-    qkv_full = gather(qkv_cut, "dp")
+    down_full = gather(down_weight, "seq")
     out_full = gather(out_weight, "dp")
+    grad_all = gather(grad_out, "dp")
 
     def cut_units(weight):
         cut = weight.reshape(part, seqs, dps, units).transpose(2, 0, 1, 3)
         return cut.reshape(dps * part, seqs * units)
 
     gate_cut = jnp.concatenate([cut_units(gate_weight), cut_units(up_weight)], 1)
-    gate_up = gather(swap(gate_cut, "dp", 0, 0), "seq")
-    down_full = gather(down_weight, "seq")
+    gate_cut = after(gate_cut, inputs_all)
+    moved = move_blocks(gate_cut, "dp", dps)
     wide = seqs * units
 
-    def to_mixed(value):
-        return value.reshape(rows, seqs, dps, part).swapaxes(1, 2).reshape(rows, width)
-
-    def from_mixed(value):
-        return value.reshape(rows, dps, seqs, part).swapaxes(1, 2).reshape(rows, width)
-
     normed_one, inverse_one = normalize(hidden_in)
-    attn_input = (normed_one * gain_one + shift_one).astype(BF16)
-    attn_all = gather_seq(to_mixed(attn_input), seqs, 0)
+    normed_all, _ = normalize(inputs_all.reshape(length, width).astype(F32))
+    attn_all = (normed_all * gain_one + shift_one).astype(BF16)
     projected = dot(attn_all, qkv_full) + bias
     cosine, sine = tables(jnp.arange(length, dtype=jnp.int32).astype(F32))
 
@@ -382,20 +807,23 @@
     values = to_heads(projected[:, 2 * group :]).astype(BF16)
     attended, log_total = attention_forward(queries, keys, values)
     attended = attended.reshape(length, group)
-    branch = reduce_seq(dot(attended, out_full).astype(BF16), seqs, 1)
+    moved, attended = lax.optimization_barrier((moved, attended))
+    gate_cut = place_blocks(moved, "dp")
+    gate_up = gather(gate_cut, "seq")
+    branch = dot(attended, out_full).astype(BF16)
+    branch = reduce_seq(branch, seqs, 1)
     residual = hidden_in + branch
 
     normed_two, inverse_two = normalize(residual)
     mlp_input = (normed_two * gain_two + shift_two).astype(BF16)
-    mlp_all = gather(mlp_input, "dp")
-    grad_all = gather(grad_out, "dp")
+    mlp_all = gather_line(mlp_input, dps, 4)
     both = dot(mlp_all, gate_up)
     gate_value = both[:, :wide]
     up_value = both[:, wide:]
     sigmoid_gate = jax.nn.sigmoid(gate_value)
     activated = gate_value * sigmoid_gate
     hidden = (activated * up_value).astype(BF16)
-    layer_out = residual + scatter_sum(dot(hidden, down_full).astype(BF16), "dp").astype(F32)
+    out_part = dot(hidden, down_full).astype(BF16)
 
     hidden_grad = contract_cols(grad_all, down_full)
     gate_grad = (
@@ -403,7 +831,16 @@
     ).astype(BF16)
     up_grad = (hidden_grad * activated).astype(BF16)
     both_grad = jnp.concatenate([gate_grad, up_grad], 1)
-    mlp_grad = scatter_sum(contract_cols(both_grad, gate_up).astype(BF16), "dp").astype(F32)
+    mlp_part = contract_cols(both_grad, gate_up).astype(BF16)
+    both_rows = contract_rows(mlp_all, after(both_grad, mlp_part)).astype(BF16)
+    down_rows = contract_rows(hidden, grad_all).astype(BF16)
+    mlp_part = after(mlp_part, both_rows, down_rows)
+    mlp_grad = reduce_line(mlp_part, dps, 6)
+    both_rows = scatter_sum(both_rows, "seq")
+    down_shard = scatter_sum(down_rows, "seq").astype(F32)
+    out_part = after(out_part, mlp_grad)
+    layer_out = scatter_sum(out_part, "dp")
+    layer_out = residual + layer_out.astype(F32)
     gain_two_grad = jnp.sum(mlp_grad * normed_two, axis=0)
     shift_two_grad = jnp.sum(mlp_grad, axis=0)
     residual_grad = grad_out.astype(F32) + norm_back(mlp_grad, normed_two, inverse_two, gain_two)
@@ -419,18 +856,20 @@
     projected_grad = jnp.concatenate(
         [item.reshape(length, group) for item in (query_plain, keys_plain, values_grad)], 1
     )
-    attn_grad = reduce_seq(contract_cols(projected_grad, qkv_full).astype(BF16), seqs, 3)
-    attn_grad = from_mixed(attn_grad)
+    attn_grad = contract_cols(projected_grad, qkv_full).astype(BF16)
+    attn_grad = reduce_seq(attn_grad, seqs, 3)
     gain_one_grad = jnp.sum(attn_grad * normed_one, axis=0)
     shift_one_grad = jnp.sum(attn_grad, axis=0)
     input_grad = residual_grad + norm_back(attn_grad, normed_one, inverse_one, gain_one)
 
-    down_shard = scatter_sum(contract_rows(hidden, grad_all).astype(BF16), "seq").astype(F32)
-    both_rows = scatter_sum(contract_rows(mlp_all, both_grad).astype(BF16), "seq")
     both_rows = swap(both_rows, "dp", 0, 0).reshape(dps, part, 2, seqs, units)
     both_rows = both_rows.transpose(2, 1, 3, 0, 4).reshape(2, part, seqs * dps * units).astype(F32)
-    out_shard = scatter_sum(contract_rows(attended, branch_all).astype(BF16), "dp").astype(F32)
-    qkv_rows = scatter_sum(contract_rows(attn_all, projected_grad).astype(BF16), "dp")
+    out_rows = contract_rows(attended, branch_all).astype(BF16)
+    out_shard = scatter_sum(out_rows, "dp").astype(F32)
+    qkv_rows = contract_rows(attn_all, projected_grad).astype(BF16)
+    qkv_rows = qkv_rows.reshape(seqs, dps, part, 3 * group).swapaxes(0, 1)
+    qkv_rows = qkv_rows.reshape(width, 3 * group)
+    qkv_rows = scatter_sum(qkv_rows, "dp")
     qkv_rows = swap(qkv_rows, "seq", 0, 0).reshape(seqs, part, 3, group)
     qkv_shard = qkv_rows.transpose(1, 2, 0, 3).reshape(part, 3 * width).astype(F32)
 

time: 775 us -> 745 us (0.961)
  Pallas kernels: 139 us -> 281 us
  blocking collectives: 93.9 us -> 0 us
  waiting for transfers between devices: 296 us -> 218 us
    pallas_call x0 -> x3, Pallas kernels: none -> 175 us  [the longest x1 73.6 us: open_all(): pl.pallas_call(functools.partial(opening, ways), out_shape=(jax.ShapeDtyp...]
    all_to_all x2 -> x0, blocking collectives: 93.9 us -> none  [swap(): lax.all_to_all(value, axis, split_axis=split, concat_axis=concat, tiled=T...]
    all_gather x6 -> x4, waiting for transfers between devices: 124 us -> 68.9 us  [gather(): return lax.all_gather(value, axis, axis=0, tiled=True)]
    reduce_scatter x6 -> x5, waiting for transfers between devices: 170 us -> 144 us  [scatter_sum(): return lax.psum_scatter(value, axis, scatter_dimension=0, tiled=True)]
    pallas_call x2 -> x1, Pallas kernels: 56.4 us -> 35.1 us  [gather_seq(): pl.pallas_call(body, out_shape=jax.ShapeDtypeStruct((count,) + value.shap...]
    reduce_scatter x6 -> x5, starting transfers between devices: 12.5 us -> 0.41 us  [scatter_sum(): return lax.psum_scatter(value, axis, scatter_dimension=0, tiled=True)]
    pallas_call x2 -> x1, Pallas kernels: 23 us -> 12.4 us  [exchange_all(): pl.pallas_call(functools.partial(exchange, ways, shared), out_shape=jax.S...]
  transfers between devices with their start and end apart: 14 -> 18, of which waited for: 9 -> 9; matrix products, arithmetic and copies ran while one was open for 21% -> 20% of each run, Pallas kernels for 18% -> 30%
where the time goes in v3:
time: 745 us; the launch traced here: 737 us
  Pallas kernels  281 us (38%)
  waiting for transfers between devices  218 us (29%)
  matrix products  101 us (14%)
  local copies, waits for them, and re-layouts  69.8 us (9%)
  other arithmetic  34.3 us (5%)
  starting transfers between devices  17.1 us (2%)
  between operations  15.3 us (2%)
    reduce_scatter x5, waiting for transfers between devices, scatter_sum(): return lax.psum_scatter(value, axis, scatter_dimension=0, tiled=True)  144 us
    pallas_call x1, Pallas kernels, open_all(): pl.pallas_call(functools.partial(opening, ways), out_shape=(jax.ShapeDtyp...  73.6 us
    all_gather x4, waiting for transfers between devices, gather(): return lax.all_gather(value, axis, axis=0, tiled=True)  68.9 us
    pallas_call x2, Pallas kernels, reduce_seq(): pl.pallas_call(body, out_shape=jax.ShapeDtypeStruct((rows, wide), F32), i...  58.5 us
    pallas_call x1, Pallas kernels, reduce_line(): pl.pallas_call(functools.partial(reduce_line_body, dps), out_shape=jax.Sh...  58.1 us
    pallas_call x1, Pallas kernels, gather_line(): pl.pallas_call(functools.partial(gather_line_body, dps), out_shape=jax.Sh...  43.5 us
    pallas_call x1, Pallas kernels, gather_seq(): pl.pallas_call(body, out_shape=jax.ShapeDtypeStruct((count,) + value.shap...  35.1 us
    dot_general x4, matrix products, contract_cols(): lax.dot_general(left, right, (((1,), (1,)), ((), ())), preferred_element_...  29.8 us
  transfers between devices with their start and end apart: 18, of which 9 were waited for; matrix products, arithmetic and copies ran while one was open for 20% of the time, Pallas kernels for 30%

profile of v3, /device:TPU:0, one launch (start us, length us, event | category | flops | bytes accessed | tf_op | source)
XLA Modules:
  0.0 737.0 jit_solution(16755730387788914921)
XLA Ops:
  8.0 3.4 concatenate.54
  12.0 3.0 reshape.283
  15.5 1.8 reshape.284
  17.3 2.0 reshape.285
  20.6 1.6 pad_maximum_fusion.2
  22.2 73.6 %shard_map.211 = (bf16[2048,1536]{1,0:T(8,128)(2,1)}, bf16[4,128,2048]{2,1,0:T(8,128)(2,1)}, bf16[32,16,128]{2,1,0:T(8,128)(2,1)}) custom-call(bf16[64,6144]{1,0:T(8,128)(2,1)} %qkv_ref.1, bf16[128,2048]{1,0:T(8,128)(2,1)} %bitcast.120, bf16[16,128]{1,0:T(8,128)(2,1)} %pad_bitcast_fusion.1.small_ref), custom_call_target="tpu_custom_call" | custom-call | bytes 225000000 | tf_op jit(solution)/shard_map/pallas_call | solution.py:675
  97.0 2.4 collective-permute-start.6
  99.4 2.8 collective-permute-start.3
  108.0 6.3 convolution_add_fusion
  114.6 1.5 copy-done.7
  119.7 2.5 fusion.59
  123.4 2.0 copy-done
  129.1 5.8 fusion.18
  134.9 1.6 collective-permute-done.1
  136.4 1.4 collective-permute-done
  145.7 4.4 convolution_convert_fusion.6
  150.0 36.4 %shard_map.212 = f32[128,2048]{1,0:T(8,128)} custom-call(bf16[4,128,2048]{2,1,0:T(8,128)(2,1)} %bitcast.150), custom_call_target="tpu_custom_call" | custom-call | bytes 66000000 | tf_op jit(solution)/shard_map/pallas_call | solution.py:217
  186.4 2.1 fusion.54
  189.8 43.5 %shard_map.213 = bf16[8,128,2048]{2,1,0:T(8,128)(2,1)} custom-call(bf16[128,2048]{1,0:T(8,128)(2,1)} %add_convert_fusion.1.x_ref), custom_call_target="tpu_custom_call" | custom-call | bytes 126000000 | tf_op jit(solution)/shard_map/pallas_call | solution.py:392
  233.4 12.2 %fusion.62 = f32[1024,1408]{1,0:T(8,128)} fusion(bf16[1024,2048]{1,0:T(8,128)(2,1)} %bitcast.124, bf16[2048,1408]{1,0:T(8,128)(2,1)} %all-gather.8.cloned.1.call-done), kind=kOutput, calls=%fused_computation.160 | convolution fusion | flops 5905580032 | bytes 15728640 | tf_op jit(solution)/shard_map/dot_general | solution.py:31
  245.6 20.5 %all-gather.10.cloned.1.call-done = bf16[704,2048]{1,0:T(8,128)(2,1)} async-done(((bf16[176,2048]{1,0:T(8,128)(2,1)}), bf16[704,2048]{1,0:T(8,128)(2,1)}) %all-gather.10.cloned.1.call-update) | async-done | bytes 2883600 | tf_op jit(solution)/shard_map/all_gather | solution.py:60
  266.1 48.4 %all-gather.12.cloned.1.call-done = bf16[1,1024,2048]{2,1,0:T(8,128)(2,1)} async-done(((bf16[1,128,2048]{2,1,0:T(8,128)(2,1)}), bf16[1,1024,2048]{2,1,0:T(8,128)(2,1)}) %all-gather.12.cloned.1.call-update) | async-done | bytes 4194320 | tf_op jit(solution)/shard_map/all_gather | solution.py:60
  314.4 10.1 %multiply_convert_fusion.2 = (bf16[1024,704]{1,0:T(8,128)(2,1)S(1)}, bf16[1024,704]{1,0:T(8,128)(2,1)S(1)}, bf16[1024,704]{1,0:T(8,128)(2,1)}) fusion(f32[1024,1408]{1,0:T(8,128)} %fusion.62, bf16[704,2048]{1,0:T(8,128)(2,1)} %all-gather.10.cloned.1.call-done, bf16[1,1024,2048]{2,1,0:T(8,128)(2,1)} %all-gather.12.cloned.1.call-done), kind=kOutput, calls=%fused_computation.30 | convolution fusion | flops 2963603456 | bytes 17170432 | tf_op jit(solution)/shard_map/dot_general | solution.py:39
  325.4 1.7 copy-done.43
  327.2 8.2 %convolution_convert_fusion.2 = bf16[1024,2048]{1,0:T(8,128)(2,1)} fusion(bf16[1024,1408]{1,0:T(8,128)(2,1)S(1)} %pad_maximum_fusion, bf16[2048,1408]{1,0:T(8,128)(2,1)S(1)} %copy-done.43), kind=kOutput, calls=%fused_computation.24 | convolution fusion | flops 5907677184 | bytes 12845056 | tf_op jit(solution)/shard_map/dot_general | solution.py:39
  335.4 8.7 %convolution_convert_fusion.1 = bf16[2048,1408]{1,0:T(8,128)(2,1)} fusion(bf16[1024,2048]{1,0:T(8,128)(2,1)S(1)} %bitcast.125, bf16[1024,1408]{1,0:T(8,128)(2,1)S(1)} %pad_maximum_fusion), kind=kOutput, calls=%fused_computation.7 | convolution fusion | flops 5908463616 | bytes 12845056 | tf_op jit(solution)/shard_map/dot_general | solution.py:35
  344.2 6.9 fusion.14
  351.1 58.1 %shard_map.214 = f32[128,2048]{1,0:T(8,128)} custom-call(bf16[8,128,2048]{2,1,0:T(8,128)(2,1)} %bitcast.123), custom_call_target="tpu_custom_call" | custom-call | bytes 144000000 | tf_op jit(solution)/shard_map/pallas_call | solution.py:487
  409.2 6.8 convolution_convert_fusion.3
  417.8 1.8 multiply_reduce_fusion.2
  420.6 44.7 %reduce-scatter.6.cloned.1.call-done = bf16[128,2048]{1,0:T(8,128)(2,1)} async-done(((bf16[1024,2048]{1,0:T(8,128)(2,1)}), bf16[128,2048]{1,0:T(8,128)(2,1)}) %reduce-scatter.6.cloned.1.call-update) | async-done | bytes 524304 | tf_op jit(solution)/shard_map/reduce_scatter | solution.py:64
  465.2 3.1 fusion.53
  468.3 35.1 %shard_map.215 = bf16[4,128,2048]{2,1,0:T(8,128)(2,1)} custom-call(bf16[128,2048]{1,0:T(8,128)(2,1)} %get-tuple-element.52.x_ref), custom_call_target="tpu_custom_call" | custom-call | bytes 66000000 | tf_op jit(solution)/shard_map/pallas_call | solution.py:147
  503.5 3.9 convolution_convert_fusion.7
  507.4 5.6 multiply_reduce_fusion
  513.5 2.5 multiply_convert_fusion
  516.1 1.4 fusion.61
  518.7 1.4 fusion.19
  520.7 4.7 convolution_convert_fusion
  525.4 3.3 copy.65
  528.8 1.5 copy-done.10
  530.3 3.7 convolution_convert_fusion.4
  534.6 9.6 %reduce-scatter.12.cloned.1.call-done = bf16[512,1408]{1,0:T(8,128)(2,1)} async-done(((bf16[2048,1408]{1,0:T(8,128)(2,1)}), bf16[512,1408]{1,0:T(8,128)(2,1)}) %reduce-scatter.12.cloned.1.call-update) | async-done | bytes 1441808 | tf_op jit(solution)/shard_map/reduce_scatter | solution.py:64
  544.2 4.9 all-to-all-start.1
  551.7 37.4 %reduce-scatter.14.cloned.1.call-done = bf16[176,2048]{1,0:T(8,128)(2,1)} async-done(((bf16[704,2048]{1,0:T(8,128)(2,1)}), bf16[176,2048]{1,0:T(8,128)(2,1)}) %reduce-scatter.14.cloned.1.call-update) | async-done | bytes 720912 | tf_op jit(solution)/shard_map/reduce_scatter | solution.py:64
  589.1 2.4 convert_element_type.236
  591.4 7.5 %convolution_convert_fusion.5 = bf16[512,2048]{1,0:T(8,128)(2,1)} fusion(bf16[2048,1536]{1,0:T(8,128)(2,1)} %get-tuple-element.31, bf16[512,512]{0,1:T(8,128)(2,1)S(1)} %bitcast.135, bf16[512,512]{0,1:T(8,128)(2,1)S(1)} %bitcast.148, bf16[512,512]{0,1:T(8,128)(2,1)S(1)} %bitcast.145), kind=kOutput, calls=%fused_computation.35 | convolution fusion | flops 3226992640 | bytes 9961472 | tf_op jit(solution)/shard_map/dot_general | solution.py:39
  598.9 22.2 %shard_map.216 = f32[128,2048]{1,0:T(8,128)} custom-call(bf16[4,128,2048]{2,1,0:T(8,128)(2,1)} %bitcast.149), custom_call_target="tpu_custom_call" | custom-call | bytes 66000000 | tf_op jit(solution)/shard_map/pallas_call | solution.py:217
  621.1 1.6 convert_reduce_fusion
  623.5 1.7 fusion.36
  626.9 12.4 %shard_map.217 = f32[8,128]{1,0:T(8,128)} custom-call(f32[32,8,128]{2,1,0:T(8,128)} %bitcast.153), custom_call_target="tpu_custom_call" | custom-call | bytes 30000000 | tf_op jit(solution)/shard_map/pallas_call | solution.py:295
  640.7 2.5 fusion.39
  643.2 20.0 %reduce-scatter.8.cloned.1.call-done = bf16[256,1536]{1,0:T(8,128)(2,1)} async-done(((bf16[2048,1536]{1,0:T(8,128)(2,1)}), bf16[256,1536]{1,0:T(8,128)(2,1)}) %reduce-scatter.8.cloned.1.call-update) | async-done | bytes 786448 | tf_op jit(solution)/shard_map/reduce_scatter | solution.py:64
  663.2 4.2 all-to-all-start
  668.0 32.2 %reduce-scatter.10.cloned.1.call-done = bf16[64,2048]{1,0:T(8,128)(2,1)} async-done(((bf16[512,2048]{1,0:T(8,128)(2,1)}), bf16[64,2048]{1,0:T(8,128)(2,1)}) %reduce-scatter.10.cloned.1.call-update) | async-done | bytes 262160 | tf_op jit(solution)/shard_map/reduce_scatter | solution.py:64
  700.2 1.8 convert_element_type.232
  702.0 7.5 %reshape.310 = f32[8,64,2,4,176]{4,3,2,1,0:T(4,128)} reshape(bf16[8,64,1408]{2,1,0:T(8,128)(2,1)S(1)} %all-to-all-done.1) | data formatting | bytes 4325376 | tf_op jit(solution)/shard_map/convert_element_type | solution.py:866
  709.5 4.6 copy.79
  714.1 1.8 fusion.55
  715.9 3.3 squeeze.18
  719.2 2.6 squeeze.17
  721.9 2.7 reshape.311
  724.6 2.2 copy.66
  726.8 3.2 reshape.309
  (204 shorter events, 41.0 us)
Async XLA Ops:
  7.2 10.1 %copy-start.20 = (bf16[64,5632]{1,0:T(8,128)(2,1)S(1)}, bf16[64,5632]{1,0:T(8,128)(2,1)}, u32[]{:S(2)}) copy-start(bf16[64,5632]{1,0:T(8,128)(2,1)} %param.21) | copy-start | bytes 2162692
  7.2 138.5 %all-gather.6.cloned.1.call-start = ((), (), s32[]{:S(2)}) async-start(), calls=%async_computation.7 | async-start | bytes 2359296 | tf_op jit(solution)/shard_map/all_gather | solution.py:60
  7.9 225.5 %all-gather.8.cloned.1.call-start = ((), (), s32[]{:S(2)}) async-start(), calls=%async_computation.8 | async-start | bytes 7208960 | tf_op jit(solution)/shard_map/all_gather | solution.py:60
  95.8 8.5 %copy-start.1 = (bf16[4,128,2048]{2,1,0:T(8,128)(2,1)S(1)}, bf16[4,128,2048]{2,1,0:T(8,128)(2,1)}, u32[]{:S(2)}) copy-start(bf16[4,128,2048]{2,1,0:T(8,128)(2,1)} %get-tuple-element.28) | copy-start | bytes 6291460
  97.0 30.0 %collective-permute-start.6 = (bf16[64,1408]{1,0:T(8,128)(2,1)}, bf16[64,1408]{1,0:T(8,128)(2,1)}, u32[]{:S(2)}, u32[]{:S(2)}) collective-permute-start(bf16[64,1408]{1,0:T(8,128)(2,1)} %get-tuple-element.63), channel_id=1, source_target_pairs={{0,7},{1,0},{2,1},{3,2},{4,3},{5,4},{6,5},{7,6},{8,15},{9,8},{10,9... | collective-permute-start | bytes 540680 | tf_op jit(solution)/shard_map/ppermute | solution.py:237
  99.4 28.7 %collective-permute-start.5 = (bf16[64,1408]{1,0:T(8,128)(2,1)}, bf16[64,1408]{1,0:T(8,128)(2,1)}, u32[]{:S(2)}, u32[]{:S(2)}) collective-permute-start(bf16[64,1408]{1,0:T(8,128)(2,1)} %get-tuple-element.64), channel_id=1, source_target_pairs={{0,6},{1,7},{2,0},{3,1},{4,2},{5,3},{6,4},{7,5},{8,14},{9,15},{10,... | collective-permute-start | bytes 540680 | tf_op jit(solution)/shard_map/ppermute | solution.py:237
  99.4 35.4 %collective-permute-start.4 = (bf16[64,1408]{1,0:T(8,128)(2,1)}, bf16[64,1408]{1,0:T(8,128)(2,1)}, u32[]{:S(2)}, u32[]{:S(2)}) collective-permute-start(bf16[64,1408]{1,0:T(8,128)(2,1)} %get-tuple-element.65), channel_id=1, source_target_pairs={{0,5},{1,6},{2,7},{3,0},{4,1},{5,2},{6,3},{7,4},{8,13},{9,14},{10,... | collective-permute-start | bytes 540680 | tf_op jit(solution)/shard_map/ppermute | solution.py:237
  99.4 35.4 %collective-permute-start.3 = (bf16[64,1408]{1,0:T(8,128)(2,1)}, bf16[64,1408]{1,0:T(8,128)(2,1)}, u32[]{:S(2)}, u32[]{:S(2)}) collective-permute-start(bf16[64,1408]{1,0:T(8,128)(2,1)} %get-tuple-element.66), channel_id=1, source_target_pairs={{0,4},{1,5},{2,6},{3,7},{4,0},{5,1},{6,2},{7,3},{8,12},{9,13},{10,... | collective-permute-start | bytes 540680 | tf_op jit(solution)/shard_map/ppermute | solution.py:237
  102.2 32.7 %collective-permute-start.2 = (bf16[64,1408]{1,0:T(8,128)(2,1)}, bf16[64,1408]{1,0:T(8,128)(2,1)}, u32[]{:S(2)}, u32[]{:S(2)}) collective-permute-start(bf16[64,1408]{1,0:T(8,128)(2,1)} %get-tuple-element.67), channel_id=1, source_target_pairs={{0,3},{1,4},{2,5},{3,6},{4,7},{5,0},{6,1},{7,2},{8,11},{9,12},{10,... | collective-permute-start | bytes 540680 | tf_op jit(solution)/shard_map/ppermute | solution.py:237
  107.1 7.2 copy-start.30
  108.0 6.3 copy-start.8
  114.4 1.6 copy-start.7
  117.5 2.2 copy-start.18
  119.2 3.0 copy-start.22
  119.2 3.0 copy-start.24
  122.2 3.3 copy-start
  122.2 6.9 copy-start.34
  122.2 4.8 copy-start.29
  122.2 5.8 copy-start.28
  125.5 9.4 %copy-start.35 = (f32[8,512]{1,0:T(8,128)}, f32[8,512]{1,0:T(8,128)S(1)}, u32[]{:S(2)}) copy-start(f32[8,512]{1,0:T(8,128)S(1)} %fusion) | copy-start | bytes 49156
  127.0 7.8 %copy-start.12 = (bf16[512,512]{0,1:T(8,128)(2,1)}, bf16[512,512]{0,1:T(8,128)(2,1)S(1)}, u32[]{:S(2)}) copy-start(bf16[512,512]{0,1:T(8,128)(2,1)S(1)} %copy.56) | copy-start | bytes 1572868
  127.0 9.4 %collective-permute-start.1 = (bf16[64,1408]{1,0:T(8,128)(2,1)S(1)}, bf16[64,1408]{1,0:T(8,128)(2,1)S(1)}, u32[]{:S(2)}, u32[]{:S(2)}) collective-permute-start(bf16[64,1408]{1,0:T(8,128)(2,1)S(1)} %copy-done.29), channel_id=1, source_target_pairs={{0,2},{1,3},{2,4},{3,5},{4,6},{5,7},{6,0},{7,1},{8,10},{9,11},{10,... | collective-permute-start | bytes 540680 | tf_op jit(solution)/shard_map/ppermute | solution.py:237
  128.0 9.8 %collective-permute-start = (bf16[64,1408]{1,0:T(8,128)(2,1)S(1)}, bf16[64,1408]{1,0:T(8,128)(2,1)S(1)}, u32[]{:S(2)}, u32[]{:S(2)}) collective-permute-start(bf16[64,1408]{1,0:T(8,128)(2,1)S(1)} %copy-done.28), channel_id=1, source_target_pairs={{0,1},{1,2},{2,3},{3,4},{4,5},{5,6},{6,7},{7,0},{8,9},{9,10},{10,1... | collective-permute-start | bytes 540680 | tf_op jit(solution)/shard_map/ppermute | solution.py:237
  129.1 8.8 %copy-start.21 = (bf16[64,1408]{1,0:T(8,128)(2,1)S(1)}, bf16[64,1408]{1,0:T(8,128)(2,1)}, u32[]{:S(2)}) copy-start(bf16[64,1408]{1,0:T(8,128)(2,1)} %get-tuple-element.33) | copy-start | bytes 540676
  137.9 7.4 %copy-start.36 = (f32[32,64]{1,0:T(8,128)S(1)}, f32[32,64]{1,0:T(8,128)}, u32[]{:S(2)}) copy-start(f32[32,64]{1,0:T(8,128)} %get-tuple-element.79) | copy-start | bytes 24580
  137.9 7.5 %copy-start.2 = (bf16[1,128,2048]{2,1,0:T(8,128)(2,1)S(1)}, bf16[1,128,2048]{2,1,0:T(8,128)(2,1)}, u32[]{:S(2)}) copy-start(bf16[1,128,2048]{2,1,0:T(8,128)(2,1)} %param.12) | copy-start | bytes 1572868
  142.8 1.1 copy-start.5
  143.9 122.1 %all-gather.10.cloned.1.call-start = ((), (), s32[]{:S(2)}) async-start(), calls=%async_computation.9 | async-start | bytes 3604480 | tf_op jit(solution)/shard_map/all_gather | solution.py:60
  144.7 169.7 %all-gather.12.cloned.1.call-start = ((), (), s32[]{:S(2)}) async-start(), calls=%async_computation.15 | async-start | bytes 4718592 | tf_op jit(solution)/shard_map/all_gather | solution.py:60
  145.3 320.0 %reduce-scatter.6.cloned.1.call-start = ((), (), s32[]{:S(2)}) async-start(), calls=%async_computation.10 | async-start | bytes 4718592 | tf_op jit(solution)/shard_map/reduce_scatter | solution.py:64
  145.4 43.4 %copy-start.32 = (f32[2048]{0:T(1024)}, f32[2048]{0:T(1024)S(1)}, u32[]{:S(2)}) copy-start(f32[2048]{0:T(1024)S(1)} %mul.329) | copy-start | bytes 24580
  145.6 40.8 %copy-start.42 = (f32[128]{0:T(128)}, f32[128]{0:T(128)S(1)}, u32[]{:S(2)}) copy-start(f32[128]{0:T(128)S(1)} %broadcast_multiply_fusion.4) | copy-start | bytes 1540
  188.5 44.8 %copy-start.40 = (f32[128]{0:T(128)}, f32[128]{0:T(128)S(1)}, u32[]{:S(2)}) copy-start(f32[128]{0:T(128)S(1)} %broadcast_multiply_fusion.7) | copy-start | bytes 1540
  188.8 44.6 %copy-start.41 = (f32[128]{0:T(128)}, f32[128]{0:T(128)S(1)}, u32[]{:S(2)}) copy-start(f32[128]{0:T(128)S(1)} %add_rsqrt_fusion.1) | copy-start | bytes 1540
  324.5 2.6 copy-start.43
  327.2 8.2 %copy-start.6 = (bf16[8,128,2048]{2,1,0:T(8,128)(2,1)S(1)}, bf16[8,128,2048]{2,1,0:T(8,128)(2,1)}, u32[]{:S(2)}) copy-start(bf16[8,128,2048]{2,1,0:T(8,128)(2,1)} %shard_map.213) | copy-start | bytes 12582916
  335.4 8.7 %copy-start.44 = (bf16[1024,704]{1,0:T(8,128)(2,1)S(1)}, bf16[1024,704]{1,0:T(8,128)(2,1)}, u32[]{:S(2)}) copy-start(bf16[1024,704]{1,0:T(8,128)(2,1)} %get-tuple-element.58) | copy-start | bytes 4325380
  416.1 1.7 copy-start.3
  416.1 128.2 %reduce-scatter.12.cloned.1.call-start = ((), (), s32[]{:S(2)}) async-start(), calls=%async_computation.13 | async-start | bytes 7208960 | tf_op jit(solution)/shard_map/reduce_scatter | solution.py:64
  416.6 48.6 %copy-start.11 = (bf16[1,128,2048]{2,1,0:T(8,128)(2,1)S(1)}, bf16[1,128,2048]{2,1,0:T(8,128)(2,1)}, u32[]{:S(2)}) copy-start(bf16[1,128,2048]{2,1,0:T(8,128)(2,1)} %param.23) | copy-start | bytes 1572868
  416.7 172.4 %reduce-scatter.14.cloned.1.call-start = ((), (), s32[]{:S(2)}) async-start(), calls=%async_computation.14 | async-start | bytes 3604480 | tf_op jit(solution)/shard_map/reduce_scatter | solution.py:64
  417.5 245.7 %reduce-scatter.8.cloned.1.call-start = ((), (), s32[]{:S(2)}) async-start(), calls=%async_computation.11 | async-start | bytes 7077888 | tf_op jit(solution)/shard_map/reduce_scatter | solution.py:64
  503.4 4.0 copy-start.13
  507.4 5.6 slice-start
  507.4 6.1 slice-start.1
  513.5 2.6 copy-start.19
  513.5 2.6 copy-start.25
  516.1 1.4 copy-start.23
  517.5 0.9 copy-start.27
  517.5 0.9 copy-start.33
  518.7 1.5 copy-start.14
  518.7 1.5 copy-start.16
  518.7 2.0 copy-start.9
  528.7 1.6 copy-start.10
  528.8 171.4 %reduce-scatter.10.cloned.1.call-start = ((), (), s32[]{:S(2)}) async-start(), calls=%async_computation.12 | async-start | bytes 2359296 | tf_op jit(solution)/shard_map/reduce_scatter | solution.py:64
  534.0 16.3 %copy-start.38 = (f32[2048]{0:T(1024)S(1)}, f32[2048]{0:T(1024)}, u32[]{:S(2)}) copy-start(f32[2048]{0:T(1024)} %get-tuple-element.44) | copy-start | bytes 24580
  534.0 17.0 %copy-start.37 = (f32[2048]{0:T(1024)S(1)}, f32[2048]{0:T(1024)}, u32[]{:S(2)}) copy-start(f32[2048]{0:T(1024)} %get-tuple-element.50) | copy-start | bytes 24580
  534.0 57.4 %copy-start.15 = (bf16[512,8,64]{0,2,1:T(8,128)(2,1)S(1)}, bf16[512,8,64]{0,2,1:T(8,128)(2,1)}, u32[]{:S(2)}) copy-start(bf16[512,8,64]{0,2,1:T(8,128)(2,1)} %copy-done.14) | copy-start | bytes 1572868
  534.0 57.4 %copy-start.17 = (bf16[512,8,64]{0,2,1:T(8,128)(2,1)S(1)}, bf16[512,8,64]{0,2,1:T(8,128)(2,1)}, u32[]{:S(2)}) copy-start(bf16[512,8,64]{0,2,1:T(8,128)(2,1)} %copy-done.16) | copy-start | bytes 1572868
  544.2 99.0 %all-to-all-start.1 = ((bf16[8,64,1408]{2,1,0:T(8,128)(2,1)}), bf16[8,64,1408]{2,1,0:T(8,128)(2,1)S(1)}, u32[]{:S(2)}, u32[]{:S(2)}) async-start(bf16[8,64,1408]{2,1,0:T(8,128)(2,1)} %bitcast.151), calls=%async_computation.5 | async-start | bytes 2883584 | tf_op jit(solution)/shard_map/all_to_all | solution.py:68
  598.9 24.6 %copy-start.31 = (f32[2048]{0:T(1024)S(1)}, f32[2048]{0:T(1024)}, u32[]{:S(2)}) copy-start(f32[2048]{0:T(1024)} %copy-done.30) | copy-start | bytes 24580
  621.1 19.6 %copy-start.4 = (f32[128,2048]{1,0:T(8,128)S(1)}, f32[128,2048]{1,0:T(8,128)}, u32[]{:S(2)}) copy-start(f32[128,2048]{1,0:T(8,128)} %shard_map.216) | copy-start | bytes 3145732
  639.4 28.1 %copy-start.39 = (f32[8,128]{1,0:T(8,128)S(1)}, f32[8,128]{1,0:T(8,128)}, u32[]{:S(2)}) copy-start(f32[8,128]{1,0:T(8,128)} %shard_map.217) | copy-start | bytes 12292
  663.2 58.6 %all-to-all-start = ((bf16[4,64,1536]{2,1,0:T(8,128)(2,1)}), bf16[4,64,1536]{2,1,0:T(8,128)(2,1)}, u32[]{:S(2)}, u32[]{:S(2)}) async-start(bf16[4,64,1536]{2,1,0:T(8,128)(2,1)} %bitcast.152), calls=%async_computation.2 | async-start | bytes 1572864 | tf_op jit(solution)/shard_map/all_to_all | solution.py:68
  (1 other events, 0.6 us)
Sparse Core Ops, SparseCore 0:
  9.6 36.7 all-gather.5
  144.1 78.3 all-gather.7
  224.4 41.6 all-gather.9
  267.5 46.8 all-gather.11
  416.2 49.0 reduce-scatter.5
  468.1 76.1 reduce-scatter.11
  547.3 41.7 reduce-scatter.13
  591.4 71.8 reduce-scatter.7
  665.5 34.6 reduce-scatter.9

commit v4 on v1

--- a/solution.py
+++ b/solution.py
@@ -1,7 +1,12 @@
+import functools
+
 import jax
 import jax.numpy as jnp
 from jax import lax
+from jax.experimental import pallas as pl
+from jax.experimental.pallas import tpu as pltpu
 from jax.sharding import PartitionSpec as P
+
 
 HEAD_DIM = 64
 ROT = 16
@@ -61,6 +66,914 @@
 
 def swap(value, axis, split, concat):
     return lax.all_to_all(value, axis, split_axis=split, concat_axis=concat, tiled=True)
+
+
+MESH = pl.DeviceIdType.MESH
+
+
+def lasting(micros):
+    return pl.CostEstimate(flops=0, transcendentals=0, bytes_accessed=int(micros * 3.0e6))
+
+
+def meet(peers):
+    barrier = pltpu.get_barrier_semaphore()
+    for peer in peers:
+        pl.semaphore_signal(barrier, inc=1, device_id=peer, device_id_type=MESH)
+    pl.semaphore_wait(barrier, len(peers))
+
+
+def push(source, target, send, recv, at, peer):
+    copy = pltpu.make_async_remote_copy(
+        src_ref=source,
+        dst_ref=target,
+        send_sem=send.at[at],
+        recv_sem=recv.at[at],
+        device_id=peer,
+        device_id_type=MESH,
+    )
+    copy.start()
+    return copy
+
+
+def corners():
+    me = lax.axis_index("seq")
+    high, low = me // 2, lax.rem(me, 2)
+    across = high * 2 + (1 - low)
+    along = (1 - high) * 2 + low
+    return me, across, along, 3 - me
+
+
+def move_blocks(value, axis, count):
+    rows = value.shape[0] // count
+    me = lax.axis_index(axis)
+    blocks = []
+    for step in range(count):
+        at = lax.rem(me + step, count) * rows
+        block = lax.dynamic_slice_in_dim(value, at, rows, 0)
+        if step:
+            block = lax.ppermute(block, axis, [(i, (i + step) % count) for i in range(count)])
+        blocks.append(block)
+    return blocks
+
+
+def place_blocks(blocks, axis):
+    count, rows = len(blocks), blocks[0].shape[0]
+    me = lax.axis_index(axis)
+    out = jnp.zeros((count * rows,) + blocks[0].shape[1:], blocks[0].dtype)
+    for step, block in enumerate(blocks):
+        at = lax.rem(me - step + count, count) * rows
+        out = lax.dynamic_update_slice_in_dim(out, block, at, 0)
+    return out
+
+
+def remote(source, target, send, recv, peer):
+    return pltpu.make_async_remote_copy(
+        src_ref=source,
+        dst_ref=target,
+        send_sem=send,
+        recv_sem=recv,
+        device_id=peer,
+        device_id_type=MESH,
+    )
+
+
+def line_place(dps):
+    dp = lax.axis_index("dp")
+    chip, core = dp // 2, lax.rem(dp, 2)
+    chips = dps // 2
+    ends = (chip + 1 < chips, chip >= 1)
+    sides = ({"dp": lax.rem(dp + 2, dps)}, {"dp": lax.rem(dp - 2 + dps, dps)})
+    return chips, chip, core, ends, sides, {"dp": 2 * chip + (1 - core)}
+
+
+class Plane:
+
+    def __init__(self, count, x_ref, pair, got, send, recv):
+        self.count, self.x, self.pair, self.got = count, x_ref, pair, got
+        self.send, self.recv = send, recv
+        self.square = count == 4
+
+    def begin(self):
+        x, got, send, recv = self.x, self.got, self.send, self.recv
+        if not self.square:
+            me = lax.axis_index("seq")
+            targets = [lax.rem(me + step, self.count) for step in range(1, self.count)]
+            self.copies = [
+                push(x.at[target], got.at[at], send, recv, at, {"seq": target})
+                for at, target in enumerate(targets)
+            ]
+            return
+        _, across, along, far = corners()
+        half = x.shape[1] // 2
+        top, low = pl.ds(0, half), pl.ds(half, half)
+        to_across, to_along = {"seq": across}, {"seq": along}
+        self.copies = [
+            push(x.at[far, top], self.pair.at[0], send, recv, 0, to_across),
+            push(x.at[far, low], self.pair.at[1], send, recv, 1, to_along),
+            push(x.at[across, top], got.at[0, top], send, recv, 2, to_across),
+            push(x.at[along, low], got.at[1, low], send, recv, 3, to_along),
+        ]
+
+    def relay(self):
+        if not self.square:
+            return
+        x, pair, got, send, recv = self.x, self.pair, self.got, self.send, self.recv
+        _, across, along, _ = corners()
+        half = x.shape[1] // 2
+        top, low = pl.ds(0, half), pl.ds(half, half)
+        self.copies[0].wait_recv()
+        pair[2] = (pair[0].astype(F32) + x[along, top].astype(F32)).astype(pair.dtype)
+        self.copies.append(push(pair.at[2], got.at[1, top], send, recv, 4, {"seq": along}))
+        self.copies[1].wait_recv()
+        pair[3] = (pair[1].astype(F32) + x[across, low].astype(F32)).astype(pair.dtype)
+        self.copies.append(push(pair.at[3], got.at[0, low], send, recv, 5, {"seq": across}))
+
+    def end(self):
+        for at, copy in enumerate(self.copies):
+            copy.wait_send()
+            if not self.square or at > 1:
+                copy.wait_recv()
+
+    def total(self, rows):
+        value = self.x[lax.axis_index("seq"), rows].astype(F32)
+        for at in range(2 if self.square else self.count - 1):
+            value = value + self.got[at, rows].astype(F32)
+        return value
+
+    @staticmethod
+    def scratch(count, rows, wide, dtype):
+        slots = 6 if count == 4 else count - 1
+        return [
+            pltpu.VMEM((4, rows // 2, wide), dtype),
+            pltpu.VMEM((2 if count == 4 else count - 1, rows, wide), dtype),
+            pltpu.SemaphoreType.DMA((slots,)),
+            pltpu.SemaphoreType.DMA((slots,)),
+        ]
+
+
+class LineSum:
+
+    def __init__(self, dps, block, pair, moving, line_s, line_r, pair_s, pair_r):
+        self.block, self.pair, self.moving = block, pair, moving
+        self.sems = (line_s, line_r, pair_s, pair_r)
+        self.chips, self.chip, self.core, self.ends, self.sides, self.sibling = line_place(dps)
+
+    def share(self, owner, owner_core):
+        return remote(
+            self.block(2 * owner + owner_core),
+            self.pair.at[owner],
+            self.sems[2].at[owner],
+            self.sems[3].at[owner],
+            self.sibling,
+        )
+
+    def onward(self, side, owner):
+        at = (side, owner)
+        return remote(
+            self.pair.at[owner],
+            self.moving.at[at],
+            self.sems[0].at[at],
+            self.sems[1].at[at],
+            self.sides[side],
+        )
+
+    def begin(self):
+        order = [
+            at for both in zip(range(self.chips - 1, -1, -1), range(self.chips)) for at in both
+        ]
+        for owner in dict.fromkeys(order):
+            self.share(owner, 1 - self.core).start()
+
+    def add(self, owner, side):
+        own = self.block(2 * owner + self.core)
+
+        def one(at):
+            value = self.pair[(owner,) + at].astype(F32) + own[at].astype(F32)
+            if side is not None:
+                value = value + self.moving[(side, owner) + at].astype(F32)
+            self.pair[(owner,) + at] = value.astype(self.pair.dtype)
+
+        if len(own.shape) > 2:
+            for at in range(own.shape[0]):
+                one((at,))
+        else:
+            by_chunks(own.shape[0], lambda here: one((here,)))
+
+    def step(self, at):
+        for side in range(2):
+            owner = self.chips - 1 - at if side == 0 else at
+            passing = self.chip < owner if side == 0 else self.chip > owner
+            fed = jnp.logical_and(passing, self.ends[1 - side])
+
+            @pl.when(passing)
+            def _(owner=owner):
+                self.share(owner, self.core).wait_recv()
+
+            @pl.when(fed)
+            def _(side=side, owner=owner):
+                self.onward(side, owner).wait_recv()
+                self.add(owner, side)
+
+            @pl.when(jnp.logical_and(passing, jnp.logical_not(fed)))
+            def _(owner=owner):
+                self.add(owner, None)
+
+            @pl.when(passing)
+            def _(side=side, owner=owner):
+                self.onward(side, owner).start()
+
+    def end(self):
+        for owner in range(self.chips):
+
+            @pl.when(self.chip == owner)
+            def _(owner=owner):
+                self.share(owner, self.core).wait_recv()
+
+            for side in range(2):
+
+                @pl.when(jnp.logical_and(self.chip == owner, self.ends[1 - side]))
+                def _(side=side, owner=owner):
+                    self.onward(side, owner).wait_recv()
+
+                @pl.when(jnp.logical_and(self.chip == owner, jnp.logical_not(self.ends[1 - side])))
+                def _(side=side, owner=owner):
+                    self.moving[side, owner] = jnp.zeros(self.moving.shape[2:], self.moving.dtype)
+
+    def total(self, at):
+        own = self.block(2 * self.chip + self.core)
+        value = own[at].astype(F32) + self.pair[(self.chip,) + at].astype(F32)
+        for side in range(2):
+            value = value + self.moving[(side, self.chip) + at].astype(F32)
+        return value
+
+    def drain(self):
+        for owner in range(self.chips):
+            for side in range(2):
+                passing = self.chip < owner if side == 0 else self.chip > owner
+
+                @pl.when(passing)
+                def _(side=side, owner=owner):
+                    self.onward(side, owner).wait_send()
+
+            self.share(owner, 1 - self.core).wait_send()
+
+    @staticmethod
+    def scratch(dps, shape, dtype):
+        dma, chips = pltpu.SemaphoreType.DMA, dps // 2
+        return [
+            pltpu.VMEM((chips,) + shape, dtype),
+            pltpu.VMEM((2, chips) + shape, dtype),
+            dma((2, chips)),
+            dma((2, chips)),
+            dma((chips,)),
+            dma((chips,)),
+        ]
+
+
+class PlaneGather:
+
+    def __init__(self, count, x_ref, o_ref, send, recv, local):
+        self.count, self.x, self.o = count, x_ref, o_ref
+        self.send, self.recv, self.local = send, recv, local
+        self.square = count == 4
+
+    def begin(self):
+        x, o, send, recv = self.x, self.o, self.send, self.recv
+        me = lax.axis_index("seq")
+        if self.square:
+            _, across, along, _ = corners()
+            half = x.shape[0] // 2
+            top, low = pl.ds(0, half), pl.ds(half, half)
+            to_across, to_along = {"seq": across}, {"seq": along}
+            self.copies = [
+                push(x.at[top], o.at[me, top], send, recv, 0, to_across),
+                push(x.at[low], o.at[me, low], send, recv, 1, to_along),
+                push(x.at[low], o.at[me, low], send, recv, 2, to_across),
+                push(x.at[top], o.at[me, top], send, recv, 3, to_along),
+            ]
+        else:
+            self.copies = [
+                push(x, o.at[me], send, recv, step - 1, {"seq": lax.rem(me + step, self.count)})
+                for step in range(1, self.count)
+            ]
+        self.own = pltpu.make_async_copy(x, o.at[me], self.local)
+        self.own.start()
+
+    def relay(self):
+        if not self.square:
+            return
+        o, send, recv = self.o, self.send, self.recv
+        _, across, along, _ = corners()
+        half = self.x.shape[0] // 2
+        top, low = pl.ds(0, half), pl.ds(half, half)
+        self.copies[0].wait_recv()
+        self.copies.append(
+            push(o.at[across, top], o.at[across, top], send, recv, 4, {"seq": along})
+        )
+        self.copies[1].wait_recv()
+        self.copies.append(
+            push(o.at[along, low], o.at[along, low], send, recv, 5, {"seq": across})
+        )
+
+    def end(self):
+        for at, copy in enumerate(self.copies):
+            copy.wait_send()
+            if not self.square or at > 1:
+                copy.wait_recv()
+        self.own.wait()
+
+    @staticmethod
+    def scratch(count):
+        slots = 6 if count == 4 else count - 1
+        dma = pltpu.SemaphoreType.DMA
+        return [dma((slots,)), dma((slots,)), dma]
+
+
+class LineGather:
+
+    def __init__(self, dps, x_ref, o_ref, line_s, line_r, pair_s, pair_r, local):
+        self.x, self.o, self.local = x_ref, o_ref, local
+        self.sems = (line_s, line_r, pair_s, pair_r)
+        self.chips, self.chip, self.core, self.ends, self.sides, self.sibling = line_place(dps)
+
+    def onward(self, side, hop, owner, source=None):
+        block = self.o.at[2 * owner + self.core]
+        at = (side, hop)
+        return remote(
+            block if source is None else source,
+            block,
+            self.sems[0].at[at],
+            self.sems[1].at[at],
+            self.sides[side],
+        )
+
+    def share(self, owner, owner_core, source=None):
+        block = self.o.at[2 * owner + owner_core]
+        return remote(
+            block if source is None else source,
+            block,
+            self.sems[2].at[owner],
+            self.sems[3].at[owner],
+            self.sibling,
+        )
+
+    def begin(self):
+        for side in range(2):
+
+            @pl.when(self.ends[side])
+            def _(side=side):
+                self.onward(side, 0, self.chip, self.x).start()
+
+        self.share(self.chip, self.core, self.x).start()
+        self.own = pltpu.make_async_copy(
+            self.x, self.o.at[2 * self.chip + self.core], self.local
+        )
+        self.own.start()
+
+    def hop(self, hop):
+        for side in range(2):
+            origin = self.chip - 1 - hop if side == 0 else self.chip + 1 + hop
+            there = origin >= 0 if side == 0 else origin < self.chips
+
+            @pl.when(there)
+            def _(side=side, origin=origin):
+                self.onward(side, hop, origin).wait_recv()
+
+            if hop < self.chips - 2:
+
+                @pl.when(jnp.logical_and(there, self.ends[side]))
+                def _(side=side, origin=origin):
+                    self.onward(side, hop + 1, origin).start()
+
+            @pl.when(there)
+            def _(origin=origin):
+                self.share(origin, self.core).start()
+
+    def end(self):
+        self.own.wait()
+        for hop in range(self.chips - 1):
+            for side in range(2):
+                origin = self.chip - hop if side == 0 else self.chip + hop
+                there = origin >= 0 if side == 0 else origin < self.chips
+
+                @pl.when(jnp.logical_and(there, self.ends[side]))
+                def _(side=side, hop=hop, origin=origin):
+                    self.onward(side, hop, origin).wait_send()
+
+        for owner in range(self.chips):
+            self.share(owner, self.core).wait_send()
+            self.share(owner, 1 - self.core).wait_recv()
+
+    @staticmethod
+    def scratch(dps):
+        dma, chips = pltpu.SemaphoreType.DMA, dps // 2
+        return [dma((2, chips - 1)), dma((2, chips - 1)), dma((chips,)), dma((chips,)), dma]
+
+
+CHUNK = 16
+
+
+def by_chunks(rows, body):
+    @pl.loop(0, rows // CHUNK)
+    def _(at):
+        body(pl.ds(pl.multiple_of(at * CHUNK, CHUNK), CHUNK))
+
+
+def meet_cross(ways):
+    seqs, dps = ways
+    seq, dp = lax.axis_index("seq"), lax.axis_index("dp")
+    seq_peers = [lax.rem(seq + step, seqs) for step in range(1, seqs)]
+    dp_peers = [lax.rem(dp + step, dps) for step in range(1, dps)]
+    meet([{"seq": peer} for peer in seq_peers] + [{"dp": peer} for peer in dp_peers])
+    return seq_peers, dp_peers
+
+
+def middle(ways, part_ref, x_ref, gain_ref, shift_ref, grad_ref, cut_ref, *rest):
+    seqs, dps = ways
+    resid_ref, all_ref, grads_ref, gate_ref = rest[:4]
+    plane = Plane(seqs, part_ref, *rest[4:8])
+    own = rest[8]
+    moved = LineGather(dps, own, all_ref, *rest[9:14])
+    grads = LineGather(dps, grad_ref, grads_ref, *rest[14:19])
+    gates = PlaneGather(seqs, cut_ref, gate_ref, *rest[19:22])
+    hops = dps // 2 - 1
+    meet_cross(ways)
+    plane.begin()
+    grads.begin()
+    plane.relay()
+    plane.end()
+    gates.begin()
+    gain, shift = gain_ref[...], shift_ref[...]
+
+    def one(here):
+        resid = x_ref[here, :].astype(F32) + plane.total(here)
+        resid_ref[here, :] = resid
+        normed, _ = normalize(resid)
+        own[here, :] = (normed * gain + shift).astype(own.dtype)
+
+    by_chunks(x_ref.shape[0], one)
+    moved.begin()
+    for hop in range(hops):
+        grads.hop(hop)
+        if hop == hops - 1:
+            gates.relay()
+        moved.hop(hop)
+    grads.end()
+    moved.end()
+    gates.end()
+
+
+def middle_all(ways, part, inputs, gain, shift, grad_out, cut, tag):
+    seqs, dps = ways
+    rows, wide = inputs.shape
+    vmem, anywhere = (pl.BlockSpec(memory_space=space) for space in (pltpu.VMEM, pl.ANY))
+    resid, moved, grads, gate = pl.pallas_call(
+        functools.partial(middle, ways),
+        out_shape=(
+            jax.ShapeDtypeStruct((rows, wide), F32),
+            jax.ShapeDtypeStruct((dps, rows, wide), BF16),
+            jax.ShapeDtypeStruct((dps, rows, wide), BF16),
+            jax.ShapeDtypeStruct((seqs,) + cut.shape, BF16),
+        ),
+        in_specs=[vmem] * 6,
+        out_specs=(vmem, anywhere, anywhere, anywhere),
+        scratch_shapes=Plane.scratch(seqs, rows, wide, BF16)
+        + [pltpu.VMEM((rows, wide), BF16)]
+        + LineGather.scratch(dps)
+        + LineGather.scratch(dps)
+        + PlaneGather.scratch(seqs),
+        cost_estimate=lasting(75),
+        compiler_params=pltpu.CompilerParams(collective_id=tag, has_side_effects=True),
+    )(part.reshape(seqs, rows, wide), inputs, gain, shift, grad_out, cut)
+    moved, grads = (item.reshape(dps * rows, wide) for item in (moved, grads))
+    return resid, moved, grads, gate.reshape(seqs * cut.shape[0], cut.shape[1])
+
+
+def turning(ways, part_ref, resid_ref, gain_ref, grad_ref, out_ref, both_ref, *rest):
+    seqs, dps = ways
+    total_ref, all_ref, sums_ref, layer_ref, rows_ref = rest[:5]
+    line = LineSum(dps, lambda owner: part_ref.at[owner], *rest[5:11])
+    own = rest[11]
+    gathered = PlaneGather(seqs, own, all_ref, *rest[12:15])
+    outs = LineSum(dps, lambda owner: out_ref.at[owner], *rest[15:21])
+    both = Plane(seqs, both_ref, *rest[21:25])
+    chips = dps // 2
+    meet_cross(ways)
+    line.begin()
+    both.begin()
+    line.step(0)
+    both.relay()
+    outs.begin()
+    for at in range(1, chips):
+        line.step(at)
+    outs.step(0)
+    line.end()
+    sums_ref[...] = jnp.zeros(sums_ref.shape, F32)
+    gain = gain_ref[...]
+
+    def one(here):
+        grad = line.total((here,))
+        normed, inverse = normalize(resid_ref[here, :])
+        sums_ref[2:3, :] += jnp.sum(grad * normed, axis=0, keepdims=True)
+        sums_ref[3:4, :] += jnp.sum(grad, axis=0, keepdims=True)
+        total = grad_ref[here, :].astype(F32) + norm_back(grad, normed, inverse, gain)
+        total_ref[here, :] = total
+        own[here, :] = total.astype(own.dtype)
+
+    by_chunks(resid_ref.shape[0], one)
+    gathered.begin()
+    if chips > 1:
+        outs.step(1)
+    gathered.relay()
+    for at in range(2, chips):
+        outs.step(at)
+    both.end()
+
+    def two(here):
+        rows_ref[here, :] = both.total(here).astype(rows_ref.dtype)
+
+    by_chunks(rows_ref.shape[0], two)
+    gathered.end()
+    outs.end()
+
+    def three(here):
+        layer_ref[here, :] = (resid_ref[here, :] + outs.total((here,))).astype(layer_ref.dtype)
+
+    by_chunks(resid_ref.shape[0], three)
+    line.drain()
+    outs.drain()
+
+
+def turn_all(ways, part, resid, gain, grad_out, out_part, both, tag):
+    seqs, dps = ways
+    rows, wide = resid.shape
+    cut = (both.shape[0] // seqs, both.shape[1])
+    vmem, anywhere = (pl.BlockSpec(memory_space=space) for space in (pltpu.VMEM, pl.ANY))
+    total, gathered, sums, layer, both = pl.pallas_call(
+        functools.partial(turning, ways),
+        out_shape=(
+            jax.ShapeDtypeStruct((rows, wide), F32),
+            jax.ShapeDtypeStruct((seqs, rows, wide), BF16),
+            jax.ShapeDtypeStruct((8, wide), F32),
+            jax.ShapeDtypeStruct((rows, wide), BF16),
+            jax.ShapeDtypeStruct(cut, BF16),
+        ),
+        in_specs=[vmem] * 6,
+        out_specs=(vmem, anywhere, vmem, vmem, vmem),
+        scratch_shapes=LineSum.scratch(dps, (rows, wide), BF16)
+        + [pltpu.VMEM((rows, wide), BF16)]
+        + PlaneGather.scratch(seqs)
+        + LineSum.scratch(dps, (rows, wide), BF16)
+        + Plane.scratch(seqs, cut[0], cut[1], BF16),
+        cost_estimate=lasting(85),
+        compiler_params=pltpu.CompilerParams(
+            collective_id=tag, has_side_effects=True, vmem_limit_bytes=60 * 2**20
+        ),
+    )(
+        part.reshape(dps, rows, wide),
+        resid,
+        gain,
+        grad_out,
+        out_part.reshape(dps, rows, wide),
+        both.reshape((seqs,) + cut),
+    )
+    return total, gathered.reshape(seqs * rows, wide), sums, layer, both
+
+
+def closing(ways, w_ref, g_ref, sums_ref, x_ref, gain_ref, resid_ref, both_ref, *rest):
+    seqs, dps = ways
+    qkv_ref, grad_ref, tiny_ref, gate_ref, up_ref = rest[:5]
+    plane = Plane(seqs, g_ref, *rest[5:9])
+    line = LineSum(dps, lambda owner: w_ref.at[:, owner], *rest[9:15])
+    landed, mine, near, far, part_sum = rest[15:20]
+    swap_s, swap_r, near_s, near_r, far_s, far_r = rest[20:]
+    seq, dp = lax.axis_index("seq"), lax.axis_index("dp")
+    seq_peers, dp_peers = meet_cross(ways)
+    line.begin()
+    plane.begin()
+    plane.relay()
+    line.step(0)
+    plane.end()
+    part_sum[...] = sums_ref[...]
+    gain = gain_ref[...]
+
+    def one(here):
+        grad = plane.total(here)
+        normed, inverse = normalize(x_ref[here, :].astype(F32))
+        part_sum[0:1, :] += jnp.sum(grad * normed, axis=0, keepdims=True)
+        part_sum[1:2, :] += jnp.sum(grad, axis=0, keepdims=True)
+        grad_ref[here, :] = (
+            resid_ref[here, :] + norm_back(grad, normed, inverse, gain)
+        ).astype(grad_ref.dtype)
+
+    by_chunks(x_ref.shape[0], one)
+    wide = x_ref.shape[1]
+    nears = [
+        push(part_sum, near.at[seq], near_s, near_r, at, {"seq": peer})
+        for at, peer in enumerate(seq_peers)
+    ]
+    near[seq] = part_sum[...]
+    line.step(1)
+    for copy in nears:
+        copy.wait()
+    far[dp] = jnp.sum(near[...], axis=0)
+    units = gate_ref.shape[1] // (seqs * dps)
+    for at, weight in enumerate((gate_ref, up_ref)):
+        for source in range(seqs):
+            for owner in range(dps):
+                weight[:, pl.ds((source * dps + owner) * units, units)] = both_ref[
+                    owner, :, pl.ds((at * seqs + source) * units, units)
+                ].astype(F32)
+    fars = [
+        push(far.at[dp], far.at[dp], far_s, far_r, at, {"dp": peer})
+        for at, peer in enumerate(dp_peers)
+    ]
+    for at in range(2, dps // 2):
+        line.step(at)
+    line.end()
+    for source in range(seqs):
+        mine[source] = line.total((source,)).astype(mine.dtype)
+    swaps = [
+        push(mine.at[peer], landed.at[seq], swap_s, swap_r, at, {"seq": peer})
+        for at, peer in enumerate(seq_peers)
+    ]
+    landed[seq] = mine[seq]
+    for copy in fars:
+        copy.wait()
+    tiny_ref[...] = jnp.sum(far[...], axis=0)
+    for copy in swaps:
+        copy.wait()
+    group = w_ref.shape[3] // 3
+    for source in range(seqs):
+        for third in range(3):
+            qkv_ref[:, pl.ds(third * wide + source * group, group)] = landed[
+                source, :, pl.ds(third * group, group)
+            ].astype(F32)
+    line.drain()
+
+
+def close_all(ways, qkv_rows, attn_part, sums, inputs, gain, resid, both, tag):
+    seqs, dps = ways
+    part = qkv_rows.shape[0] // (seqs * dps)
+    wide3 = qkv_rows.shape[1]
+    rows, wide = inputs.shape
+    dma = pltpu.SemaphoreType.DMA
+    vmem = pl.BlockSpec(memory_space=pltpu.VMEM)
+    return pl.pallas_call(
+        functools.partial(closing, ways),
+        out_shape=(
+            jax.ShapeDtypeStruct((part, 3 * wide), F32),
+            jax.ShapeDtypeStruct((rows, wide), BF16),
+            jax.ShapeDtypeStruct(sums.shape, F32),
+            jax.ShapeDtypeStruct((part, dps * both.shape[2] // 2), F32),
+            jax.ShapeDtypeStruct((part, dps * both.shape[2] // 2), F32),
+        ),
+        in_specs=[vmem] * 7,
+        out_specs=(vmem,) * 5,
+        scratch_shapes=Plane.scratch(seqs, rows, wide, BF16)
+        + LineSum.scratch(dps, (seqs, part, wide3), BF16)
+        + [
+            pltpu.VMEM((seqs, part, wide3), BF16),
+            pltpu.VMEM((seqs, part, wide3), BF16),
+            pltpu.VMEM((seqs,) + sums.shape, F32),
+            pltpu.VMEM((dps,) + sums.shape, F32),
+            pltpu.VMEM(sums.shape, F32),
+            dma((seqs - 1,)),
+            dma((seqs - 1,)),
+            dma((seqs - 1,)),
+            dma((seqs - 1,)),
+            dma((dps - 1,)),
+            dma((dps - 1,)),
+        ],
+        cost_estimate=lasting(75),
+        compiler_params=pltpu.CompilerParams(collective_id=tag, has_side_effects=True),
+    )(
+        qkv_rows.reshape(seqs, dps, part, wide3),
+        attn_part.reshape(seqs, rows, wide),
+        sums,
+        inputs,
+        gain,
+        resid,
+        both,
+    )
+
+
+def opening(ways, qkv_ref, x_ref, small_ref, gate_ref, up_ref, w_ref, all_ref, given_ref, cut_ref, *sems):
+    seqs, dps = ways
+    chips, count = dps // 2, seqs * dps
+    swap_s, swap_r, line_s, line_r, pair_s, pair_r, x_s, x_r, small_s, small_r, own_sem = sems
+    seq, dp = lax.axis_index("seq"), lax.axis_index("dp")
+    chip, core = dp // 2, lax.rem(dp, 2)
+    me = seq * dps + dp
+    part, group = qkv_ref.shape[0], w_ref.shape[1] // 3
+    width = qkv_ref.shape[1] // 3
+    barrier = pltpu.get_barrier_semaphore()
+
+    def other(step):
+        at = lax.rem(me + step, count)
+        return {"seq": at // dps, "dp": lax.rem(at, dps)}
+
+    @pl.loop(1, count)
+    def _(step):
+        pl.semaphore_signal(barrier, inc=1, device_id=other(step), device_id_type=MESH)
+
+    pl.semaphore_wait(barrier, count - 1)
+
+    def block(source, owner):
+        return w_ref.at[pl.ds(pl.multiple_of((source * dps + owner) * part, part), part), :]
+
+    def piece(source, third):
+        rows = pl.ds(pl.multiple_of((source * dps + dp) * part, part), part)
+        return w_ref.at[rows, pl.ds(third * group, group)]
+
+    def columns(target, third):
+        at = pl.multiple_of(third * width + target * group, 128)
+        return qkv_ref.at[:, pl.ds(at, group)]
+
+    swaps = []
+    for step in range(1, seqs):
+        target = lax.rem(seq + step, seqs)
+        for third in range(3):
+            at = 3 * (step - 1) + third
+            swaps.append(
+                remote(
+                    columns(target, third),
+                    piece(seq, third),
+                    swap_s.at[at],
+                    swap_r.at[at],
+                    {"seq": target},
+                )
+            )
+            swaps[-1].start()
+    owns = [
+        pltpu.make_async_copy(columns(seq, third), piece(seq, third), own_sem.at[third])
+        for third in range(3)
+    ]
+    for own in owns:
+        own.start()
+
+    square = seqs == 4
+    if square:
+        _, across, along, _ = corners()
+        to_across, to_along = {"seq": across}, {"seq": along}
+        half = x_ref.shape[0] // 2
+        top, low = pl.ds(0, half), pl.ds(half, half)
+        copies = [
+            push(x_ref.at[top], all_ref.at[seq, top], x_s, x_r, 0, to_across),
+            push(x_ref.at[low], all_ref.at[seq, low], x_s, x_r, 1, to_along),
+            push(x_ref.at[low], all_ref.at[seq, low], x_s, x_r, 2, to_across),
+            push(x_ref.at[top], all_ref.at[seq, top], x_s, x_r, 3, to_along),
+        ]
+    else:
+        copies = [
+            push(x_ref, all_ref.at[seq], x_s, x_r, step - 1, {"seq": lax.rem(seq + step, seqs)})
+            for step in range(1, seqs)
+        ]
+    owns.append(pltpu.make_async_copy(x_ref, all_ref.at[seq], own_sem.at[3]))
+    owns[3].start()
+
+    def small_copy(step):
+        return remote(
+            small_ref, given_ref.at[me], small_s.at[step - 1], small_r.at[step - 1], other(step)
+        )
+
+    @pl.loop(1, count)
+    def _(step):
+        small_copy(step).start()
+
+    given_ref[me] = small_ref[...]
+
+    units = gate_ref.shape[1] // count
+
+    def cut_columns():
+        for at, weight in enumerate((gate_ref, up_ref)):
+            for source in range(seqs):
+                for owner in range(dps):
+                    cut_ref[owner, :, pl.ds((at * seqs + source) * units, units)] = weight[
+                        :, pl.ds((source * dps + owner) * units, units)
+                    ]
+
+    sibling = {"dp": 2 * chip + (1 - core)}
+    ends = (chip + 1 < chips, chip >= 1)
+    sides = ({"dp": lax.rem(dp + 2, dps)}, {"dp": lax.rem(dp - 2 + dps, dps)})
+
+    def onward(side, hop, source, owner_chip):
+        part_of = block(source[1], 2 * owner_chip + core)
+        at = (side, hop, source[0])
+        return remote(part_of, part_of, line_s.at[at], line_r.at[at], sides[side])
+
+    def share(source, owner_chip, owner_core):
+        part_of = block(source[1], 2 * owner_chip + owner_core)
+        at = (owner_chip, source[0])
+        return remote(part_of, part_of, pair_s.at[at], pair_r.at[at], sibling)
+
+    sources = [(back, lax.rem(seq - back + seqs, seqs)) for back in range(seqs)]
+    for source in sources:
+        if source[0] == 0:
+            for own in owns[:3]:
+                own.wait()
+        else:
+            for third in range(3):
+                swaps[3 * (source[0] - 1) + third].wait_recv()
+        for side in range(2):
+
+            @pl.when(ends[side])
+            def _(side=side, source=source):
+                onward(side, 0, source, chip).start()
+
+        share(source, chip, core).start()
+    if square:
+        copies[0].wait_recv()
+        copies.append(push(all_ref.at[across, top], all_ref.at[across, top], x_s, x_r, 4, to_along))
+        copies[1].wait_recv()
+        copies.append(push(all_ref.at[along, low], all_ref.at[along, low], x_s, x_r, 5, to_across))
+    cut_columns()
+    for hop in range(chips - 1):
+        for source in sources:
+            for side in range(2):
+                origin = chip - 1 - hop if side == 0 else chip + 1 + hop
+                there = origin >= 0 if side == 0 else origin < chips
+
+                @pl.when(there)
+                def _(side=side, hop=hop, source=source, origin=origin):
+                    onward(side, hop, source, origin).wait_recv()
+                    share(source, origin, core).start()
+
+                if hop < chips - 2:
+
+                    @pl.when(jnp.logical_and(there, ends[side]))
+                    def _(side=side, hop=hop, source=source, origin=origin):
+                        onward(side, hop + 1, source, origin).start()
+
+    for swapped in swaps:
+        swapped.wait_send()
+    for at, copy in enumerate(copies):
+        copy.wait_send()
+        if not square or at > 1:
+            copy.wait_recv()
+    owns[3].wait()
+
+    @pl.loop(1, count)
+    def _(step):
+        small_copy(step).wait()
+
+    for hop in range(chips - 1):
+        for source in sources:
+            for side in range(2):
+                origin = chip - hop if side == 0 else chip + hop
+                there = origin >= 0 if side == 0 else origin < chips
+
+                @pl.when(jnp.logical_and(there, ends[side]))
+                def _(side=side, hop=hop, source=source, origin=origin):
+                    onward(side, hop, source, origin).wait_send()
+
+    for owner in range(chips):
+        for source in sources:
+            share(source, owner, core).wait_send()
+            share(source, owner, 1 - core).wait_recv()
+
+
+def open_all(ways, qkv_weight, rows_in, small, gate_weight, up_weight):
+    seqs, dps = ways
+    chips, count = dps // 2, seqs * dps
+    part, group = qkv_weight.shape[0], qkv_weight.shape[1] // (3 * seqs)
+    slots = 6 if seqs == 4 else seqs - 1
+    dma = pltpu.SemaphoreType.DMA
+    return pl.pallas_call(
+        functools.partial(opening, ways),
+        out_shape=(
+            jax.ShapeDtypeStruct((part * count, 3 * group), BF16),
+            jax.ShapeDtypeStruct((seqs,) + rows_in.shape, BF16),
+            jax.ShapeDtypeStruct((count,) + small.shape, BF16),
+            jax.ShapeDtypeStruct((dps, part, 2 * gate_weight.shape[1] // dps), BF16),
+        ),
+        in_specs=[pl.BlockSpec(memory_space=pltpu.VMEM)] * 5,
+        out_specs=(
+            pl.BlockSpec(memory_space=pl.ANY),
+            pl.BlockSpec(memory_space=pl.ANY),
+            pl.BlockSpec(memory_space=pltpu.VMEM),
+            pl.BlockSpec(memory_space=pltpu.VMEM),
+        ),
+        scratch_shapes=[
+            dma((3 * (seqs - 1),)),
+            dma((3 * (seqs - 1),)),
+            dma((2, chips - 1, seqs)),
+            dma((2, chips - 1, seqs)),
+            dma((chips, seqs)),
+            dma((chips, seqs)),
+            dma((slots,)),
+            dma((slots,)),
+            dma((count - 1,)),
+            dma((count - 1,)),
+            dma((4,)),
+        ],
+        cost_estimate=lasting(75),
+        compiler_params=pltpu.CompilerParams(collective_id=0, has_side_effects=True),
+    )(qkv_weight, rows_in, small, gate_weight, up_weight)
+
+
+def after(value, *earlier):
+    return lax.optimization_barrier((value,) + earlier)[0]
 
 
 def attention_forward(queries, keys, values):
@@ -121,12 +1034,15 @@
     heads = group // HEAD_DIM
     me_seq = lax.axis_index("seq")
     grad_out = out_cotangent[0]
-    hidden_in = inputs[0].astype(F32)
-
-    small = gather(
-        jnp.concatenate([first_gain, first_shift, second_gain, second_shift, qkv_bias])[None],
-        ("seq", "dp"),
-    ).astype(F32)
+
+    small = jnp.concatenate([first_gain, first_shift, second_gain, second_shift, qkv_bias])
+    total = small.shape[0]
+    padded = -(-total // 2048) * 2048
+    small = jnp.pad(small, (0, padded - total)).reshape(padded // 128, 128)
+    qkv_full, inputs_all, small, gate_cut = open_all(
+        ways, qkv_weight, inputs[0], small, gate_weight, up_weight
+    )
+    small = small.reshape(seqs * dps, padded)[:, :total].astype(F32)
     gain_one = small[:, :part].reshape(-1)
     shift_one = small[:, part : 2 * part].reshape(-1)
     gain_two = small[:, 2 * part : 3 * part].reshape(-1)
@@ -134,29 +1050,15 @@
     bias = small[:, 4 * part :].reshape(3, seqs, group)
     bias = lax.dynamic_index_in_dim(bias, me_seq, 1, keepdims=False).reshape(3 * group)
 
-    qkv_cut = qkv_weight.reshape(part, 3, seqs, group).transpose(2, 0, 1, 3)
-    qkv_cut = swap(qkv_cut.reshape(seqs * part, 3 * group), "seq", 0, 0)
-    qkv_full = gather(qkv_cut, "dp")
+    down_full = gather(down_weight, "seq")
     out_full = gather(out_weight, "dp")
 
-    def cut_units(weight):
-        cut = weight.reshape(part, seqs, dps, units).transpose(2, 0, 1, 3)
-        return cut.reshape(dps * part, seqs * units)
-
-    gate_cut = jnp.concatenate([cut_units(gate_weight), cut_units(up_weight)], 1)
-    gate_up = gather(swap(gate_cut, "dp", 0, 0), "seq")
-    down_full = gather(down_weight, "seq")
+    gate_cut = gate_cut.reshape(dps * part, 2 * seqs * units)
+    moved = move_blocks(gate_cut, "dp", dps)
     wide = seqs * units
 
-    def to_mixed(value):
-        return value.reshape(rows, seqs, dps, part).swapaxes(1, 2).reshape(rows, width)
-
-    def from_mixed(value):
-        return value.reshape(rows, dps, seqs, part).swapaxes(1, 2).reshape(rows, width)
-
-    normed_one, inverse_one = normalize(hidden_in)
-    attn_input = (normed_one * gain_one + shift_one).astype(BF16)
-    attn_all = gather(to_mixed(attn_input), "seq")
+    normed_all, _ = normalize(inputs_all.reshape(length, width).astype(F32))
+    attn_all = (normed_all * gain_one + shift_one).astype(BF16)
     projected = dot(attn_all, qkv_full) + bias
     cosine, sine = tables(jnp.arange(length, dtype=jnp.int32).astype(F32))
 
@@ -168,20 +1070,20 @@
     values = to_heads(projected[:, 2 * group :]).astype(BF16)
     attended, log_total = attention_forward(queries, keys, values)
     attended = attended.reshape(length, group)
-    branch = scatter_sum(dot(attended, out_full).astype(BF16), "seq").astype(F32)
-    residual = hidden_in + branch
-
-    normed_two, inverse_two = normalize(residual)
-    mlp_input = (normed_two * gain_two + shift_two).astype(BF16)
-    mlp_all = gather(mlp_input, "dp")
-    grad_all = gather(grad_out, "dp")
+    moved, attended = lax.optimization_barrier((moved, attended))
+    gate_cut = place_blocks(moved, "dp")
+    branch = dot(attended, out_full).astype(BF16)
+    residual, mlp_all, grad_all, gate_up = middle_all(
+        ways, branch, inputs[0], gain_two[None], shift_two[None], grad_out, gate_cut, 1
+    )
+
     both = dot(mlp_all, gate_up)
     gate_value = both[:, :wide]
     up_value = both[:, wide:]
     sigmoid_gate = jax.nn.sigmoid(gate_value)
     activated = gate_value * sigmoid_gate
     hidden = (activated * up_value).astype(BF16)
-    layer_out = residual + scatter_sum(dot(hidden, down_full).astype(BF16), "dp").astype(F32)
+    out_part = dot(hidden, down_full).astype(BF16)
 
     hidden_grad = contract_cols(grad_all, down_full)
     gate_grad = (
@@ -189,14 +1091,21 @@
     ).astype(BF16)
     up_grad = (hidden_grad * activated).astype(BF16)
     both_grad = jnp.concatenate([gate_grad, up_grad], 1)
-    mlp_grad = scatter_sum(contract_cols(both_grad, gate_up).astype(BF16), "dp").astype(F32)
-    gain_two_grad = jnp.sum(mlp_grad * normed_two, axis=0)
-    shift_two_grad = jnp.sum(mlp_grad, axis=0)
-    residual_grad = grad_out.astype(F32) + norm_back(mlp_grad, normed_two, inverse_two, gain_two)
-    branch_grad = residual_grad.astype(BF16)
-
-    branch_all = gather(branch_grad, "seq")
+    mlp_part = contract_cols(both_grad, gate_up).astype(BF16)
+    both_rows = contract_rows(mlp_all, after(both_grad, mlp_part)).astype(BF16)
+    down_rows = contract_rows(hidden, grad_all).astype(BF16)
+    mlp_part = after(mlp_part, both_rows, down_rows)
+    residual_grad, branch_all, sums, layer_out, both_rows = turn_all(
+        ways, mlp_part, residual, gain_two[None], grad_out, out_part, both_rows, 2
+    )
+    down_rows = after(down_rows, residual_grad)
+    down_shard = scatter_sum(down_rows, "seq").astype(F32)
+    both_rows = swap(both_rows, "dp", 0, 0)
+    both_rows = both_rows.reshape(dps, part, 2 * seqs * units)
+
     attended_grad = contract_cols(branch_all, out_full).astype(BF16)
+    out_rows = contract_rows(attended, after(branch_all, attended_grad)).astype(BF16)
+    out_shard = scatter_sum(out_rows, "dp").astype(F32)
     query_grad, keys_grad, values_grad = attention_backward(
         queries, keys, values, log_total, to_heads(attended_grad)
     )
@@ -205,39 +1114,39 @@
     projected_grad = jnp.concatenate(
         [item.reshape(length, group) for item in (query_plain, keys_plain, values_grad)], 1
     )
-    attn_grad = scatter_sum(contract_cols(projected_grad, qkv_full).astype(BF16), "seq")
-    attn_grad = from_mixed(attn_grad).astype(F32)
-    gain_one_grad = jnp.sum(attn_grad * normed_one, axis=0)
-    shift_one_grad = jnp.sum(attn_grad, axis=0)
-    input_grad = residual_grad + norm_back(attn_grad, normed_one, inverse_one, gain_one)
-
-    down_shard = scatter_sum(contract_rows(hidden, grad_all).astype(BF16), "seq").astype(F32)
-    both_rows = scatter_sum(contract_rows(mlp_all, both_grad).astype(BF16), "seq")
-    both_rows = swap(both_rows, "dp", 0, 0).reshape(dps, part, 2, seqs, units)
-    both_rows = both_rows.transpose(2, 1, 3, 0, 4).reshape(2, part, seqs * dps * units).astype(F32)
-    out_shard = scatter_sum(contract_rows(attended, branch_all).astype(BF16), "dp").astype(F32)
-    qkv_rows = scatter_sum(contract_rows(attn_all, projected_grad).astype(BF16), "dp")
-    qkv_rows = swap(qkv_rows, "seq", 0, 0).reshape(seqs, part, 3, group)
-    qkv_shard = qkv_rows.transpose(1, 2, 0, 3).reshape(part, 3 * width).astype(F32)
-
+    attn_part = contract_cols(projected_grad, qkv_full).astype(BF16)
+    qkv_rows = contract_rows(attn_all, projected_grad).astype(BF16)
     bias_term = jnp.sum(projected_grad.astype(F32), axis=0).reshape(3, 1, group)
     here = (jnp.arange(seqs, dtype=jnp.int32) == me_seq).astype(F32)[None, :, None]
-    bias_term = (bias_term * here).reshape(seqs * dps, 3 * part)
-    terms = [gain_one_grad, shift_one_grad, gain_two_grad, shift_two_grad]
-    terms = [item.reshape(seqs * dps, part) for item in terms] + [bias_term]
-    tiny = scatter_sum(jnp.concatenate(terms, 1), ("seq", "dp"))[0]
+    bias_term = jnp.pad((bias_term * here).reshape(3, width), ((4, 1), (0, 0)))
+    sums = sums + bias_term
+    qkv_shard, input_grad, tiny, gate_shard, up_shard = close_all(
+        ways,
+        qkv_rows,
+        attn_part,
+        sums,
+        inputs[0],
+        gain_one[None],
+        residual_grad,
+        both_rows,
+        3,
+    )
+    me = me_seq * dps + lax.axis_index("dp")
+    mine = lax.dynamic_slice_in_dim(tiny, me * part, part, 1)
+    bias_shard = lax.dynamic_slice_in_dim(tiny[4:7].reshape(-1), me * 3 * part, 3 * part, 0)
+
     return (
-        layer_out.astype(BF16)[None],
-        input_grad.astype(BF16)[None],
-        tiny[:part],
-        tiny[part : 2 * part],
+        layer_out[None],
+        input_grad[None],
+        mine[0],
+        mine[1],
         qkv_shard,
-        tiny[4 * part :],
+        bias_shard,
         out_shard,
-        tiny[2 * part : 3 * part],
-        tiny[3 * part : 4 * part],
-        both_rows[0],
-        both_rows[1],
+        mine[2],
+        mine[3],
+        gate_shard,
+        up_shard,
         down_shard,
     )
 

time: 895 us -> 609 us (0.68)
  waiting for transfers between devices: 521 us -> 18.2 us
  Pallas kernels: 0 us -> 385 us
  blocking collectives: 141 us -> 0 us
  local copies, waits for them, and re-layouts: 66 us -> 34.9 us
  other arithmetic: 32.6 us -> 20.2 us
    pallas_call x0 -> x4, Pallas kernels: none -> 385 us  [the longest x1 113 us: close_all(): pl.pallas_call(functools.partial(closing, ways), out_shape=(jax.ShapeDtyp...]
    all_gather x8 -> x2, waiting for transfers between devices: 289 us -> 0.02 us  [gather(): return lax.all_gather(value, axis, axis=0, tiled=True)]
    reduce_scatter x8 -> x2, waiting for transfers between devices: 230 us -> 0.01 us  [scatter_sum(): return lax.psum_scatter(value, axis, scatter_dimension=0, tiled=True)]
    unnamed x2 -> x0, blocking collectives: 83.4 us -> none
    all_to_all x2 -> x0, blocking collectives: 57.8 us -> none  [swap(): lax.all_to_all(value, axis, split_axis=split, concat_axis=concat, tiled=T...]
    convert_element_type x10 -> x0, local copies, waits for them, and re-layouts: 25.6 us -> none  [the longest x2 12.2 us: shards(): both_rows.transpose(2, 1, 3, 0, 4).reshape(2, part, seqs * dps * units)]
    all_to_all x2 -> x1, waiting for transfers between devices: 0.01 us -> 15.4 us  [swap(): lax.all_to_all(value, axis, split_axis=split, concat_axis=concat, tiled=T...]
  transfers between devices with their start and end apart: 18 -> 12, of which waited for: 15 -> 3; matrix products, arithmetic and copies ran while one was open for 16% -> 16% of each run, Pallas kernels for 0% -> 48%
where the time goes in v4:
time: 609 us; the launch traced here: 600 us
  Pallas kernels  385 us (63%)
  matrix products  110 us (18%)
  local copies, waits for them, and re-layouts  34.9 us (6%)
  other arithmetic  20.2 us (3%)
  waiting for transfers between devices  18.2 us (3%)
  starting transfers between devices  17.2 us (3%)
  between operations  14.9 us (2%)
    pallas_call x1, Pallas kernels, close_all(): pl.pallas_call(functools.partial(closing, ways), out_shape=(jax.ShapeDtyp...  113 us
    pallas_call x1, Pallas kernels, turn_all(): pl.pallas_call(functools.partial(turning, ways), out_shape=(jax.ShapeDtyp...  98.8 us
    pallas_call x1, Pallas kernels, middle_all(): pl.pallas_call(functools.partial(middle, ways), out_shape=(jax.ShapeDtype...  89.2 us
    pallas_call x1, Pallas kernels, open_all(): pl.pallas_call(functools.partial(opening, ways), out_shape=(jax.ShapeDtyp...  84 us
    dot_general x4, matrix products, contract_rows(): lax.dot_general(left, right, (((0,), (0,)), ((), ())), preferred_element_...  34.2 us
    dot_general x4, matrix products, contract_cols(): lax.dot_general(left, right, (((1,), (1,)), ((), ())), preferred_element_...  27.9 us
    dot_general x4, matrix products, dot(): return jnp.dot(left, right, preferred_element_type=F32)  27.6 us
    all_to_all x1, waiting for transfers between devices, swap(): lax.all_to_all(value, axis, split_axis=split, concat_axis=concat, tiled=T...  15.4 us
  transfers between devices with their start and end apart: 12, of which 3 were waited for; matrix products, arithmetic and copies ran while one was open for 16% of the time, Pallas kernels for 48%

profile of v4, /device:TPU:0, one launch (start us, length us, event | category | flops | bytes accessed | tf_op | source)
XLA Modules:
  0.0 600.5 jit_solution(10128668310134897901)
XLA Ops:
  8.0 3.4 concatenate.47
  12.0 84.0 %shard_map.211 = (bf16[2048,1536]{1,0:T(8,128)(2,1)}, bf16[4,128,2048]{2,1,0:T(8,128)(2,1)}, bf16[32,16,128]{2,1,0:T(8,128)(2,1)}, bf16[8,64,1408]{2,1,0:T(8,128)(2,1)}) custom-call(bf16[64,6144]{1,0:T(8,128)(2,1)} %qkv_ref.1, bf16[128,2048]{1,0:T(8,128)(2,1)} %bitcast.97, bf16[16,128]{1,0:T(8,128)(2,1)} %pad_bitcast_fusion.small_ref, ...), custom_call_target="tpu_custom_call" | custom-call | bytes 225000000 | tf_op jit(solution)/shard_map/pallas_call | solution.py:942
  96.1 2.7 constant_dynamic-slice_fusion.1
  98.7 1.8 collective-permute-start.6
  100.7 2.7 collective-permute-start.3
  104.9 0.8 iota_compare_fusion
  107.8 0.8 fusion.7
  108.6 6.5 %convolution_add_fusion = f32[512,1536]{1,0:T(8,128)S(1)} fusion(bf16[512,2048]{1,0:T(8,128)(2,1)S(1)} %fusion.7, bf16[2048,1536]{1,0:T(8,128)(2,1)} %get-tuple-element.46, f32[1536]{0:T(1024)S(1)} %add.189), kind=kOutput, calls=%fused_computation.22 | convolution fusion | flops 3222011904 | bytes 11540480 | tf_op jit(solution)/shard_map/dot_general | solution.py:31
  115.4 1.5 copy-done.4
  117.7 0.9 multiply_cosine_fusion
  119.8 1.5 fusion.34
  121.4 1.2 fusion
  122.6 2.1 copy-done
  124.7 1.3 slice.208
  126.8 1.4 collective-permute-start
  128.2 5.0 fusion.11
  133.2 0.8 broadcast_in_dim_reshape.14.shift_ref
  134.7 0.8 collective-permute-done.1
  135.5 1.2 collective-permute-done
  136.9 0.9 constant_dynamic-update-slice_fusion.4
  137.8 0.9 constant_dynamic-update-slice_fusion.3
  138.8 0.9 constant_dynamic-update-slice_fusion.2
  139.7 0.9 constant_dynamic-update-slice_fusion.1
  140.7 0.9 constant_dynamic-update-slice_fusion.cut_ref
  141.7 4.7 convolution_convert_fusion.7
  146.4 89.2 %shard_map.212 = (f32[128,2048]{1,0:T(8,128)}, bf16[8,128,2048]{2,1,0:T(8,128)(2,1)}, bf16[8,128,2048]{2,1,0:T(8,128)(2,1)}, bf16[4,512,1408]{2,1,0:T(8,128)(2,1)}) custom-call(bf16[4,128,2048]{2,1,0:T(8,128)(2,1)} %bitcast.124, bf16[128,2048]{1,0:T(8,128)(2,1)} %bitcast.98, f32[1,2048]{1,0:T(1,128)} %broadcast_in_dim_reshape.6.gain_ref, ...), custom_call_target="tpu_custom_call" | custom-call | bytes 225000000 | tf_op jit(solution)/shard_map/pallas_call | solution.py:530
  235.6 11.3 %fusion.37 = f32[1024,1408]{0,1:T(8,128)} fusion(bf16[1024,2048]{1,0:T(8,128)(2,1)} %bitcast.135, bf16[2048,1408]{1,0:T(8,128)(2,1)} %bitcast.133), kind=kOutput, calls=%fused_computation.121 | convolution fusion | flops 5905580032 | bytes 15728640 | tf_op jit(solution)/shard_map/dot_general | solution.py:31
  247.0 9.0 %multiply_convert_fusion.3 = (bf16[1024,704]{0,1:T(8,128)(2,1)S(1)}, bf16[1024,704]{0,1:T(8,128)(2,1)S(1)}, bf16[1024,704]{0,1:T(8,128)(2,1)S(1)}) fusion(f32[1024,1408]{0,1:T(8,128)} %fusion.37, bf16[1024,2048]{1,0:T(8,128)(2,1)} %bitcast.137, bf16[704,2048]{1,0:T(8,128)(2,1)} %all-gather.5.cloned.1.call-done), kind=kOutput, calls=%fused_computation.30 | convolution fusion | flops 2963603456 | bytes 17170432 | tf_op jit(solution)/shard_map/dot_general | solution.py:39
  255.9 8.3 %convolution_convert_fusion.3 = bf16[1024,2048]{1,0:T(8,128)(2,1)} fusion(bf16[2048,1408]{1,0:T(8,128)(2,1)S(1)} %bitcast.134, bf16[1024,704]{0,1:T(8,128)(2,1)S(1)} %get-tuple-element.75, bf16[1024,704]{0,1:T(8,128)(2,1)S(1)} %get-tuple-element.74), kind=kOutput, calls=%fused_computation.20 | convolution fusion | flops 5913444352 | bytes 12845056 | tf_op jit(solution)/shard_map/dot_general | solution.py:39
  264.6 1.9 copy-done.28
  266.5 12.7 %convolution_convert_fusion.4 = bf16[704,2048]{1,0:T(8,128)(2,1)} fusion(bf16[1024,704]{0,1:T(8,128)(2,1)S(1)} %get-tuple-element.76, bf16[1024,2048]{1,0:T(8,128)(2,1)S(1)} %bitcast.138), kind=kOutput, calls=%fused_computation.21 | convolution fusion | flops 2954231808 | bytes 8519680 | tf_op jit(solution)/shard_map/dot_general | solution.py:35
  279.1 11.0 %convolution_convert_fusion.1 = bf16[2048,1408]{1,0:T(8,128)(2,1)} fusion(bf16[1024,2048]{1,0:T(8,128)(2,1)} %bitcast.136, bf16[1024,1408]{0,1:T(8,128)(2,1)S(1)} %pad_maximum_fusion), kind=kOutput, calls=%fused_computation.7 | convolution fusion | flops 5908463616 | bytes 12845056 | tf_op jit(solution)/shard_map/dot_general | solution.py:35
  290.2 5.1 convolution_convert_fusion.2
  295.3 98.8 %shard_map.213 = (f32[128,2048]{1,0:T(8,128)}, bf16[4,128,2048]{2,1,0:T(8,128)(2,1)}, f32[8,2048]{1,0:T(8,128)}, bf16[128,2048]{1,0:T(8,128)(2,1)}, bf16[512,1408]{1,0:T(8,128)(2,1)}) custom-call(bf16[8,128,2048]{2,1,0:T(8,128)(2,1)} %bitcast.100, f32[128,2048]{1,0:T(8,128)} %get-tuple-element.61.resid_ref, f32[1,2048]{1,0:T(1,128)} %broadcast_in_dim_reshape.6.gain_ref, ...), custom_call_target="tpu_custom_call" | custom-call | bytes 255000000 | tf_op jit(solution)/shard_map/pallas_call | solution.py:612
  394.1 3.0 convolution_convert_fusion.8
  397.2 2.6 convolution_convert_fusion.5
  401.4 5.4 multiply_reduce_fusion
  407.3 2.5 multiply_convert_fusion
  409.9 1.4 fusion.36
  411.3 0.8 slice.167
  412.0 1.8 fusion.35
  413.9 0.8 slice.163
  414.6 9.9 %all-to-all-start = ((bf16[8,64,1408]{2,1,0:T(8,128)(2,1)}), bf16[8,64,1408]{2,1,0:T(8,128)(2,1)S(1)}, u32[]{:S(2)}, u32[]{:S(2)}) async-start(bf16[8,64,1408]{2,1,0:T(8,128)(2,1)} %bitcast.125), calls=%async_computation | async-start | bytes 2883584 | tf_op jit(solution)/shard_map/all_to_all | solution.py:68
  424.6 0.9 slice_negate_fusion.1
  425.5 1.1 fusion.22
  426.6 1.0 pad_maximum_fusion.4
  427.7 1.0 pad_maximum_fusion.5
  428.7 4.8 fusion.12
  433.9 0.7 broadcast_multiply_fusion
  434.6 1.5 pad_add_fusion.sums_ref
  436.1 7.9 %convolution_convert_fusion = bf16[2048,1536]{1,0:T(8,128)(2,1)} fusion(bf16[512,2048]{1,0:T(8,128)(2,1)} %copy-done.5, bf16[512,512]{0,1:T(8,128)(2,1)S(1)} %bitcast.114, bf16[512,512]{0,1:T(8,128)(2,1)S(1)} %bitcast.122, bf16[512,512]{0,1:T(8,128)(2,1)S(1)} %bitcast.119), kind=kOutput, calls=%fused_computation.6 | convolution fusion | flops 3229089792 | bytes 9961472 | tf_op jit(solution)/shard_map/dot_general | solution.py:35
  444.0 7.6 %convolution_convert_fusion.6 = bf16[512,2048]{1,0:T(8,128)(2,1)} fusion(bf16[2048,1536]{1,0:T(8,128)(2,1)} %get-tuple-element.46, bf16[512,512]{0,1:T(8,128)(2,1)S(1)} %bitcast.115, bf16[512,512]{0,1:T(8,128)(2,1)S(1)} %bitcast.123, bf16[512,512]{0,1:T(8,128)(2,1)S(1)} %bitcast.120), kind=kOutput, calls=%fused_computation.25 | convolution fusion | flops 3226992640 | bytes 9961472 | tf_op jit(solution)/shard_map/dot_general | solution.py:39
  451.6 15.4 %all-to-all-done.both_ref = bf16[8,64,1408]{2,1,0:T(8,128)(2,1)S(1)} async-done(((bf16[8,64,1408]{2,1,0:T(8,128)(2,1)}), bf16[8,64,1408]{2,1,0:T(8,128)(2,1)S(1)}, u32[]{:S(2)}, u32[]{:S(2)}) %all-to-all-start) | async-done | bytes 1441824 | tf_op jit(solution)/shard_map/all_to_all | solution.py:68
  466.9 1.1 copy-done.2
  468.0 113.4 %shard_map.214 = (f32[64,6144]{1,0:T(8,128)}, bf16[128,2048]{1,0:T(8,128)(2,1)}, f32[8,2048]{1,0:T(8,128)}, f32[64,5632]{1,0:T(8,128)}, f32[64,5632]{1,0:T(8,128)}) custom-call(bf16[4,8,64,1536]{3,2,1,0:T(8,128)(2,1)} %bitcast.95, bf16[4,128,2048]{2,1,0:T(8,128)(2,1)} %bitcast.108, f32[8,2048]{1,0:T(8,128)} %pad_add_fusion.sums_ref, ...), custom_call_target="tpu_custom_call" | custom-call | bytes 225000000 | tf_op jit(solution)/shard_map/pallas_call | solution.py:722
  581.5 1.0 slice.138
  583.1 0.8 constant_dynamic-slice_fusion
  584.4 1.8 convert_element_type.178
  586.2 2.4 convert_element_type.179
  588.6 0.8 copy.72
  589.4 0.8 copy.73
  590.2 1.1 copy.74
  591.3 1.1 copy.75
  592.4 1.1 copy.76
  (140 shorter events, 12.8 us)
Async XLA Ops:
  7.2 134.5 %all-gather.3.cloned.1.call-start = ((), (), s32[]{:S(2)}) async-start(), calls=%async_computation.3 | async-start | bytes 2359296 | tf_op jit(solution)/shard_map/all_gather | solution.py:60
  7.9 239.0 %all-gather.5.cloned.1.call-start = ((), (), s32[]{:S(2)}) async-start(), calls=%async_computation.4 | async-start | bytes 3604480 | tf_op jit(solution)/shard_map/all_gather | solution.py:60
  96.0 9.6 %copy-start.24 = (bf16[32,16,128]{2,1,0:T(8,128)(2,1)S(1)}, bf16[32,16,128]{2,1,0:T(8,128)(2,1)}, u32[]{:S(2)}) copy-start(bf16[32,16,128]{2,1,0:T(8,128)(2,1)} %get-tuple-element.45) | copy-start | bytes 393220
  96.1 10.3 %copy-start.1 = (bf16[4,128,2048]{2,1,0:T(8,128)(2,1)S(1)}, bf16[4,128,2048]{2,1,0:T(8,128)(2,1)}, u32[]{:S(2)}) copy-start(bf16[4,128,2048]{2,1,0:T(8,128)(2,1)} %get-tuple-element.44) | copy-start | bytes 6291460
  98.7 27.4 %collective-permute-start.6 = (bf16[64,1408]{1,0:T(8,128)(2,1)}, bf16[64,1408]{1,0:T(8,128)(2,1)}, u32[]{:S(2)}, u32[]{:S(2)}) collective-permute-start(bf16[64,1408]{1,0:T(8,128)(2,1)} %get-tuple-element.79), channel_id=1, source_target_pairs={{0,7},{1,0},{2,1},{3,2},{4,3},{5,4},{6,5},{7,6},{8,15},{9,8},{10,9... | collective-permute-start | bytes 540680 | tf_op jit(solution)/shard_map/ppermute | solution.py:114
  100.6 26.2 %collective-permute-start.5 = (bf16[64,1408]{1,0:T(8,128)(2,1)}, bf16[64,1408]{1,0:T(8,128)(2,1)}, u32[]{:S(2)}, u32[]{:S(2)}) collective-permute-start(bf16[64,1408]{1,0:T(8,128)(2,1)} %get-tuple-element.80), channel_id=1, source_target_pairs={{0,6},{1,7},{2,0},{3,1},{4,2},{5,3},{6,4},{7,5},{8,14},{9,15},{10,... | collective-permute-start | bytes 540680 | tf_op jit(solution)/shard_map/ppermute | solution.py:114
  100.7 34.0 %collective-permute-start.4 = (bf16[64,1408]{1,0:T(8,128)(2,1)}, bf16[64,1408]{1,0:T(8,128)(2,1)}, u32[]{:S(2)}, u32[]{:S(2)}) collective-permute-start(bf16[64,1408]{1,0:T(8,128)(2,1)} %get-tuple-element.81), channel_id=1, source_target_pairs={{0,5},{1,6},{2,7},{3,0},{4,1},{5,2},{6,3},{7,4},{8,13},{9,14},{10,... | collective-permute-start | bytes 540680 | tf_op jit(solution)/shard_map/ppermute | solution.py:114
  100.7 34.0 %collective-permute-start.3 = (bf16[64,1408]{1,0:T(8,128)(2,1)}, bf16[64,1408]{1,0:T(8,128)(2,1)}, u32[]{:S(2)}, u32[]{:S(2)}) collective-permute-start(bf16[64,1408]{1,0:T(8,128)(2,1)} %get-tuple-element.82), channel_id=1, source_target_pairs={{0,4},{1,5},{2,6},{3,7},{4,0},{5,1},{6,2},{7,3},{8,12},{9,13},{10,... | collective-permute-start | bytes 540680 | tf_op jit(solution)/shard_map/ppermute | solution.py:114
  103.4 31.3 %collective-permute-start.2 = (bf16[64,1408]{1,0:T(8,128)(2,1)}, bf16[64,1408]{1,0:T(8,128)(2,1)}, u32[]{:S(2)}, u32[]{:S(2)}) collective-permute-start(bf16[64,1408]{1,0:T(8,128)(2,1)} %get-tuple-element.83), channel_id=1, source_target_pairs={{0,3},{1,4},{2,5},{3,6},{4,7},{5,0},{6,1},{7,2},{8,11},{9,12},{10,... | collective-permute-start | bytes 540680 | tf_op jit(solution)/shard_map/ppermute | solution.py:114
  103.7 480.7 %reduce-scatter.3.cloned.1.call-start = ((), (), s32[]{:S(2)}) async-start(), calls=%async_computation.5 | async-start | bytes 2359296 | tf_op jit(solution)/shard_map/reduce_scatter | solution.py:64
  108.6 6.6 %copy-start.5 = (bf16[512,2048]{1,0:T(8,128)(2,1)}, bf16[512,2048]{1,0:T(8,128)(2,1)S(1)}, u32[]{:S(2)}) copy-start(bf16[512,2048]{1,0:T(8,128)(2,1)S(1)} %fusion.7) | copy-start | bytes 6291460
  115.2 1.7 copy-start.4
  117.2 4.1 copy-start.9
  117.6 2.2 copy-start.21
  117.6 3.7 copy-start.7
  119.2 0.6 copy-start.20
  119.3 2.0 copy-start.16
  119.3 2.0 copy-start.18
  121.4 3.3 copy-start
  121.4 4.8 copy-start.23
  121.4 5.4 copy-start.22
  126.2 9.3 %collective-permute-start.1 = (bf16[64,1408]{1,0:T(8,128)(2,1)S(1)}, bf16[64,1408]{1,0:T(8,128)(2,1)S(1)}, u32[]{:S(2)}, u32[]{:S(2)}) collective-permute-start(bf16[64,1408]{1,0:T(8,128)(2,1)S(1)} %copy-done.23), channel_id=1, source_target_pairs={{0,2},{1,3},{2,4},{3,5},{4,6},{5,7},{6,0},{7,1},{8,10},{9,11},{10,... | collective-permute-start | bytes 540680 | tf_op jit(solution)/shard_map/ppermute | solution.py:114
  126.8 9.9 %collective-permute-start = (bf16[64,1408]{1,0:T(8,128)(2,1)S(1)}, bf16[64,1408]{1,0:T(8,128)(2,1)S(1)}, u32[]{:S(2)}, u32[]{:S(2)}) collective-permute-start(bf16[64,1408]{1,0:T(8,128)(2,1)S(1)} %copy-done.22), channel_id=1, source_target_pairs={{0,1},{1,2},{2,3},{3,4},{4,5},{5,6},{6,7},{7,0},{8,9},{9,10},{10,1... | collective-permute-start | bytes 540680 | tf_op jit(solution)/shard_map/ppermute | solution.py:114
  128.2 5.0 copy-start.26
  128.2 5.8 copy-start.25
  128.2 8.6 %copy-start.13 = (bf16[64,1408]{1,0:T(8,128)(2,1)S(1)}, bf16[64,1408]{1,0:T(8,128)(2,1)}, u32[]{:S(2)}) copy-start(bf16[64,1408]{1,0:T(8,128)(2,1)} %get-tuple-element.48) | copy-start | bytes 540676
  133.2 13.2 %copy-start.32 = (bf16[8,64,512]{2,1,0:T(8,128)(2,1)}, bf16[8,64,512]{2,1,0:T(8,128)(2,1)S(1)}, u32[]{:S(2)}) copy-start(bf16[8,64,512]{2,1,0:T(8,128)(2,1)S(1)} %fusion.11) | copy-start | bytes 1572868
  141.6 4.8 copy-start.3
  247.0 9.0 %copy-start.27 = (bf16[4,512,1408]{2,1,0:T(8,128)(2,1)S(1)}, bf16[4,512,1408]{2,1,0:T(8,128)(2,1)}, u32[]{:S(2)}) copy-start(bf16[4,512,1408]{2,1,0:T(8,128)(2,1)} %get-tuple-element.58) | copy-start | bytes 17301508
  255.9 8.6 %copy-start.34 = (bf16[1024,704]{0,1:T(8,128)(2,1)}, bf16[1024,704]{0,1:T(8,128)(2,1)S(1)}, u32[]{:S(2)}) copy-start(bf16[1024,704]{0,1:T(8,128)(2,1)S(1)} %get-tuple-element.76) | copy-start | bytes 4325380
  264.3 2.2 copy-start.28
  279.1 11.0 %copy-start.29 = (bf16[704,2048]{1,0:T(8,128)(2,1)S(1)}, bf16[704,2048]{1,0:T(8,128)(2,1)}, u32[]{:S(2)}) copy-start(bf16[704,2048]{1,0:T(8,128)(2,1)} %all-gather.5.cloned.1.call-done) | copy-start | bytes 8650756
  279.1 11.0 %copy-start.35 = (bf16[1024,704]{0,1:T(8,128)(2,1)S(1)}, bf16[1024,704]{0,1:T(8,128)(2,1)}, u32[]{:S(2)}) copy-start(bf16[1024,704]{0,1:T(8,128)(2,1)} %copy-done.34) | copy-start | bytes 4325380
  295.3 98.8 %copy-start.30 = (bf16[512,2048]{1,0:T(8,128)(2,1)S(1)}, bf16[512,2048]{1,0:T(8,128)(2,1)}, u32[]{:S(2)}) copy-start(bf16[512,2048]{1,0:T(8,128)(2,1)} %all-gather.3.cloned.1.call-done) | copy-start | bytes 6291460
  394.1 3.1 copy-start.31
  394.1 3.1 copy-start.33
  399.7 186.4 %reduce-scatter.5.cloned.1.call-start = ((), (), s32[]{:S(2)}) async-start(), calls=%async_computation.6 | async-start | bytes 3604480 | tf_op jit(solution)/shard_map/reduce_scatter | solution.py:64
  401.4 5.5 slice-start
  401.4 5.8 slice-start.1
  407.3 2.6 copy-start.10
  407.3 2.6 copy-start.19
  409.8 2.2 copy-start.8
  409.9 2.2 copy-start.17
  414.6 52.3 %all-to-all-start = ((bf16[8,64,1408]{2,1,0:T(8,128)(2,1)}), bf16[8,64,1408]{2,1,0:T(8,128)(2,1)S(1)}, u32[]{:S(2)}, u32[]{:S(2)}) async-start(bf16[8,64,1408]{2,1,0:T(8,128)(2,1)} %bitcast.125), calls=%async_computation | async-start | bytes 2883584 | tf_op jit(solution)/shard_map/all_to_all | solution.py:68
  466.9 1.1 copy-start.2
  581.4 7.1 %copy-start.14 = (bf16[128,2048]{1,0:T(8,128)(2,1)S(1)}, bf16[128,2048]{1,0:T(8,128)(2,1)}, u32[]{:S(2)}) copy-start(bf16[128,2048]{1,0:T(8,128)(2,1)} %get-tuple-element.62) | copy-start | bytes 1572868
  581.4 7.9 %copy-start.15 = (bf16[128,2048]{1,0:T(8,128)(2,1)S(1)}, bf16[128,2048]{1,0:T(8,128)(2,1)}, u32[]{:S(2)}) copy-start(bf16[128,2048]{1,0:T(8,128)(2,1)} %get-tuple-element.67) | copy-start | bytes 1572868
  581.5 8.7 %copy-start.6 = (f32[64,6144]{1,0:T(8,128)S(1)}, f32[64,6144]{1,0:T(8,128)}, u32[]{:S(2)}) copy-start(f32[64,6144]{1,0:T(8,128)} %get-tuple-element.136) | copy-start | bytes 4718596
  588.6 2.7 copy-start.12
  590.2 2.2 copy-start.11
Sparse Core Ops, SparseCore 0:
  9.6 43.7 all-gather.2
  103.8 41.3 all-gather.4
  399.9 47.8 reduce-scatter.2
  450.7 58.5 reduce-scatter.4

commit v5 on v4

--- a/solution.py
+++ b/solution.py
@@ -39,21 +39,26 @@
     return lax.dot_general(left, right, (((1,), (1,)), ((), ())), preferred_element_type=F32)
 
 
-def tables(positions):
+def tables(length):
     half_rot = ROT // 2
-    freqs = 10000.0 ** (-(2.0 * jnp.arange(half_rot, dtype=F32)) / ROT)
-    angles = positions[:, None] * freqs[None, :]
-    cosine = jnp.cos(angles)
-    sine = jnp.sin(angles)
-    return (jnp.concatenate([cosine, cosine], -1), jnp.concatenate([sine, sine], -1))
-
-
-def rotate(heads_in, cosine, sine):
+    lane = lax.rem(lax.broadcasted_iota(jnp.int32, (length, 128), 1), HEAD_DIM)
+    position = lax.broadcasted_iota(jnp.int32, (length, 128), 0).astype(F32)
+    freqs = 10000.0 ** (-(2.0 * lax.rem(lane, half_rot).astype(F32)) / ROT)
+    angles = position * freqs
+    cosine, sine = jnp.cos(angles), jnp.sin(angles)
+    return jnp.stack(
+        [
+            jnp.where(lane < ROT, cosine, 1.0),
+            jnp.where(lane < half_rot, -sine, 0.0),
+            jnp.where((lane >= half_rot) & (lane < ROT), sine, 0.0),
+        ]
+    )
+
+
+def turn_lanes(value, table_ref, sign):
     half_rot = ROT // 2
-    rotary = heads_in[..., :ROT]
-    turned = jnp.concatenate([-rotary[..., half_rot:], rotary[..., :half_rot]], -1)
-    moved = rotary * cosine[:, None, :] + turned * sine[:, None, :]
-    return jnp.concatenate([moved, heads_in[..., ROT:]], -1)
+    ahead, behind = pltpu.roll(value, 128 - half_rot, 1), pltpu.roll(value, half_rot, 1)
+    return value * table_ref[0] + sign * (ahead * table_ref[1] + behind * table_ref[2])
 
 
 def gather(value, axis):
@@ -62,10 +67,6 @@
 
 def scatter_sum(value, axis):
     return lax.psum_scatter(value, axis, scatter_dimension=0, tiled=True)
-
-
-def swap(value, axis, split, concat):
-    return lax.all_to_all(value, axis, split_axis=split, concat_axis=concat, tiled=True)
 
 
 MESH = pl.DeviceIdType.MESH
@@ -101,29 +102,6 @@
     across = high * 2 + (1 - low)
     along = (1 - high) * 2 + low
     return me, across, along, 3 - me
-
-
-def move_blocks(value, axis, count):
-    rows = value.shape[0] // count
-    me = lax.axis_index(axis)
-    blocks = []
-    for step in range(count):
-        at = lax.rem(me + step, count) * rows
-        block = lax.dynamic_slice_in_dim(value, at, rows, 0)
-        if step:
-            block = lax.ppermute(block, axis, [(i, (i + step) % count) for i in range(count)])
-        blocks.append(block)
-    return blocks
-
-
-def place_blocks(blocks, axis):
-    count, rows = len(blocks), blocks[0].shape[0]
-    me = lax.axis_index(axis)
-    out = jnp.zeros((count * rows,) + blocks[0].shape[1:], blocks[0].dtype)
-    for step, block in enumerate(blocks):
-        at = lax.rem(me - step + count, count) * rows
-        out = lax.dynamic_update_slice_in_dim(out, block, at, 0)
-    return out
 
 
 def remote(source, target, send, recv, peer):
@@ -217,20 +195,22 @@
         self.block, self.pair, self.moving = block, pair, moving
         self.sems = (line_s, line_r, pair_s, pair_r)
         self.chips, self.chip, self.core, self.ends, self.sides, self.sibling = line_place(dps)
-
-    def share(self, owner, owner_core):
+        self.pieces = pair.shape[1]
+
+    def share(self, owner, owner_core, piece):
+        at = (owner, piece)
         return remote(
-            self.block(2 * owner + owner_core),
-            self.pair.at[owner],
-            self.sems[2].at[owner],
-            self.sems[3].at[owner],
+            self.block(2 * owner + owner_core).at[piece],
+            self.pair.at[at],
+            self.sems[2].at[at],
+            self.sems[3].at[at],
             self.sibling,
         )
 
-    def onward(self, side, owner):
-        at = (side, owner)
+    def onward(self, side, owner, piece):
+        at = (side, owner, piece)
         return remote(
-            self.pair.at[owner],
+            self.pair.at[owner, piece],
             self.moving.at[at],
             self.sems[0].at[at],
             self.sems[1].at[at],
@@ -242,91 +222,93 @@
             at for both in zip(range(self.chips - 1, -1, -1), range(self.chips)) for at in both
         ]
         for owner in dict.fromkeys(order):
-            self.share(owner, 1 - self.core).start()
-
-    def add(self, owner, side):
+            for piece in range(self.pieces):
+                self.share(owner, 1 - self.core, piece).start()
+
+    def add(self, owner, piece, side):
         own = self.block(2 * owner + self.core)
 
-        def one(at):
-            value = self.pair[(owner,) + at].astype(F32) + own[at].astype(F32)
+        def one(here):
+            value = self.pair[owner, piece, here].astype(F32) + own[piece, here].astype(F32)
             if side is not None:
-                value = value + self.moving[(side, owner) + at].astype(F32)
-            self.pair[(owner,) + at] = value.astype(self.pair.dtype)
-
-        if len(own.shape) > 2:
-            for at in range(own.shape[0]):
-                one((at,))
-        else:
-            by_chunks(own.shape[0], lambda here: one((here,)))
+                value = value + self.moving[side, owner, piece, here].astype(F32)
+            self.pair[owner, piece, here] = value.astype(self.pair.dtype)
+
+        by_chunks(self.pair.shape[2], one)
 
     def step(self, at):
-        for side in range(2):
-            owner = self.chips - 1 - at if side == 0 else at
-            passing = self.chip < owner if side == 0 else self.chip > owner
-            fed = jnp.logical_and(passing, self.ends[1 - side])
-
-            @pl.when(passing)
-            def _(owner=owner):
-                self.share(owner, self.core).wait_recv()
-
-            @pl.when(fed)
-            def _(side=side, owner=owner):
-                self.onward(side, owner).wait_recv()
-                self.add(owner, side)
-
-            @pl.when(jnp.logical_and(passing, jnp.logical_not(fed)))
-            def _(owner=owner):
-                self.add(owner, None)
-
-            @pl.when(passing)
-            def _(side=side, owner=owner):
-                self.onward(side, owner).start()
+        for piece in range(self.pieces):
+            for side in range(2):
+                owner = self.chips - 1 - at if side == 0 else at
+                passing = self.chip < owner if side == 0 else self.chip > owner
+                fed = jnp.logical_and(passing, self.ends[1 - side])
+
+                @pl.when(passing)
+                def _(owner=owner, piece=piece):
+                    self.share(owner, self.core, piece).wait_recv()
+
+                @pl.when(fed)
+                def _(side=side, owner=owner, piece=piece):
+                    self.onward(side, owner, piece).wait_recv()
+                    self.add(owner, piece, side)
+
+                @pl.when(jnp.logical_and(passing, jnp.logical_not(fed)))
+                def _(owner=owner, piece=piece):
+                    self.add(owner, piece, None)
+
+                @pl.when(passing)
+                def _(side=side, owner=owner, piece=piece):
+                    self.onward(side, owner, piece).start()
 
     def end(self):
         for owner in range(self.chips):
-
-            @pl.when(self.chip == owner)
-            def _(owner=owner):
-                self.share(owner, self.core).wait_recv()
-
-            for side in range(2):
-
-                @pl.when(jnp.logical_and(self.chip == owner, self.ends[1 - side]))
-                def _(side=side, owner=owner):
-                    self.onward(side, owner).wait_recv()
-
-                @pl.when(jnp.logical_and(self.chip == owner, jnp.logical_not(self.ends[1 - side])))
-                def _(side=side, owner=owner):
-                    self.moving[side, owner] = jnp.zeros(self.moving.shape[2:], self.moving.dtype)
-
-    def total(self, at):
+            for piece in range(self.pieces):
+
+                @pl.when(self.chip == owner)
+                def _(owner=owner, piece=piece):
+                    self.share(owner, self.core, piece).wait_recv()
+
+                for side in range(2):
+
+                    @pl.when(jnp.logical_and(self.chip == owner, self.ends[1 - side]))
+                    def _(side=side, owner=owner, piece=piece):
+                        self.onward(side, owner, piece).wait_recv()
+
+        for side in range(2):
+
+            @pl.when(jnp.logical_not(self.ends[1 - side]))
+            def _(side=side):
+                self.moving[side, self.chip] = jnp.zeros(self.moving.shape[2:], self.moving.dtype)
+
+    def total(self, piece, here):
         own = self.block(2 * self.chip + self.core)
-        value = own[at].astype(F32) + self.pair[(self.chip,) + at].astype(F32)
+        value = own[piece, here].astype(F32) + self.pair[self.chip, piece, here].astype(F32)
         for side in range(2):
-            value = value + self.moving[(side, self.chip) + at].astype(F32)
+            value = value + self.moving[side, self.chip, piece, here].astype(F32)
         return value
 
     def drain(self):
         for owner in range(self.chips):
-            for side in range(2):
-                passing = self.chip < owner if side == 0 else self.chip > owner
-
-                @pl.when(passing)
-                def _(side=side, owner=owner):
-                    self.onward(side, owner).wait_send()
-
-            self.share(owner, 1 - self.core).wait_send()
+            for piece in range(self.pieces):
+                for side in range(2):
+                    passing = self.chip < owner if side == 0 else self.chip > owner
+
+                    @pl.when(passing)
+                    def _(side=side, owner=owner, piece=piece):
+                        self.onward(side, owner, piece).wait_send()
+
+                self.share(owner, 1 - self.core, piece).wait_send()
 
     @staticmethod
     def scratch(dps, shape, dtype):
-        dma, chips = pltpu.SemaphoreType.DMA, dps // 2
+        dma, chips, pieces = pltpu.SemaphoreType.DMA, dps // 2, shape[0]
         return [
             pltpu.VMEM((chips,) + shape, dtype),
             pltpu.VMEM((2, chips) + shape, dtype),
-            dma((2, chips)),
-            dma((2, chips)),
-            dma((chips,)),
-            dma((chips,)),
+            dma((2, chips, pieces)),
+            dma((2, chips, pieces)),
+            dma((chips, pieces)),
+            dma((chips, pieces)),
         ]
 
 
@@ -479,6 +461,19 @@
         body(pl.ds(pl.multiple_of(at * CHUNK, CHUNK), CHUNK))
 
 
+PIECES = 2
+
+
+def by_pieces(rows, body):
+    size = rows // PIECES
+    for piece in range(PIECES):
+
+        @pl.loop(0, size // CHUNK)
+        def _(at, piece=piece):
+            here = pl.multiple_of(at * CHUNK, CHUNK)
+            body(pl.ds(pl.multiple_of(piece * size + here, CHUNK), CHUNK), piece, pl.ds(here, CHUNK))
+
+
 def meet_cross(ways):
     seqs, dps = ways
     seq, dp = lax.axis_index("seq"), lax.axis_index("dp")
@@ -486,67 +481,6 @@
     dp_peers = [lax.rem(dp + step, dps) for step in range(1, dps)]
     meet([{"seq": peer} for peer in seq_peers] + [{"dp": peer} for peer in dp_peers])
     return seq_peers, dp_peers
-
-
-def middle(ways, part_ref, x_ref, gain_ref, shift_ref, grad_ref, cut_ref, *rest):
-    seqs, dps = ways
-    resid_ref, all_ref, grads_ref, gate_ref = rest[:4]
-    plane = Plane(seqs, part_ref, *rest[4:8])
-    own = rest[8]
-    moved = LineGather(dps, own, all_ref, *rest[9:14])
-    grads = LineGather(dps, grad_ref, grads_ref, *rest[14:19])
-    gates = PlaneGather(seqs, cut_ref, gate_ref, *rest[19:22])
-    hops = dps // 2 - 1
-    meet_cross(ways)
-    plane.begin()
-    grads.begin()
-    plane.relay()
-    plane.end()
-    gates.begin()
-    gain, shift = gain_ref[...], shift_ref[...]
-
-    def one(here):
-        resid = x_ref[here, :].astype(F32) + plane.total(here)
-        resid_ref[here, :] = resid
-        normed, _ = normalize(resid)
-        own[here, :] = (normed * gain + shift).astype(own.dtype)
-
-    by_chunks(x_ref.shape[0], one)
-    moved.begin()
-    for hop in range(hops):
-        grads.hop(hop)
-        if hop == hops - 1:
-            gates.relay()
-        moved.hop(hop)
-    grads.end()
-    moved.end()
-    gates.end()
-
-
-def middle_all(ways, part, inputs, gain, shift, grad_out, cut, tag):
-    seqs, dps = ways
-    rows, wide = inputs.shape
-    vmem, anywhere = (pl.BlockSpec(memory_space=space) for space in (pltpu.VMEM, pl.ANY))
-    resid, moved, grads, gate = pl.pallas_call(
-        functools.partial(middle, ways),
-        out_shape=(
-            jax.ShapeDtypeStruct((rows, wide), F32),
-            jax.ShapeDtypeStruct((dps, rows, wide), BF16),
-            jax.ShapeDtypeStruct((dps, rows, wide), BF16),
-            jax.ShapeDtypeStruct((seqs,) + cut.shape, BF16),
-        ),
-        in_specs=[vmem] * 6,
-        out_specs=(vmem, anywhere, anywhere, anywhere),
-        scratch_shapes=Plane.scratch(seqs, rows, wide, BF16)
-        + [pltpu.VMEM((rows, wide), BF16)]
-        + LineGather.scratch(dps)
-        + LineGather.scratch(dps)
-        + PlaneGather.scratch(seqs),
-        cost_estimate=lasting(75),
-        compiler_params=pltpu.CompilerParams(collective_id=tag, has_side_effects=True),
-    )(part.reshape(seqs, rows, wide), inputs, gain, shift, grad_out, cut)
-    moved, grads = (item.reshape(dps * rows, wide) for item in (moved, grads))
-    return resid, moved, grads, gate.reshape(seqs * cut.shape[0], cut.shape[1])
 
 
 def turning(ways, part_ref, resid_ref, gain_ref, grad_ref, out_ref, both_ref, *rest):
@@ -571,8 +505,8 @@
     sums_ref[...] = jnp.zeros(sums_ref.shape, F32)
     gain = gain_ref[...]
 
-    def one(here):
-        grad = line.total((here,))
+    def one(here, piece, inner):
+        grad = line.total(piece, inner)
         normed, inverse = normalize(resid_ref[here, :])
         sums_ref[2:3, :] += jnp.sum(grad * normed, axis=0, keepdims=True)
         sums_ref[3:4, :] += jnp.sum(grad, axis=0, keepdims=True)
@@ -580,7 +514,7 @@
         total_ref[here, :] = total
         own[here, :] = total.astype(own.dtype)
 
-    by_chunks(resid_ref.shape[0], one)
+    by_pieces(resid_ref.shape[0], one)
     gathered.begin()
     if chips > 1:
         outs.step(1)
@@ -596,10 +530,10 @@
     gathered.end()
     outs.end()
 
-    def three(here):
-        layer_ref[here, :] = (resid_ref[here, :] + outs.total((here,))).astype(layer_ref.dtype)
-
-    by_chunks(resid_ref.shape[0], three)
+    def three(here, piece, inner):
+        layer_ref[here, :] = (resid_ref[here, :] + outs.total(piece, inner)).astype(layer_ref.dtype)
+
+    by_pieces(resid_ref.shape[0], three)
     line.drain()
     outs.drain()
 
@@ -620,24 +554,181 @@
         ),
         in_specs=[vmem] * 6,
         out_specs=(vmem, anywhere, vmem, vmem, vmem),
-        scratch_shapes=LineSum.scratch(dps, (rows, wide), BF16)
+        scratch_shapes=LineSum.scratch(dps, (PIECES, rows // PIECES, wide), BF16)
         + [pltpu.VMEM((rows, wide), BF16)]
         + PlaneGather.scratch(seqs)
-        + LineSum.scratch(dps, (rows, wide), BF16)
+        + LineSum.scratch(dps, (PIECES, rows // PIECES, wide), BF16)
         + Plane.scratch(seqs, cut[0], cut[1], BF16),
         cost_estimate=lasting(85),
         compiler_params=pltpu.CompilerParams(
             collective_id=tag, has_side_effects=True, vmem_limit_bytes=60 * 2**20
         ),
     )(
-        part.reshape(dps, rows, wide),
+        part.reshape(dps, PIECES, rows // PIECES, wide),
         resid,
         gain,
         grad_out,
-        out_part.reshape(dps, rows, wide),
+        out_part.reshape(dps, PIECES, rows // PIECES, wide),
         both.reshape((seqs,) + cut),
     )
     return total, gathered.reshape(seqs * rows, wide), sums, layer, both
+
+
+class SwapDp:
+
+    def __init__(self, dps, x_ref, o_ref, send, recv, local):
+        dp = lax.axis_index("dp")
+        self.peers = [lax.rem(dp + step, dps) for step in range(1, dps)]
+        self.parts = (x_ref, o_ref, send, recv, local, dp)
+
+    def begin(self):
+        x, o, send, recv, local, dp = self.parts
+        self.copies = [
+            push(x.at[peer], o.at[dp], send, recv, at, {"dp": peer})
+            for at, peer in enumerate(self.peers)
+        ]
+        self.own = pltpu.make_async_copy(x.at[dp], o.at[dp], local)
+        self.own.start()
+
+    def end(self):
+        for copy in self.copies:
+            copy.wait()
+        self.own.wait()
+
+    @staticmethod
+    def scratch(dps):
+        dma = pltpu.SemaphoreType.DMA
+        return [dma((dps - 1,)), dma((dps - 1,)), dma]
+
+
+def halves():
+    lane = lax.broadcasted_iota(jnp.int32, (1, 128), 1)
+    return lane, (lane < HEAD_DIM, lane >= HEAD_DIM)
+
+
+def reversing(
+    ways, grads_ref, out_ref, qkv_ref, lse_ref, table_ref, w_ref, attn_ref, att_ref, both_ref, *rest
+):
+    dps = ways[1]
+    part_ref, rows_ref, bias_ref, outs_ref, swapped_ref = rest[:5]
+    swap = SwapDp(dps, both_ref, swapped_ref, *rest[5:8])
+    pg_ref, grad_ref = rest[8:10]
+    dp = lax.axis_index("dp")
+    meet([{"dp": lax.rem(dp + step, dps)} for step in range(1, dps)])
+    swap.begin()
+    length, wide = grads_ref.shape
+    group = out_ref.shape[0]
+    scale = HEAD_DIM ** (-0.5)
+    size = min(256, length)
+    tile = min(256, group)
+
+    @pl.loop(0, group // tile)
+    def _(at):
+        columns = pl.ds(pl.multiple_of(at * tile, tile), tile)
+        grad_ref[:, columns] = contract_cols(grads_ref[...], out_ref[columns, :]).astype(
+            grad_ref.dtype
+        )
+
+    _, sides = halves()
+    triangle = lax.broadcasted_iota(jnp.int32, (size, size), 0) <= lax.broadcasted_iota(
+        jnp.int32, (size, size), 1
+    )
+
+    @pl.loop(0, group // 128)
+    def _(at):
+        base = pl.multiple_of(at * 128, 128)
+        query_lanes, key_lanes, value_lanes = (
+            pl.ds(third * group + base, 128) for third in range(3)
+        )
+        key_sums = [[None] * (length // size) for _ in range(2)]
+        value_sums = [[None] * (length // size) for _ in range(2)]
+        for block in range(length // size):
+            rows = pl.ds(block * size, size)
+            seen = (block + 1) * size
+            query = qkv_ref[rows, query_lanes]
+            key = qkv_ref[pl.ds(0, seen), key_lanes]
+            value = qkv_ref[pl.ds(0, seen), value_lanes]
+            grad = grad_ref[rows, pl.ds(base, 128)]
+            query_sums = []
+            for half in range(2):
+                mine = jnp.where(sides[half], query, jnp.zeros_like(query))
+                given = jnp.where(sides[half], grad, jnp.zeros_like(grad))
+                scores = contract_cols(key, mine) * scale
+                total = lse_ref[pl.ds(2 * at + half, 1), rows]
+                probs = jnp.exp(scores - total)
+                last = jnp.where(triangle, probs[block * size :], 0.0)
+                probs = jnp.concatenate([probs[: block * size], last], 0) if block else last
+                probs_grad = contract_cols(value, given)
+                tilt = jnp.sum(probs * probs_grad, axis=0, keepdims=True)
+                scores_grad = (probs * (probs_grad - tilt)).astype(BF16)
+                probs_low = probs.astype(BF16)
+                query_sums.append(contract_rows(scores_grad, key))
+                for part in range(block + 1):
+                    cut = slice(part * size, (part + 1) * size)
+                    for sums, left, right in (
+                        (key_sums, scores_grad, query),
+                        (value_sums, probs_low, grad),
+                    ):
+                        more = dot(left[cut], right)
+                        held = sums[half][part]
+                        sums[half][part] = more if held is None else held + more
+            total = (jnp.where(sides[0], query_sums[0], query_sums[1]) * scale).astype(BF16)
+            table = table_ref.at[:, rows]
+            pg_ref[rows, query_lanes] = turn_lanes(total.astype(F32), table, -1.0).astype(BF16)
+        for part in range(length // size):
+            rows = pl.ds(part * size, size)
+            total = jnp.where(sides[0], key_sums[0][part], key_sums[1][part]) * scale
+            table = table_ref.at[:, rows]
+            total = total.astype(BF16).astype(F32)
+            pg_ref[rows, key_lanes] = turn_lanes(total, table, -1.0).astype(BF16)
+            total = jnp.where(sides[0], value_sums[0][part], value_sums[1][part])
+            pg_ref[rows, value_lanes] = total.astype(BF16)
+
+    bias_ref[...] = jnp.zeros(bias_ref.shape, F32)
+
+    @pl.loop(0, length // CHUNK)
+    def _(at):
+        here = pl.ds(pl.multiple_of(at * CHUNK, CHUNK), CHUNK)
+        bias_ref[0:1, :] += jnp.sum(pg_ref[here, :].astype(F32), axis=0, keepdims=True)
+
+    step = min(256, wide)
+
+    @pl.loop(0, wide // step)
+    def _(at):
+        columns = pl.ds(pl.multiple_of(at * step, step), step)
+        part_ref[:, columns] = contract_cols(pg_ref[...], w_ref[columns, :]).astype(part_ref.dtype)
+        rows_ref[columns, :] = contract_rows(attn_ref[:, columns], pg_ref[...]).astype(
+            rows_ref.dtype
+        )
+        outs_ref[:, columns] = contract_rows(att_ref[...], grads_ref[:, columns]).astype(
+            outs_ref.dtype
+        )
+
+    swap.end()
+
+
+def reverse_all(ways, grads, out_full, qkv, lse, table, qkv_full, attn_all, attended, both, tag):
+    length, wide = grads.shape
+    group = out_full.shape[0]
+    vmem, anywhere = (pl.BlockSpec(memory_space=space) for space in (pltpu.VMEM, pl.ANY))
+    return pl.pallas_call(
+        functools.partial(reversing, ways),
+        out_shape=(
+            jax.ShapeDtypeStruct((length, wide), BF16),
+            jax.ShapeDtypeStruct((wide, 3 * group), BF16),
+            jax.ShapeDtypeStruct((8, 3 * group), F32),
+            jax.ShapeDtypeStruct((group, wide), BF16),
+            jax.ShapeDtypeStruct(both.shape, BF16),
+        ),
+        in_specs=[vmem] * 9,
+        out_specs=(vmem,) * 4 + (anywhere,),
+        scratch_shapes=SwapDp.scratch(ways[1])
+        + [pltpu.VMEM((length, 3 * group), BF16), pltpu.VMEM((length, group), BF16)],
+        cost_estimate=lasting(45),
+        compiler_params=pltpu.CompilerParams(
+            collective_id=tag, has_side_effects=True, vmem_limit_bytes=60 * 2**20
+        ),
+    )(grads, out_full, qkv, lse, table, qkv_full, attn_all, attended, both)
 
 
 def closing(ways, w_ref, g_ref, sums_ref, x_ref, gain_ref, resid_ref, both_ref, *rest):
@@ -692,7 +783,11 @@
         line.step(at)
     line.end()
     for source in range(seqs):
-        mine[source] = line.total((source,)).astype(mine.dtype)
+
+        def three(here, source=source):
+            mine[source, here] = line.total(source, here).astype(mine.dtype)
+
+        by_chunks(mine.shape[1], three)
     swaps = [
         push(mine.at[peer], landed.at[seq], swap_s, swap_r, at, {"seq": peer})
         for at, peer in enumerate(seq_peers)
@@ -758,15 +853,53 @@
     )
 
 
-def opening(ways, qkv_ref, x_ref, small_ref, gate_ref, up_ref, w_ref, all_ref, given_ref, cut_ref, *sems):
+def front(
+    ways,
+    qkv_weight_ref,
+    in_ref,
+    small_ref,
+    gate_ref,
+    up_ref,
+    out_weight_ref,
+    grad_ref,
+    table_ref,
+    w_ref,
+    attn_ref,
+    qkv_ref,
+    att_ref,
+    lse_ref,
+    out_ref,
+    vec_ref,
+    resid_ref,
+    all_ref,
+    grads_ref,
+    both_ref,
+    *rest,
+):
     seqs, dps = ways
     chips, count = dps // 2, seqs * dps
-    swap_s, swap_r, line_s, line_r, pair_s, pair_r, x_s, x_r, small_s, small_r, own_sem = sems
+    rest = list(rest)
+
+    def take(size):
+        taken = rest[:size]
+        del rest[:size]
+        return taken
+
+    x_ref, given_ref, bias_ref, cut_ref, swapped_ref, branch_ref, own_ref = take(7)
+    gathered = PlaneGather(seqs, in_ref, x_ref, *take(3))
+    outs = LineGather(dps, out_weight_ref, out_ref, *take(5))
+    swap = SwapDp(dps, cut_ref, swapped_ref, *take(3))
+    plane = Plane(seqs, branch_ref, *take(4))
+    moved = LineGather(dps, own_ref, all_ref, *take(5))
+    grads = LineGather(dps, grad_ref, grads_ref, *take(5))
+    gates = PlaneGather(seqs, swapped_ref, both_ref, *take(3))
+    swap_s, swap_r, line_s, line_r, pair_s, pair_r, small_s, small_r, own_sem = take(9)
     seq, dp = lax.axis_index("seq"), lax.axis_index("dp")
-    chip, core = dp // 2, lax.rem(dp, 2)
+    _, chip, core, ends, sides, sibling = line_place(dps)
     me = seq * dps + dp
-    part, group = qkv_ref.shape[0], w_ref.shape[1] // 3
-    width = qkv_ref.shape[1] // 3
+    part, group = qkv_weight_ref.shape[0], w_ref.shape[1] // 3
+    rows, width = in_ref.shape
+    length = rows * seqs
     barrier = pltpu.get_barrier_semaphore()
 
     def other(step):
@@ -783,12 +916,12 @@
         return w_ref.at[pl.ds(pl.multiple_of((source * dps + owner) * part, part), part), :]
 
     def piece(source, third):
-        rows = pl.ds(pl.multiple_of((source * dps + dp) * part, part), part)
-        return w_ref.at[rows, pl.ds(third * group, group)]
+        here = pl.ds(pl.multiple_of((source * dps + dp) * part, part), part)
+        return w_ref.at[here, pl.ds(third * group, group)]
 
     def columns(target, third):
         at = pl.multiple_of(third * width + target * group, 128)
-        return qkv_ref.at[:, pl.ds(at, group)]
+        return qkv_weight_ref.at[:, pl.ds(at, group)]
 
     swaps = []
     for step in range(1, seqs):
@@ -796,15 +929,15 @@
         for third in range(3):
             at = 3 * (step - 1) + third
             swaps.append(
-                remote(
+                push(
                     columns(target, third),
                     piece(seq, third),
-                    swap_s.at[at],
-                    swap_r.at[at],
+                    swap_s,
+                    swap_r,
+                    at,
                     {"seq": target},
                 )
             )
-            swaps[-1].start()
     owns = [
         pltpu.make_async_copy(columns(seq, third), piece(seq, third), own_sem.at[third])
         for third in range(3)
@@ -812,26 +945,6 @@
     for own in owns:
         own.start()
 
-    square = seqs == 4
-    if square:
-        _, across, along, _ = corners()
-        to_across, to_along = {"seq": across}, {"seq": along}
-        half = x_ref.shape[0] // 2
-        top, low = pl.ds(0, half), pl.ds(half, half)
-        copies = [
-            push(x_ref.at[top], all_ref.at[seq, top], x_s, x_r, 0, to_across),
-            push(x_ref.at[low], all_ref.at[seq, low], x_s, x_r, 1, to_along),
-            push(x_ref.at[low], all_ref.at[seq, low], x_s, x_r, 2, to_across),
-            push(x_ref.at[top], all_ref.at[seq, top], x_s, x_r, 3, to_along),
-        ]
-    else:
-        copies = [
-            push(x_ref, all_ref.at[seq], x_s, x_r, step - 1, {"seq": lax.rem(seq + step, seqs)})
-            for step in range(1, seqs)
-        ]
-    owns.append(pltpu.make_async_copy(x_ref, all_ref.at[seq], own_sem.at[3]))
-    owns[3].start()
-
     def small_copy(step):
         return remote(
             small_ref, given_ref.at[me], small_s.at[step - 1], small_r.at[step - 1], other(step)
@@ -842,20 +955,7 @@
         small_copy(step).start()
 
     given_ref[me] = small_ref[...]
-
-    units = gate_ref.shape[1] // count
-
-    def cut_columns():
-        for at, weight in enumerate((gate_ref, up_ref)):
-            for source in range(seqs):
-                for owner in range(dps):
-                    cut_ref[owner, :, pl.ds((at * seqs + source) * units, units)] = weight[
-                        :, pl.ds((source * dps + owner) * units, units)
-                    ]
-
-    sibling = {"dp": 2 * chip + (1 - core)}
-    ends = (chip + 1 < chips, chip >= 1)
-    sides = ({"dp": lax.rem(dp + 2, dps)}, {"dp": lax.rem(dp - 2 + dps, dps)})
+    gathered.begin()
 
     def onward(side, hop, source, owner_chip):
         part_of = block(source[1], 2 * owner_chip + core)
@@ -870,7 +970,7 @@
     sources = [(back, lax.rem(seq - back + seqs, seqs)) for back in range(seqs)]
     for source in sources:
         if source[0] == 0:
-            for own in owns[:3]:
+            for own in owns:
                 own.wait()
         else:
             for third in range(3):
@@ -882,41 +982,182 @@
                 onward(side, 0, source, chip).start()
 
         share(source, chip, core).start()
-    if square:
-        copies[0].wait_recv()
-        copies.append(push(all_ref.at[across, top], all_ref.at[across, top], x_s, x_r, 4, to_along))
-        copies[1].wait_recv()
-        copies.append(push(all_ref.at[along, low], all_ref.at[along, low], x_s, x_r, 5, to_across))
-    cut_columns()
-    for hop in range(chips - 1):
+    gathered.relay()
+
+    def pass_on(hop):
         for source in sources:
             for side in range(2):
                 origin = chip - 1 - hop if side == 0 else chip + 1 + hop
                 there = origin >= 0 if side == 0 else origin < chips
 
                 @pl.when(there)
-                def _(side=side, hop=hop, source=source, origin=origin):
+                def _(side=side, source=source, origin=origin):
                     onward(side, hop, source, origin).wait_recv()
                     share(source, origin, core).start()
 
                 if hop < chips - 2:
 
                     @pl.when(jnp.logical_and(there, ends[side]))
-                    def _(side=side, hop=hop, source=source, origin=origin):
+                    def _(side=side, source=source, origin=origin):
                         onward(side, hop + 1, source, origin).start()
 
-    for swapped in swaps:
-        swapped.wait_send()
-    for at, copy in enumerate(copies):
-        copy.wait_send()
-        if not square or at > 1:
-            copy.wait_recv()
-    owns[3].wait()
+    units = gate_ref.shape[1] // count
+    for at, weight in enumerate((gate_ref, up_ref)):
+        for source in range(seqs):
+            for owner in range(dps):
+                cut_ref[owner, :, pl.ds((at * seqs + source) * units, units)] = weight[
+                    :, pl.ds((source * dps + owner) * units, units)
+                ]
+    pass_on(0)
 
     @pl.loop(1, count)
     def _(step):
         small_copy(step).wait()
 
+    lane, sides_of = halves()
+    per = 128 // part
+
+    def row_of(pick):
+        value = jnp.zeros((1, 128), F32)
+        for unit in range(per):
+            found = pick(unit)
+            found = pltpu.roll(found, unit * part, 1) if unit else found
+            mask = (lane >= unit * part) & (lane < (unit + 1) * part)
+            value = jnp.where(mask, found, value)
+        return value
+
+    for kind in range(4):
+        for chunk in range(width // 128):
+            vec_ref[kind : kind + 1, pl.ds(chunk * 128, 128)] = row_of(
+                lambda unit, kind=kind, chunk=chunk: given_ref[chunk * per + unit, kind : kind + 1]
+            )
+    for chunk in range(3 * group // 128):
+        third, inner = chunk * 128 // group, chunk * 128 % group // part
+        first = third * count + seq * dps + inner
+
+        def pick(unit, first=first):
+            at = first + unit
+            return given_ref[at // 3, pl.ds(4 + lax.rem(at, 3), 1)]
+
+        bias_ref[0:1, pl.ds(chunk * 128, 128)] = row_of(pick)
+    for hop in range(1, chips - 1):
+        pass_on(hop)
+    outs.begin()
+    gathered.end()
+    gain_one, shift_one = vec_ref[0:1, :], vec_ref[1:2, :]
+
+    for source in range(seqs):
+
+        def norm(here, source=source):
+            normed, _ = normalize(x_ref[source, here, :].astype(F32))
+            at = pl.ds(pl.multiple_of(source * rows + here.start, CHUNK), CHUNK)
+            attn_ref[at, :] = (normed * gain_one + shift_one).astype(attn_ref.dtype)
+
+        by_chunks(rows, norm)
+    for owner in range(chips):
+        for source in sources:
+            share(source, owner, 1 - core).wait_recv()
+    tile = min(256, group)
+
+    def product(at):
+        here = pl.ds(pl.multiple_of(at * tile, tile), tile)
+        return here, dot(attn_ref[...], w_ref[:, here]) + bias_ref[0:1, here]
+
+    @pl.loop(0, 2 * group // tile)
+    def _(at):
+        _, value = product(at)
+        for half in range(tile // 128):
+            turned = turn_lanes(value[:, half * 128 : (half + 1) * 128], table_ref, 1.0)
+            here = pl.ds(pl.multiple_of(at * tile + half * 128, 128), 128)
+            qkv_ref[:, here] = turned.astype(qkv_ref.dtype)
+
+    outs.hop(0)
+
+    @pl.loop(2 * group // tile, 3 * group // tile)
+    def _(at):
+        here, value = product(at)
+        qkv_ref[:, here] = value.astype(qkv_ref.dtype)
+
+    for hop in range(1, chips - 1):
+        outs.hop(hop)
+    swap.begin()
+    scale = HEAD_DIM ** (-0.5)
+    size = min(256, length)
+    triangle = lax.broadcasted_iota(jnp.int32, (size, size), 1) <= lax.broadcasted_iota(
+        jnp.int32, (size, size), 0
+    )
+
+    @pl.loop(0, group // 128)
+    def _(at):
+        base = pl.multiple_of(at * 128, 128)
+        for part_at in range(length // size):
+            here = pl.ds(part_at * size, size)
+            seen = (part_at + 1) * size
+            query = qkv_ref[here, pl.ds(base, 128)]
+            key = qkv_ref[pl.ds(0, seen), pl.ds(group + base, 128)]
+            value = qkv_ref[pl.ds(0, seen), pl.ds(2 * group + base, 128)]
+            mixed = []
+            for half in range(2):
+                mine = jnp.where(sides_of[half], query, jnp.zeros_like(query))
+                scores = contract_cols(mine, key) * scale
+                last = jnp.where(triangle, scores[:, part_at * size :], -jnp.inf)
+                if part_at:
+                    scores = jnp.concatenate([scores[:, : part_at * size], last], 1)
+                else:
+                    scores = last
+                largest = jnp.max(scores, axis=1, keepdims=True)
+                exponent = jnp.exp(scores - largest)
+                totals = jnp.sum(exponent, axis=1, keepdims=True)
+                probs = (exponent * (1.0 / totals)).astype(value.dtype)
+                mixed.append(dot(probs, value))
+                lse_ref[here, :] = jnp.where(
+                    lane == 2 * at + half, largest + jnp.log(totals), lse_ref[here, :]
+                )
+            att_ref[here, pl.ds(base, 128)] = jnp.where(sides_of[0], mixed[0], mixed[1]).astype(
+                att_ref.dtype
+            )
+
+    outs.end()
+    step = min(256, width)
+
+    @pl.loop(0, width // step)
+    def _(at):
+        here = pl.ds(pl.multiple_of(at * step, step), step)
+        value = jnp.zeros((length, step), F32)
+        for owner in range(dps):
+            value = value + dot(att_ref[:, pl.ds(owner * part, part)], out_ref[owner, :, here])
+        for source in range(seqs):
+            branch_ref[source, :, here] = value[source * rows : (source + 1) * rows].astype(
+                branch_ref.dtype
+            )
+
+    plane.begin()
+    grads.begin()
+    plane.relay()
+    plane.end()
+    swap.end()
+    gates.begin()
+    gain_two, shift_two = vec_ref[2:3, :], vec_ref[3:4, :]
+
+    def one(here):
+        resid = in_ref[here, :].astype(F32) + plane.total(here)
+        resid_ref[here, :] = resid
+        normed, _ = normalize(resid)
+        own_ref[here, :] = (normed * gain_two + shift_two).astype(own_ref.dtype)
+
+    by_chunks(rows, one)
+    moved.begin()
+    for hop in range(chips - 1):
+        grads.hop(hop)
+        if hop == min(1, chips - 2):
+            gates.relay()
+        moved.hop(hop)
+    grads.end()
+    moved.end()
+    gates.end()
+
+    for swapped in swaps:
+        swapped.wait_send()
     for hop in range(chips - 1):
         for source in sources:
             for side in range(2):
@@ -930,83 +1171,73 @@
     for owner in range(chips):
         for source in sources:
             share(source, owner, core).wait_send()
-            share(source, owner, 1 - core).wait_recv()
-
-
-def open_all(ways, qkv_weight, rows_in, small, gate_weight, up_weight):
+
+
+def front_all(ways, qkv_weight, inputs, small, gate, up, out_weight, grad_out, table, tag):
     seqs, dps = ways
     chips, count = dps // 2, seqs * dps
-    part, group = qkv_weight.shape[0], qkv_weight.shape[1] // (3 * seqs)
-    slots = 6 if seqs == 4 else seqs - 1
+    part, width = out_weight.shape
+    rows = inputs.shape[0]
+    length, group, cols = rows * seqs, width // seqs, 2 * gate.shape[1] // dps
     dma = pltpu.SemaphoreType.DMA
+    vmem, anywhere = (pl.BlockSpec(memory_space=space) for space in (pltpu.VMEM, pl.ANY))
+
+    def made(dtype, *shape):
+        return jax.ShapeDtypeStruct(shape, dtype)
+
     return pl.pallas_call(
-        functools.partial(opening, ways),
+        functools.partial(front, ways),
         out_shape=(
-            jax.ShapeDtypeStruct((part * count, 3 * group), BF16),
-            jax.ShapeDtypeStruct((seqs,) + rows_in.shape, BF16),
-            jax.ShapeDtypeStruct((count,) + small.shape, BF16),
-            jax.ShapeDtypeStruct((dps, part, 2 * gate_weight.shape[1] // dps), BF16),
+            made(BF16, width, 3 * group),
+            made(BF16, length, width),
+            made(BF16, length, 3 * group),
+            made(BF16, length, group),
+            made(F32, length, 128),
+            made(BF16, dps, part, width),
+            made(F32, 8, width),
+            made(F32, rows, width),
+            made(BF16, dps, rows, width),
+            made(BF16, dps, rows, width),
+            made(BF16, seqs, dps, part, cols),
         ),
-        in_specs=[pl.BlockSpec(memory_space=pltpu.VMEM)] * 5,
-        out_specs=(
-            pl.BlockSpec(memory_space=pl.ANY),
-            pl.BlockSpec(memory_space=pl.ANY),
-            pl.BlockSpec(memory_space=pltpu.VMEM),
-            pl.BlockSpec(memory_space=pltpu.VMEM),
-        ),
+        in_specs=[vmem] * 8,
+        out_specs=(vmem,) * 8 + (anywhere,) * 3,
         scratch_shapes=[
+            pltpu.VMEM((seqs, rows, width), BF16),
+            pltpu.VMEM((count, 8, 128), F32),
+            pltpu.VMEM((8, 3 * group), F32),
+            pltpu.VMEM((dps, part, cols), BF16),
+            pltpu.VMEM((dps, part, cols), BF16),
+            pltpu.VMEM((seqs, rows, width), BF16),
+            pltpu.VMEM((rows, width), BF16),
+        ]
+        + PlaneGather.scratch(seqs)
+        + LineGather.scratch(dps)
+        + SwapDp.scratch(dps)
+        + Plane.scratch(seqs, rows, width, BF16)
+        + LineGather.scratch(dps)
+        + LineGather.scratch(dps)
+        + PlaneGather.scratch(seqs)
+        + [
             dma((3 * (seqs - 1),)),
             dma((3 * (seqs - 1),)),
             dma((2, chips - 1, seqs)),
             dma((2, chips - 1, seqs)),
             dma((chips, seqs)),
             dma((chips, seqs)),
-            dma((slots,)),
-            dma((slots,)),
             dma((count - 1,)),
             dma((count - 1,)),
-            dma((4,)),
+            dma((3,)),
         ],
-        cost_estimate=lasting(75),
-        compiler_params=pltpu.CompilerParams(collective_id=0, has_side_effects=True),
-    )(qkv_weight, rows_in, small, gate_weight, up_weight)
+        cost_estimate=lasting(180),
+        compiler_params=pltpu.CompilerParams(
+            collective_id=tag, has_side_effects=True, vmem_limit_bytes=60 * 2**20
+        ),
+    )(qkv_weight, inputs, small, gate, up, out_weight, grad_out, table)
 
 
 def after(value, *earlier):
     return lax.optimization_barrier((value,) + earlier)[0]
-
-
-def attention_forward(queries, keys, values):
-    length = queries.shape[0]
-    scale = HEAD_DIM ** (-0.5)
-    index = jnp.arange(length, dtype=jnp.int32)
-    allowed = index[None, :] <= index[:, None]
-    scores = jnp.einsum("qhd,khd->hqk", queries, keys, preferred_element_type=F32) * scale
-    scores = jnp.where(allowed[None], scores, -jnp.inf)
-    largest = jnp.max(scores, axis=-1, keepdims=True)
-    exponent = jnp.exp(scores - largest)
-    totals = jnp.sum(exponent, axis=-1, keepdims=True)
-    probs = exponent / totals
-    mixed = jnp.einsum("hqk,khd->qhd", probs.astype(BF16), values, preferred_element_type=F32)
-    return mixed.astype(BF16), (largest + jnp.log(totals))
-
-
-def attention_backward(queries, keys, values, log_total, grad):
-    length = queries.shape[0]
-    scale = HEAD_DIM ** (-0.5)
-    index = jnp.arange(length, dtype=jnp.int32)
-    allowed = index[None, :] <= index[:, None]
-    scores = jnp.einsum("qhd,khd->hqk", queries, keys, preferred_element_type=F32) * scale
-    scores = jnp.where(allowed[None], scores, -jnp.inf)
-    probs = jnp.exp(scores - log_total)
-    values_grad = jnp.einsum("hqk,qhd->khd", probs.astype(BF16), grad, preferred_element_type=F32)
-    probs_grad = jnp.einsum("qhd,khd->hqk", grad, values, preferred_element_type=F32)
-    scores_grad = (
-        probs * (probs_grad - jnp.sum(probs * probs_grad, axis=-1, keepdims=True))
-    ).astype(BF16)
-    query_grad = jnp.einsum("hqk,khd->qhd", scores_grad, keys, preferred_element_type=F32) * scale
-    keys_grad = jnp.einsum("hqk,qhd->khd", scores_grad, queries, preferred_element_type=F32) * scale
-    return query_grad.astype(BF16), keys_grad.astype(BF16), values_grad.astype(BF16)
 
 
 def shards(
@@ -1031,51 +1262,44 @@
     part = width // (seqs * dps)
     units = down_weight.shape[0]
     group = width // seqs
-    heads = group // HEAD_DIM
     me_seq = lax.axis_index("seq")
     grad_out = out_cotangent[0]
 
-    small = jnp.concatenate([first_gain, first_shift, second_gain, second_shift, qkv_bias])
-    total = small.shape[0]
-    padded = -(-total // 2048) * 2048
-    small = jnp.pad(small, (0, padded - total)).reshape(padded // 128, 128)
-    qkv_full, inputs_all, small, gate_cut = open_all(
-        ways, qkv_weight, inputs[0], small, gate_weight, up_weight
+    small = [item[None] for item in (first_gain, first_shift, second_gain, second_shift)]
+    small = jnp.concatenate(small + [qkv_bias.reshape(3, part)]).astype(F32)
+    small = jnp.pad(small, ((0, 1), (0, 128 - part)))
+    table = tables(length)
+    down_full = gather(down_weight, "seq")
+    (
+        qkv_full,
+        attn_all,
+        qkv,
+        attended,
+        log_total,
+        out_full,
+        vectors,
+        residual,
+        mlp_all,
+        grad_all,
+        gate_up,
+    ) = front_all(
+        ways,
+        qkv_weight,
+        inputs[0],
+        small,
+        gate_weight,
+        up_weight,
+        out_weight,
+        grad_out,
+        table,
+        0,
     )
-    small = small.reshape(seqs * dps, padded)[:, :total].astype(F32)
-    gain_one = small[:, :part].reshape(-1)
-    shift_one = small[:, part : 2 * part].reshape(-1)
-    gain_two = small[:, 2 * part : 3 * part].reshape(-1)
-    shift_two = small[:, 3 * part : 4 * part].reshape(-1)
-    bias = small[:, 4 * part :].reshape(3, seqs, group)
-    bias = lax.dynamic_index_in_dim(bias, me_seq, 1, keepdims=False).reshape(3 * group)
-
-    down_full = gather(down_weight, "seq")
-    out_full = gather(out_weight, "dp")
-
-    gate_cut = gate_cut.reshape(dps * part, 2 * seqs * units)
-    moved = move_blocks(gate_cut, "dp", dps)
+    out_full = out_full.reshape(group, width)
+    gain_one, gain_two = vectors[0:1], vectors[2:3]
+    mlp_all = mlp_all.reshape(dps * rows, width)
+    grad_all = grad_all.reshape(dps * rows, width)
+    gate_up = gate_up.reshape(width, 2 * seqs * units)
     wide = seqs * units
-
-    normed_all, _ = normalize(inputs_all.reshape(length, width).astype(F32))
-    attn_all = (normed_all * gain_one + shift_one).astype(BF16)
-    projected = dot(attn_all, qkv_full) + bias
-    cosine, sine = tables(jnp.arange(length, dtype=jnp.int32).astype(F32))
-
-    def to_heads(flat):
-        return flat.reshape(length, heads, HEAD_DIM)
-
-    queries = rotate(to_heads(projected[:, :group]), cosine, sine).astype(BF16)
-    keys = rotate(to_heads(projected[:, group : 2 * group]), cosine, sine).astype(BF16)
-    values = to_heads(projected[:, 2 * group :]).astype(BF16)
-    attended, log_total = attention_forward(queries, keys, values)
-    attended = attended.reshape(length, group)
-    moved, attended = lax.optimization_barrier((moved, attended))
-    gate_cut = place_blocks(moved, "dp")
-    branch = dot(attended, out_full).astype(BF16)
-    residual, mlp_all, grad_all, gate_up = middle_all(
-        ways, branch, inputs[0], gain_two[None], shift_two[None], grad_out, gate_cut, 1
-    )
 
     both = dot(mlp_all, gate_up)
     gate_value = both[:, :wide]
@@ -1096,27 +1320,26 @@
     down_rows = contract_rows(hidden, grad_all).astype(BF16)
     mlp_part = after(mlp_part, both_rows, down_rows)
     residual_grad, branch_all, sums, layer_out, both_rows = turn_all(
-        ways, mlp_part, residual, gain_two[None], grad_out, out_part, both_rows, 2
+        ways, mlp_part, residual, gain_two, grad_out, out_part, both_rows, 2
     )
     down_rows = after(down_rows, residual_grad)
     down_shard = scatter_sum(down_rows, "seq").astype(F32)
-    both_rows = swap(both_rows, "dp", 0, 0)
-    both_rows = both_rows.reshape(dps, part, 2 * seqs * units)
-
-    attended_grad = contract_cols(branch_all, out_full).astype(BF16)
-    out_rows = contract_rows(attended, after(branch_all, attended_grad)).astype(BF16)
+
+    attn_part, qkv_rows, bias_term, out_rows, both_rows = reverse_all(
+        ways,
+        branch_all,
+        out_full,
+        qkv,
+        log_total.T,
+        table,
+        qkv_full,
+        attn_all,
+        attended,
+        both_rows.reshape(dps, part, 2 * seqs * units),
+        5,
+    )
     out_shard = scatter_sum(out_rows, "dp").astype(F32)
-    query_grad, keys_grad, values_grad = attention_backward(
-        queries, keys, values, log_total, to_heads(attended_grad)
-    )
-    query_plain = rotate(query_grad.astype(F32), cosine, -sine).astype(BF16)
-    keys_plain = rotate(keys_grad.astype(F32), cosine, -sine).astype(BF16)
-    projected_grad = jnp.concatenate(
-        [item.reshape(length, group) for item in (query_plain, keys_plain, values_grad)], 1
-    )
-    attn_part = contract_cols(projected_grad, qkv_full).astype(BF16)
-    qkv_rows = contract_rows(attn_all, projected_grad).astype(BF16)
-    bias_term = jnp.sum(projected_grad.astype(F32), axis=0).reshape(3, 1, group)
+    bias_term = bias_term[0].reshape(3, 1, group)
     here = (jnp.arange(seqs, dtype=jnp.int32) == me_seq).astype(F32)[None, :, None]
     bias_term = jnp.pad((bias_term * here).reshape(3, width), ((4, 1), (0, 0)))
     sums = sums + bias_term
@@ -1126,7 +1349,7 @@
         attn_part,
         sums,
         inputs[0],
-        gain_one[None],
+        gain_one,
         residual_grad,
         both_rows,
         3,

time: 609 us -> 527 us (0.87)
  the two profiles are of different devices: /device:TPU:0 before, /device:TPU:12 now
where the time goes in v5:
time: 527 us; the launch traced here: 519 us
  Pallas kernels  430 us (82%)
  matrix products  49.5 us (9%)
  local copies, waits for them, and re-layouts  15.5 us (3%)
  between operations  14.4 us (3%)
  other arithmetic  7.65 us (1%)
    pallas_call x1, Pallas kernels, front_all(): pl.pallas_call(functools.partial(front, ways), out_shape=(made(BF16, widt...  182 us
    pallas_call x1, Pallas kernels, close_all(): pl.pallas_call(functools.partial(closing, ways), out_shape=(jax.ShapeDtyp...  103 us
    pallas_call x1, Pallas kernels, turn_all(): pl.pallas_call(functools.partial(turning, ways), out_shape=(jax.ShapeDtyp...  103 us
    pallas_call x1, Pallas kernels, reverse_all(): pl.pallas_call(functools.partial(reversing, ways), out_shape=(jax.ShapeDt...  41.8 us
    dot_general x2, matrix products, contract_cols(): lax.dot_general(left, right, (((1,), (1,)), ((), ())), preferred_element_...  17.3 us
    dot_general x2, matrix products, dot(): return jnp.dot(left, right, preferred_element_type=F32)  16.7 us
    dot_general x2, matrix products, contract_rows(): lax.dot_general(left, right, (((0,), (0,)), ((), ())), preferred_element_...  15.5 us
  transfers between devices with their start and end apart: 3, of which 0 were waited for; matrix products, arithmetic and copies ran while one was open for 5% of the time, Pallas kernels for 55%

profile of v5, /device:TPU:12, one launch (start us, length us, event | category | flops | bytes accessed | tf_op | source)
XLA Modules:
  0.0 518.5 jit_solution(91820986540423873)
XLA Ops:
  7.2 0.0 all-gather.2.cloned.1.call-start
  7.2 0.7 all-gather.2.cloned.1.call-update
  7.9 0.0 reduce-scatter.3.cloned.1.call-start
  8.0 0.7 reshape.261
  8.7 0.7 concatenate.6
  9.5 0.6 pad_convert_fusion.small_ref
  10.1 1.0 fusion.4
  11.1 0.9 pad_maximum_fusion.1.table_ref
  12.0 182.1 %shard_map.211 = (bf16[2048,1536]{1,0:T(8,128)(2,1)}, bf16[512,2048]{1,0:T(8,128)(2,1)}, bf16[512,1536]{1,0:T(8,128)(2,1)}, bf16[512,512]{1,0:T(8,128)(2,1)}, f3...) custom-call(bf16[64,6144]{1,0:T(8,128)(2,1)} %qkv_weight_ref.1, ...), custom_call_target="tpu_custom_call" | custom-call | bytes 540000000 | tf_op jit(solution)/shard_map/pallas_call | solution.py:1188
  194.1 1.8 copy.26
  195.9 1.5 fusion.13
  197.4 11.4 %fusion.14 = f32[1024,1408]{0,1:T(8,128)} fusion(bf16[1024,2048]{1,0:T(8,128)(2,1)} %bitcast.68, bf16[2048,1408]{1,0:T(8,128)(2,1)} %bitcast.66), kind=kOutput, calls=%fused_computation.43 | convolution fusion | flops 5905580032 | bytes 15728640 | tf_op jit(solution)/shard_map/dot_general | solution.py:31
  208.8 0.0 all-gather.2.cloned.1.call-done
  208.9 0.0 copy-start.6
  208.9 9.0 %multiply_convert_fusion.2 = (bf16[1024,704]{0,1:T(8,128)(2,1)S(1)}, bf16[1024,704]{0,1:T(8,128)(2,1)S(1)}, bf16[1024,704]{0,1:T(8,128)(2,1)S(1)}) fusion(f32[1024,1408]{0,1:T(8,128)} %fusion.14, bf16[1024,2048]{1,0:T(8,128)(2,1)} %bitcast.70, bf16[704,2048]{1,0:T(8,128)(2,1)} %all-gather.2.cloned.1.call-done), kind=kOutput, calls=%fused_computation.7 | convolution fusion | flops 2963603456 | bytes 17170432 | tf_op jit(solution)/shard_map/dot_general | solution.py:39
  217.8 0.0 copy-start.9
  217.9 0.0 copy-done.6
  217.9 8.3 %convolution_convert_fusion.2 = bf16[1024,2048]{1,0:T(8,128)(2,1)} fusion(bf16[2048,1408]{1,0:T(8,128)(2,1)S(1)} %bitcast.67, bf16[1024,704]{0,1:T(8,128)(2,1)S(1)} %get-tuple-element.71, bf16[1024,704]{0,1:T(8,128)(2,1)S(1)} %get-tuple-element.70), kind=kOutput, calls=%fused_computation.2 | convolution fusion | flops 5913444352 | bytes 12845056 | tf_op jit(solution)/shard_map/dot_general | solution.py:39
  226.2 0.0 copy-start.7
  226.2 0.3 pad_maximum_fusion
  226.5 0.0 copy-done.9
  226.5 1.9 copy-done.7
  228.4 4.5 convolution_convert_fusion.3
  232.9 0.0 copy-start.8
  232.9 0.0 copy-start.10
  232.9 11.0 %convolution_convert_fusion = bf16[2048,1408]{1,0:T(8,128)(2,1)} fusion(bf16[1024,2048]{1,0:T(8,128)(2,1)} %bitcast.69, bf16[1024,1408]{0,1:T(8,128)(2,1)S(1)} %pad_maximum_fusion), kind=kOutput, calls=%fused_computation | convolution fusion | flops 5908463616 | bytes 12845056 | tf_op jit(solution)/shard_map/dot_general | solution.py:35
  243.9 0.0 copy-done.8
  243.9 0.0 copy-done.10
  243.9 5.3 %convolution_convert_fusion.1 = bf16[1024,2048]{1,0:T(8,128)(2,1)} fusion(bf16[1024,704]{0,1:T(8,128)(2,1)S(1)} %copy-done.10, bf16[704,2048]{1,0:T(8,128)(2,1)S(1)} %copy-done.8), kind=kOutput, calls=%fused_computation.1 | convolution fusion | flops 2954887168 | bytes 8519680 | tf_op jit(solution)/shard_map/dot_general | solution.py:31
  249.2 103.0 %shard_map.212 = (f32[128,2048]{1,0:T(8,128)}, bf16[4,128,2048]{2,1,0:T(8,128)(2,1)}, f32[8,2048]{1,0:T(8,128)}, bf16[128,2048]{1,0:T(8,128)(2,1)}, bf16[512,1408]{1,0:T(8,128)(2,1)}) custom-call(bf16[8,2,64,2048]{3,2,1,0:T(8,128)(2,1)} %bitcast.47, f32[128,2048]{1,0:T(8,128)} %get-tuple-element.46.resid_ref, f32[1,2048]{1,0:T(1,128)} %get-tuple-element.74.gain_ref, ...), custom_call_target="tpu_custom_call" | custom-call | bytes 255000000 | tf_op jit(solution)/shard_map/pallas_call | solution.py:546
  352.2 41.8 %shard_map.213 = (bf16[512,2048]{1,0:T(8,128)(2,1)}, bf16[2048,1536]{1,0:T(8,128)(2,1)}, f32[8,1536]{1,0:T(8,128)}, bf16[512,2048]{1,0:T(8,128)(2,1)}, bf16[8,64,1408]{2,1,0:T(8,128)(2,1)}) custom-call(bf16[512,2048]{1,0:T(8,128)(2,1)} %bitcast.55, bf16[512,2048]{1,0:T(8,128)(2,1)} %bitcast.54, bf16[512,1536]{1,0:T(8,128)(2,1)} %get-tuple-element.51.qkv_ref, ...), custom_call_target="tpu_custom_call" | custom-call | bytes 135000000 | tf_op jit(solution)/shard_map/pallas_call | solution.py:714
  394.0 0.0 copy-start.5
  394.0 0.0 reduce-scatter.3.cloned.1.call-update
  394.0 0.0 reduce-scatter.5.cloned.1.call-start
  394.1 0.7 reduce-scatter.5.cloned.1.call-update
  394.8 0.1 broadcast_bitcast_fusion.1
  394.9 0.8 slice_reduce_fusion
  395.7 0.0 copy-done.5
  395.8 0.6 pad_add_fusion.sums_ref
  396.4 103.1 %shard_map.214 = (f32[64,6144]{1,0:T(8,128)}, bf16[128,2048]{1,0:T(8,128)(2,1)}, f32[8,2048]{1,0:T(8,128)}, f32[64,5632]{1,0:T(8,128)}, f32[64,5632]{1,0:T(8,128)}) custom-call(bf16[4,8,64,1536]{3,2,1,0:T(8,128)(2,1)} %bitcast.45, bf16[4,128,2048]{2,1,0:T(8,128)(2,1)} %bitcast.49, f32[8,2048]{1,0:T(8,128)} %pad_add_fusion.sums_ref, ...), custom_call_target="tpu_custom_call" | custom-call | bytes 225000000 | tf_op jit(solution)/shard_map/pallas_call | solution.py:817
  499.5 0.0 copy-start.3
  499.5 0.0 copy-start.4
  499.5 0.0 copy-start
  499.5 1.0 slice.37
  500.6 0.6 dynamic_slice.7
  501.2 0.8 constant_dynamic-slice_fusion
  502.0 0.5 slice_bitcast_fusion
  502.5 0.0 reduce-scatter.3.cloned.1.call-done
  502.5 1.8 convert_element_type.70
  504.3 0.0 reduce-scatter.5.cloned.1.call-done
  504.3 2.4 convert_element_type.71
  506.6 0.0 copy-start.2
  506.7 0.0 copy-done.3
  506.7 0.8 copy.35
  507.4 0.0 copy-done.4
  507.4 0.8 copy.36
  508.2 0.0 copy-done
  508.2 0.0 copy-start.1
  508.2 1.1 copy.37
  509.4 0.0 copy-done.2
  509.4 1.1 copy.38
  510.5 0.0 copy-done.1
  510.5 1.1 copy.39
  (11 shorter events, 0.1 us)
Async XLA Ops:
  7.2 201.7 %all-gather.2.cloned.1.call-start = ((), (), s32[]{:S(2)}) async-start(), calls=%async_computation.2 | async-start | bytes 3604480 | tf_op jit(solution)/shard_map/all_gather | solution.py:65
  7.9 494.6 %reduce-scatter.3.cloned.1.call-start = ((), (), s32[]{:S(2)}) async-start(), calls=%async_computation.3 | async-start | bytes 2359296 | tf_op jit(solution)/shard_map/reduce_scatter | solution.py:69
  208.9 9.0 %copy-start.6 = (bf16[4,8,64,1408]{3,2,1,0:T(8,128)(2,1)S(1)}, bf16[4,8,64,1408]{3,2,1,0:T(8,128)(2,1)}, u32[]{:S(2)}) copy-start(bf16[4,8,64,1408]{3,2,1,0:T(8,128)(2,1)} %get-tuple-element.43) | copy-start | bytes 17301508
  217.8 8.6 %copy-start.9 = (bf16[1024,704]{0,1:T(8,128)(2,1)}, bf16[1024,704]{0,1:T(8,128)(2,1)S(1)}, u32[]{:S(2)}) copy-start(bf16[1024,704]{0,1:T(8,128)(2,1)S(1)} %get-tuple-element.72) | copy-start | bytes 4325380
  226.2 2.2 copy-start.7
  232.9 11.0 %copy-start.8 = (bf16[704,2048]{1,0:T(8,128)(2,1)S(1)}, bf16[704,2048]{1,0:T(8,128)(2,1)}, u32[]{:S(2)}) copy-start(bf16[704,2048]{1,0:T(8,128)(2,1)} %all-gather.2.cloned.1.call-done) | copy-start | bytes 8650756
  232.9 11.0 %copy-start.10 = (bf16[1024,704]{0,1:T(8,128)(2,1)S(1)}, bf16[1024,704]{0,1:T(8,128)(2,1)}, u32[]{:S(2)}) copy-start(bf16[1024,704]{0,1:T(8,128)(2,1)} %copy-done.9) | copy-start | bytes 4325380
  394.0 1.8 copy-start.5
  394.0 110.3 %reduce-scatter.5.cloned.1.call-start = ((), (), s32[]{:S(2)}) async-start(), calls=%async_computation.4 | async-start | bytes 3604480 | tf_op jit(solution)/shard_map/reduce_scatter | solution.py:69
  499.5 7.1 %copy-start.3 = (bf16[128,2048]{1,0:T(8,128)(2,1)S(1)}, bf16[128,2048]{1,0:T(8,128)(2,1)}, u32[]{:S(2)}) copy-start(bf16[128,2048]{1,0:T(8,128)(2,1)} %get-tuple-element.48) | copy-start | bytes 1572868
  499.5 7.9 %copy-start.4 = (bf16[128,2048]{1,0:T(8,128)(2,1)S(1)}, bf16[128,2048]{1,0:T(8,128)(2,1)}, u32[]{:S(2)}) copy-start(bf16[128,2048]{1,0:T(8,128)(2,1)} %get-tuple-element.63) | copy-start | bytes 1572868
  499.5 8.7 %copy-start = (f32[64,6144]{1,0:T(8,128)S(1)}, f32[64,6144]{1,0:T(8,128)}, u32[]{:S(2)}) copy-start(f32[64,6144]{1,0:T(8,128)} %get-tuple-element.100) | copy-start | bytes 4718596
  506.6 2.7 copy-start.2
  508.2 2.2 copy-start.1
Sparse Core Ops, SparseCore 0:
  9.8 60.4 all-gather.1
  394.1 39.4 reduce-scatter.2
  436.7 57.5 reduce-scatter.4

commit v6 on v5

--- a/solution.py
+++ b/solution.py
@@ -131,26 +131,32 @@
         self.send, self.recv = send, recv
         self.square = count == 4
 
-    def begin(self):
+    def begin(self, make=None):
         x, got, send, recv = self.x, self.got, self.send, self.recv
+        make = make or (lambda block: None)
+        me = lax.axis_index("seq")
+        self.copies = []
         if not self.square:
-            me = lax.axis_index("seq")
-            targets = [lax.rem(me + step, self.count) for step in range(1, self.count)]
-            self.copies = [
-                push(x.at[target], got.at[at], send, recv, at, {"seq": target})
-                for at, target in enumerate(targets)
-            ]
+            for at, step in enumerate(range(1, self.count)):
+                target = lax.rem(me + step, self.count)
+                make(target)
+                self.copies.append(push(x.at[target], got.at[at], send, recv, at, {"seq": target}))
+            make(me)
             return
         _, across, along, far = corners()
         half = x.shape[1] // 2
         top, low = pl.ds(0, half), pl.ds(half, half)
         to_across, to_along = {"seq": across}, {"seq": along}
+        make(far)
         self.copies = [
             push(x.at[far, top], self.pair.at[0], send, recv, 0, to_across),
             push(x.at[far, low], self.pair.at[1], send, recv, 1, to_along),
-            push(x.at[across, top], got.at[0, top], send, recv, 2, to_across),
-            push(x.at[along, low], got.at[1, low], send, recv, 3, to_along),
         ]
+        make(across)
+        self.copies.append(push(x.at[across, top], got.at[0, top], send, recv, 2, to_across))
+        make(along)
+        self.copies.append(push(x.at[along, low], got.at[1, low], send, recv, 3, to_along))
+        make(me)
 
     def relay(self):
         if not self.square:
@@ -236,28 +242,30 @@
 
         by_chunks(self.pair.shape[2], one)
 
+    def lead(self):
+        for at in range(self.chips):
+            for piece in range(self.pieces):
+                for side in range(2):
+                    owner = self.chips - 1 - at if side == 0 else at
+                    passing = self.chip < owner if side == 0 else self.chip > owner
+
+                    @pl.when(jnp.logical_and(passing, jnp.logical_not(self.ends[1 - side])))
+                    def _(side=side, owner=owner, piece=piece):
+                        self.share(owner, self.core, piece).wait_recv()
+                        self.add(owner, piece, None)
+                        self.onward(side, owner, piece).start()
+
     def step(self, at):
         for piece in range(self.pieces):
             for side in range(2):
                 owner = self.chips - 1 - at if side == 0 else at
                 passing = self.chip < owner if side == 0 else self.chip > owner
-                fed = jnp.logical_and(passing, self.ends[1 - side])
-
-                @pl.when(passing)
-                def _(owner=owner, piece=piece):
+
+                @pl.when(jnp.logical_and(passing, self.ends[1 - side]))
+                def _(side=side, owner=owner, piece=piece):
                     self.share(owner, self.core, piece).wait_recv()
-
-                @pl.when(fed)
-                def _(side=side, owner=owner, piece=piece):
                     self.onward(side, owner, piece).wait_recv()
                     self.add(owner, piece, side)
-
-                @pl.when(jnp.logical_and(passing, jnp.logical_not(fed)))
-                def _(owner=owner, piece=piece):
-                    self.add(owner, piece, None)
-
-                @pl.when(passing)
-                def _(side=side, owner=owner, piece=piece):
                     self.onward(side, owner, piece).start()
 
     def end(self):
@@ -483,24 +491,81 @@
     return seq_peers, dp_peers
 
 
-def turning(ways, part_ref, resid_ref, gain_ref, grad_ref, out_ref, both_ref, *rest):
+def turning(ways, inside, part_ref, resid_ref, gain_ref, grad_ref, *rest):
     seqs, dps = ways
-    total_ref, all_ref, sums_ref, layer_ref, rows_ref = rest[:5]
-    line = LineSum(dps, lambda owner: part_ref.at[owner], *rest[5:11])
-    own = rest[11]
-    gathered = PlaneGather(seqs, own, all_ref, *rest[12:15])
-    outs = LineSum(dps, lambda owner: out_ref.at[owner], *rest[15:21])
-    both = Plane(seqs, both_ref, *rest[21:25])
+    rest = list(rest)
+
+    def take(size):
+        taken = rest[:size]
+        del rest[:size]
+        return taken
+
+    if inside:
+        hidden_ref, down_ref, mlp_ref, back_ref, grads_ref = take(5)
+    else:
+        out_ref, both_ref = take(2)
+    total_ref, all_ref, sums_ref, layer_ref, rows_ref = take(5)
+    if inside:
+        (down_rows_ref,) = take(1)
+    line = LineSum(dps, lambda owner: part_ref.at[owner], *take(6))
+    (own,) = take(1)
+    gathered = PlaneGather(seqs, own, all_ref, *take(3))
+    outs_refs, both_refs = take(6), take(4)
+    if inside:
+        out_ref, both_ref = take(2)
+    outs = LineSum(dps, lambda owner: out_ref.at[owner], *outs_refs)
+    both = Plane(seqs, both_ref, *both_refs)
     chips = dps // 2
+    group, wide = both_ref.shape[1], resid_ref.shape[1]
+    tile = min(256, group)
+
+    def both_rows(source):
+        @pl.loop(0, group // tile)
+        def _(at):
+            columns = pl.ds(pl.multiple_of(source * group + at * tile, tile), tile)
+            here = pl.ds(pl.multiple_of(at * tile, tile), tile)
+            both_ref[source, here, :] = contract_rows(mlp_ref[:, columns], back_ref[...]).astype(
+                both_ref.dtype
+            )
+
+    def out_part():
+        step = min(256, wide)
+
+        @pl.loop(0, wide // step)
+        def _(at):
+            here = pl.ds(pl.multiple_of(at * step, step), step)
+            value = dot(hidden_ref[...], down_ref[:, here]).astype(out_ref.dtype)
+            out_ref[:, :, :, here] = value.reshape(out_ref.shape[:3] + (step,))
+
+    def down_rows():
+        count = down_rows_ref.shape[0]
+        for first in range(0, count, 256):
+            here = slice(first, min(first + 256, count))
+            down_rows_ref[here, :] = contract_rows(hidden_ref[:, here], grads_ref[...]).astype(
+                down_rows_ref.dtype
+            )
+
     meet_cross(ways)
     line.begin()
-    both.begin()
-    line.step(0)
+    line.lead()
+    served = []
+
+    def make(source):
+        if inside:
+            both_rows(source)
+        if len(served) == 1:
+            line.step(0)
+        served.append(source)
+
+    both.begin(make)
+    if inside:
+        out_part()
+    outs.begin()
+    line.step(1)
     both.relay()
-    outs.begin()
-    for at in range(1, chips):
+    for at in range(2, chips):
         line.step(at)
-    outs.step(0)
+    outs.lead()
     line.end()
     sums_ref[...] = jnp.zeros(sums_ref.shape, F32)
     gain = gain_ref[...]
@@ -516,11 +581,12 @@
 
     by_pieces(resid_ref.shape[0], one)
     gathered.begin()
-    if chips > 1:
-        outs.step(1)
+    outs.step(0)
     gathered.relay()
-    for at in range(2, chips):
+    for at in range(1, chips):
         outs.step(at)
+    if inside:
+        down_rows()
     both.end()
 
     def two(here):
@@ -538,40 +604,54 @@
     outs.drain()
 
 
-def turn_all(ways, part, resid, gain, grad_out, out_part, both, tag):
+def turn_all(ways, part, resid, gain, grad_out, hidden, down_full, mlp_all, both_grad, grad_all, tag):
     seqs, dps = ways
     rows, wide = resid.shape
-    cut = (both.shape[0] // seqs, both.shape[1])
+    cut = (wide // seqs, both_grad.shape[1])
+    inside = dps * rows <= 1024
+    pieces = (dps, PIECES, rows // PIECES, wide)
     vmem, anywhere = (pl.BlockSpec(memory_space=space) for space in (pltpu.VMEM, pl.ANY))
-    total, gathered, sums, layer, both = pl.pallas_call(
-        functools.partial(turning, ways),
-        out_shape=(
-            jax.ShapeDtypeStruct((rows, wide), F32),
-            jax.ShapeDtypeStruct((seqs, rows, wide), BF16),
-            jax.ShapeDtypeStruct((8, wide), F32),
-            jax.ShapeDtypeStruct((rows, wide), BF16),
-            jax.ShapeDtypeStruct(cut, BF16),
-        ),
-        in_specs=[vmem] * 6,
-        out_specs=(vmem, anywhere, vmem, vmem, vmem),
-        scratch_shapes=LineSum.scratch(dps, (PIECES, rows // PIECES, wide), BF16)
+    operands = [part.reshape(pieces), resid, gain, grad_out]
+    made = [
+        jax.ShapeDtypeStruct((rows, wide), F32),
+        jax.ShapeDtypeStruct((seqs, rows, wide), BF16),
+        jax.ShapeDtypeStruct((8, wide), F32),
+        jax.ShapeDtypeStruct((rows, wide), BF16),
+        jax.ShapeDtypeStruct(cut, BF16),
+    ]
+    places = [vmem, anywhere, vmem, vmem, vmem]
+    scratch = (
+        LineSum.scratch(dps, pieces[1:], BF16)
         + [pltpu.VMEM((rows, wide), BF16)]
         + PlaneGather.scratch(seqs)
-        + LineSum.scratch(dps, (PIECES, rows // PIECES, wide), BF16)
-        + Plane.scratch(seqs, cut[0], cut[1], BF16),
+        + LineSum.scratch(dps, pieces[1:], BF16)
+        + Plane.scratch(seqs, cut[0], cut[1], BF16)
+    )
+    if inside:
+        operands += [hidden, down_full, mlp_all, both_grad, grad_all]
+        made.append(jax.ShapeDtypeStruct((hidden.shape[1], wide), BF16))
+        places.append(vmem)
+        scratch += [pltpu.VMEM(pieces, BF16), pltpu.VMEM((seqs,) + cut, BF16)]
+    else:
+        out_part = dot(hidden, down_full).astype(BF16)
+        both = contract_rows(mlp_all, both_grad).astype(BF16)
+        down_rows = contract_rows(hidden, grad_all).astype(BF16)
+        operands += [out_part.reshape(pieces), both.reshape((seqs,) + cut)]
+    results = pl.pallas_call(
+        functools.partial(turning, ways, inside),
+        out_shape=tuple(made),
+        in_specs=[vmem] * len(operands),
+        out_specs=tuple(places),
+        scratch_shapes=scratch,
         cost_estimate=lasting(85),
         compiler_params=pltpu.CompilerParams(
-            collective_id=tag, has_side_effects=True, vmem_limit_bytes=60 * 2**20
+            collective_id=tag, has_side_effects=True, vmem_limit_bytes=63 * 2**20
         ),
-    )(
-        part.reshape(dps, PIECES, rows // PIECES, wide),
-        resid,
-        gain,
-        grad_out,
-        out_part.reshape(dps, PIECES, rows // PIECES, wide),
-        both.reshape((seqs,) + cut),
-    )
-    return total, gathered.reshape(seqs * rows, wide), sums, layer, both
+    )(*operands)
+    total, gathered, sums, layer, both = results[:5]
+    if inside:
+        down_rows = results[5]
+    return total, gathered.reshape(seqs * rows, wide), sums, layer, both, down_rows
 
 
 class SwapDp:
@@ -615,9 +695,11 @@
     pg_ref, grad_ref = rest[8:10]
     dp = lax.axis_index("dp")
     meet([{"dp": lax.rem(dp + step, dps)} for step in range(1, dps)])
-    swap.begin()
     length, wide = grads_ref.shape
     group = out_ref.shape[0]
+    share = outs_ref.shape[2]
+    step = min(256, wide)
+    swap.begin()
     scale = HEAD_DIM ** (-0.5)
     size = min(256, length)
     tile = min(256, group)
@@ -691,8 +773,6 @@
         here = pl.ds(pl.multiple_of(at * CHUNK, CHUNK), CHUNK)
         bias_ref[0:1, :] += jnp.sum(pg_ref[here, :].astype(F32), axis=0, keepdims=True)
 
-    step = min(256, wide)
-
     @pl.loop(0, wide // step)
     def _(at):
         columns = pl.ds(pl.multiple_of(at * step, step), step)
@@ -700,9 +780,12 @@
         rows_ref[columns, :] = contract_rows(attn_ref[:, columns], pg_ref[...]).astype(
             rows_ref.dtype
         )
-        outs_ref[:, columns] = contract_rows(att_ref[...], grads_ref[:, columns]).astype(
-            outs_ref.dtype
-        )
+
+    @pl.loop(0, wide // step)
+    def _(at):
+        columns = pl.ds(pl.multiple_of(at * step, step), step)
+        value = contract_rows(att_ref[...], grads_ref[:, columns]).astype(outs_ref.dtype)
+        outs_ref[:, 0, :, columns] = value.reshape(dps, share, step)
 
     swap.end()
 
@@ -717,7 +800,7 @@
             jax.ShapeDtypeStruct((length, wide), BF16),
             jax.ShapeDtypeStruct((wide, 3 * group), BF16),
             jax.ShapeDtypeStruct((8, 3 * group), F32),
-            jax.ShapeDtypeStruct((group, wide), BF16),
+            jax.ShapeDtypeStruct((ways[1], 1, group // ways[1], wide), BF16),
             jax.ShapeDtypeStruct(both.shape, BF16),
         ),
         in_specs=[vmem] * 9,
@@ -731,17 +814,22 @@
     )(grads, out_full, qkv, lse, table, qkv_full, attn_all, attended, both)
 
 
-def closing(ways, w_ref, g_ref, sums_ref, x_ref, gain_ref, resid_ref, both_ref, *rest):
+def closing(ways, w_ref, g_ref, sums_ref, x_ref, gain_ref, resid_ref, both_ref, o_ref, *rest):
     seqs, dps = ways
-    qkv_ref, grad_ref, tiny_ref, gate_ref, up_ref = rest[:5]
+    qkv_ref, grad_ref, tiny_ref, gate_ref, up_ref, shard_ref = rest[:6]
+    rest = rest[1:]
     plane = Plane(seqs, g_ref, *rest[5:9])
     line = LineSum(dps, lambda owner: w_ref.at[:, owner], *rest[9:15])
     landed, mine, near, far, part_sum = rest[15:20]
-    swap_s, swap_r, near_s, near_r, far_s, far_r = rest[20:]
+    swap_s, swap_r, near_s, near_r, far_s, far_r = rest[20:26]
+    outs = LineSum(dps, lambda owner: o_ref.at[owner], *rest[26:32])
     seq, dp = lax.axis_index("seq"), lax.axis_index("dp")
     seq_peers, dp_peers = meet_cross(ways)
     line.begin()
     plane.begin()
+    line.lead()
+    outs.begin()
+    outs.lead()
     plane.relay()
     line.step(0)
     plane.end()
@@ -793,6 +881,8 @@
         for at, peer in enumerate(seq_peers)
     ]
     landed[seq] = mine[seq]
+    for at in range(dps // 2):
+        outs.step(at)
     for copy in fars:
         copy.wait()
     tiny_ref[...] = jnp.sum(far[...], axis=0)
@@ -804,10 +894,17 @@
             qkv_ref[:, pl.ds(third * wide + source * group, group)] = landed[
                 source, :, pl.ds(third * group, group)
             ].astype(F32)
+    outs.end()
+
+    def last(here):
+        shard_ref[here, :] = outs.total(0, here)
+
+    by_chunks(shard_ref.shape[0], last)
     line.drain()
-
-
-def close_all(ways, qkv_rows, attn_part, sums, inputs, gain, resid, both, tag):
+    outs.drain()
+
+
+def close_all(ways, qkv_rows, attn_part, sums, inputs, gain, resid, both, out_rows, tag):
     seqs, dps = ways
     part = qkv_rows.shape[0] // (seqs * dps)
     wide3 = qkv_rows.shape[1]
@@ -822,9 +919,10 @@
             jax.ShapeDtypeStruct(sums.shape, F32),
             jax.ShapeDtypeStruct((part, dps * both.shape[2] // 2), F32),
             jax.ShapeDtypeStruct((part, dps * both.shape[2] // 2), F32),
+            jax.ShapeDtypeStruct((part, wide), F32),
         ),
-        in_specs=[vmem] * 7,
-        out_specs=(vmem,) * 5,
+        in_specs=[vmem] * 8,
+        out_specs=(vmem,) * 6,
         scratch_shapes=Plane.scratch(seqs, rows, wide, BF16)
         + LineSum.scratch(dps, (seqs, part, wide3), BF16)
         + [
@@ -839,7 +937,8 @@
             dma((seqs - 1,)),
             dma((dps - 1,)),
             dma((dps - 1,)),
-        ],
+        ]
+        + LineSum.scratch(dps, out_rows.shape[1:], BF16),
         cost_estimate=lasting(75),
         compiler_params=pltpu.CompilerParams(collective_id=tag, has_side_effects=True),
     )(
@@ -850,6 +949,7 @@
         gain,
         resid,
         both,
+        out_rows,
     )
 
 
@@ -1236,10 +1336,6 @@
     )(qkv_weight, inputs, small, gate, up, out_weight, grad_out, table)
 
 
-def after(value, *earlier):
-    return lax.optimization_barrier((value,) + earlier)[0]
-
-
 def shards(
     ways,
     inputs,
@@ -1307,7 +1403,6 @@
     sigmoid_gate = jax.nn.sigmoid(gate_value)
     activated = gate_value * sigmoid_gate
     hidden = (activated * up_value).astype(BF16)
-    out_part = dot(hidden, down_full).astype(BF16)
 
     hidden_grad = contract_cols(grad_all, down_full)
     gate_grad = (
@@ -1316,13 +1411,19 @@
     up_grad = (hidden_grad * activated).astype(BF16)
     both_grad = jnp.concatenate([gate_grad, up_grad], 1)
     mlp_part = contract_cols(both_grad, gate_up).astype(BF16)
-    both_rows = contract_rows(mlp_all, after(both_grad, mlp_part)).astype(BF16)
-    down_rows = contract_rows(hidden, grad_all).astype(BF16)
-    mlp_part = after(mlp_part, both_rows, down_rows)
-    residual_grad, branch_all, sums, layer_out, both_rows = turn_all(
-        ways, mlp_part, residual, gain_two, grad_out, out_part, both_rows, 2
+    residual_grad, branch_all, sums, layer_out, both_rows, down_rows = turn_all(
+        ways,
+        mlp_part,
+        residual,
+        gain_two,
+        grad_out,
+        hidden,
+        down_full,
+        mlp_all,
+        both_grad,
+        grad_all,
+        2,
     )
-    down_rows = after(down_rows, residual_grad)
     down_shard = scatter_sum(down_rows, "seq").astype(F32)
 
     attn_part, qkv_rows, bias_term, out_rows, both_rows = reverse_all(
@@ -1338,12 +1439,11 @@
         both_rows.reshape(dps, part, 2 * seqs * units),
         5,
     )
-    out_shard = scatter_sum(out_rows, "dp").astype(F32)
     bias_term = bias_term[0].reshape(3, 1, group)
     here = (jnp.arange(seqs, dtype=jnp.int32) == me_seq).astype(F32)[None, :, None]
     bias_term = jnp.pad((bias_term * here).reshape(3, width), ((4, 1), (0, 0)))
     sums = sums + bias_term
-    qkv_shard, input_grad, tiny, gate_shard, up_shard = close_all(
+    qkv_shard, input_grad, tiny, gate_shard, up_shard, out_shard = close_all(
         ways,
         qkv_rows,
         attn_part,
@@ -1352,6 +1452,7 @@
         gain_one,
         residual_grad,
         both_rows,
+        out_rows,
         3,
     )
     me = me_seq * dps + lax.axis_index("dp")

time: 527 us -> 503 us (0.954)
  the two profiles are of different devices: /device:TPU:12 before, /device:TPU:0 now
where the time goes in v6:
time: 503 us; the launch traced here: 502 us
  Pallas kernels  437 us (87%)
  matrix products  30.2 us (6%)
  between operations  14.2 us (3%)
  local copies, waits for them, and re-layouts  13.5 us (3%)
  other arithmetic  6.48 us (1%)
    pallas_call x1, Pallas kernels, front_all(): pl.pallas_call(functools.partial(front, ways), out_shape=(made(BF16, widt...  188 us
    pallas_call x1, Pallas kernels, close_all(): pl.pallas_call(functools.partial(closing, ways), out_shape=(jax.ShapeDtyp...  113 us
    pallas_call x1, Pallas kernels, turn_all(): pl.pallas_call(functools.partial(turning, ways, inside), out_shape=tuple(...  97.9 us
    pallas_call x1, Pallas kernels, reverse_all(): pl.pallas_call(functools.partial(reversing, ways), out_shape=(jax.ShapeDt...  38.2 us
    dot_general x2, matrix products, contract_cols(): lax.dot_general(left, right, (((1,), (1,)), ((), ())), preferred_element_...  18.6 us
    dot_general x1, matrix products, dot(): return jnp.dot(left, right, preferred_element_type=F32)  11.7 us
  transfers between devices with their start and end apart: 2, of which 0 were waited for; matrix products, arithmetic and copies ran while one was open for 4% of the time, Pallas kernels for 68%

profile of v6, /device:TPU:0, one launch (start us, length us, event | category | flops | bytes accessed | tf_op | source)
XLA Modules:
  0.0 502.3 jit_solution(16690559335956340763)
XLA Ops:
  7.2 0.0 all-gather.2.cloned.1.call-start
  7.2 0.7 all-gather.2.cloned.1.call-update
  7.9 0.0 reduce-scatter.2.cloned.1.call-start
  8.0 0.7 reshape.255
  8.7 0.7 concatenate.6
  9.5 0.6 pad_convert_fusion.small_ref
  10.1 1.0 fusion.4
  11.1 0.9 pad_maximum_fusion.1.table_ref
  12.0 188.1 %shard_map.211 = (bf16[2048,1536]{1,0:T(8,128)(2,1)}, bf16[512,2048]{1,0:T(8,128)(2,1)}, bf16[512,1536]{1,0:T(8,128)(2,1)}, bf16[512,512]{1,0:T(8,128)(2,1)}, f3...) custom-call(bf16[64,6144]{1,0:T(8,128)(2,1)} %qkv_weight_ref.1, ...), custom_call_target="tpu_custom_call" | custom-call | bytes 540000000 | tf_op jit(solution)/shard_map/pallas_call | solution.py:1288
  200.2 1.5 fusion.13
  201.7 11.7 %fusion.14 = f32[1024,1408]{1,0:T(8,128)} fusion(bf16[1024,2048]{1,0:T(8,128)(2,1)} %bitcast.39, bf16[2048,1408]{1,0:T(8,128)(2,1)} %bitcast.61), kind=kOutput, calls=%fused_computation.40 | convolution fusion | flops 5905580032 | bytes 15728640 | tf_op jit(solution)/shard_map/dot_general | solution.py:31
  213.3 0.0 all-gather.2.cloned.1.call-done.rest_1_
  213.3 0.0 slice-start
  213.4 0.0 slice-start.1
  213.4 10.3 %multiply_convert_fusion.2 = (bf16[1024,704]{1,0:T(8,128)(2,1)S(1)}, bf16[1024,704]{1,0:T(8,128)(2,1)S(1)}, bf16[1024,704]{1,0:T(8,128)(2,1)}) fusion(f32[1024,1408]{1,0:T(8,128)} %fusion.14, bf16[1024,2048]{1,0:T(8,128)(2,1)} %bitcast.41, bf16[704,2048]{1,0:T(8,128)(2,1)} %all-gather.2.cloned.1.call-done.rest_1_), kind=kOutput, calls=%fused_computation.3 | convolution fusion | flops 2963603456 | bytes 17170432 | tf_op jit(solution)/shard_map/dot_general | solution.py:39
  223.6 0.9 pad_maximum_fusion.rest_3_
  224.5 0.0 slice-done
  224.5 0.0 slice-done.1
  224.5 0.0 copy-start
  224.5 8.3 %convolution_convert_fusion = bf16[1024,2048]{1,0:T(8,128)(2,1)} fusion(bf16[1024,1408]{1,0:T(8,128)(2,1)S(1)} %pad_maximum_fusion.rest_3_, bf16[2048,1408]{1,0:T(8,128)(2,1)S(1)} %bitcast.64), kind=kOutput, calls=%fused_computation | convolution fusion | flops 5907677184 | bytes 12845056 | tf_op jit(solution)/shard_map/dot_general | solution.py:39
  232.8 0.0 copy-done
  232.8 0.0 copy-start.7
  232.8 97.9 %shard_map.212 = (f32[128,2048]{1,0:T(8,128)}, bf16[4,128,2048]{2,1,0:T(8,128)(2,1)}, f32[8,2048]{1,0:T(8,128)}, bf16[128,2048]{1,0:T(8,128)(2,1)}, bf16[512,140...) custom-call(bf16[8,2,64,2048]{3,2,1,0:T(8,128)(2,1)} %bitcast.43, f32[128,2048]{1,0:T(8,128)} %get-tuple-element.43.resid_ref, ...), custom_call_target="tpu_custom_call" | custom-call | bytes 255000000 | tf_op jit(solution)/shard_map/pallas_call | solution.py:640
  330.8 0.0 reduce-scatter.2.cloned.1.call-update
  330.8 0.0 copy-done.7
  330.8 0.8 copy.26
  331.7 0.1 broadcast_bitcast_fusion.1
  331.7 0.0 copy-start.8
  331.7 38.2 %shard_map.213 = (bf16[512,2048]{1,0:T(8,128)(2,1)}, bf16[2048,1536]{1,0:T(8,128)(2,1)}, f32[8,1536]{1,0:T(8,128)}, bf16[8,1,64,2048]{3,2,1,0:T(8,128)(2,1)}, bf16[8,64,1408]{2,1,0:T(8,128)(2,1)}) custom-call(bf16[512,2048]{1,0:T(8,128)(2,1)} %bitcast.50, bf16[512,2048]{1,0:T(8,128)(2,1)} %bitcast.49, bf16[512,1536]{1,0:T(8,128)(2,1)} %get-tuple-element.48.qkv_ref, ...), custom_call_target="tpu_custom_call" | custom-call | bytes 135000000 | tf_op jit(solution)/shard_map/pallas_call | solution.py:797
  370.0 0.8 slice_reduce_fusion
  370.9 0.0 copy-done.8
  370.9 0.6 pad_add_fusion.sums_ref
  371.5 0.0 copy-start.4
  371.5 112.9 %shard_map.214 = (f32[64,6144]{1,0:T(8,128)}, bf16[128,2048]{1,0:T(8,128)(2,1)}, f32[8,2048]{1,0:T(8,128)}, f32[64,5632]{1,0:T(8,128)}, f32[64,5632]{1,0:T(8,128)}, /*index=5*/f32[64,2048]{1,0:T(8,128)}) custom-call(bf16[4,8,64,1536]{3,2,1,0:T(8,128)(2,1)} %bitcast.38, bf16[4,128,2048]{2,1,0:T(8,128)(2,1)} %bitcast.48, f32[8,2048]{1,0:T(8,128)} %pad_add_fusion.sums_ref, ...), custom_call_target="tpu_custom_call" | custom-call | bytes 225000000 | tf_op jit(solution)/shard_map/pallas_call | solution.py:914
  484.4 0.0 copy-start.6
  484.4 0.0 copy-start.1
  484.4 1.0 slice.37
  485.4 0.6 dynamic_slice.7
  486.1 0.7 constant_dynamic-slice_fusion
  486.8 0.5 slice_bitcast_fusion
  487.4 0.0 reduce-scatter.2.cloned.1.call-done
  487.4 2.4 convert_element_type.55
  489.7 0.0 copy-start.5
  489.7 0.0 copy-done.4
  489.7 0.0 copy-start.3
  489.7 0.8 copy.36
  490.5 0.0 copy-done.6
  490.5 0.8 copy.37
  491.3 0.0 copy-done.1
  491.3 0.0 copy-start.2
  491.3 1.1 copy.38
  492.5 0.0 copy-done.5
  492.5 0.8 copy.39
  493.3 0.0 copy-done.3
  493.3 1.1 copy.40
  494.4 0.0 copy-done.2
  494.4 1.1 copy.41
  (12 shorter events, 0.1 us)
Async XLA Ops:
  7.2 206.2 %all-gather.2.cloned.1.call-start = ((), (), s32[]{:S(2)}) async-start(), calls=%async_computation.1 | async-start | bytes 3604480 | tf_op jit(solution)/shard_map/all_gather | solution.py:65
  7.9 479.4 %reduce-scatter.2.cloned.1.call-start = ((), (), s32[]{:S(2)}) async-start(), calls=%async_computation.2 | async-start | bytes 3604480 | tf_op jit(solution)/shard_map/reduce_scatter | solution.py:69
  213.3 11.2 %slice-start = ((s8[5767168]{0:T(1024)(128)(4,1)}), s8[4194304]{0:T(1024)(128)(4,1)S(1)}, s32[]{:S(2)}) async-start(s8[5767168]{0:T(1024)(128)(4,1)} %bitcast.62), calls=%async_computation.3 | async-start | bytes 8388608
  213.4 11.2 %slice-start.1 = ((s8[5767168]{0:T(1024)(128)(4,1)}), s8[1572864]{0:T(1024)(128)(4,1)S(1)}, s32[]{:S(2)}) async-start(s8[5767168]{0:T(1024)(128)(4,1)} %bitcast.62), calls=%async_computation.4 | async-start | bytes 3145728
  224.5 8.3 %copy-start = (bf16[1024,1408]{1,0:T(8,128)(2,1)}, bf16[1024,1408]{1,0:T(8,128)(2,1)S(1)}, u32[]{:S(2)}) copy-start(bf16[1024,1408]{1,0:T(8,128)(2,1)S(1)} %pad_maximum_fusion.rest_3_) | copy-start | bytes 8650756
  232.8 98.0 %copy-start.7 = (f32[512,128]{1,0:T(8,128)S(1)}, f32[512,128]{1,0:T(8,128)}, u32[]{:S(2)}) copy-start(f32[512,128]{1,0:T(8,128)} %get-tuple-element.49) | copy-start | bytes 786436
  331.7 39.1 %copy-start.8 = (f32[8,2048]{1,0:T(8,128)S(1)}, f32[8,2048]{1,0:T(8,128)}, u32[]{:S(2)}) copy-start(f32[8,2048]{1,0:T(8,128)} %get-tuple-element.56) | copy-start | bytes 196612
  371.5 118.2 %copy-start.4 = (bf16[128,2048]{1,0:T(8,128)(2,1)S(1)}, bf16[128,2048]{1,0:T(8,128)(2,1)}, u32[]{:S(2)}) copy-start(bf16[128,2048]{1,0:T(8,128)(2,1)} %get-tuple-element.45) | copy-start | bytes 1572868
  484.4 6.1 %copy-start.6 = (bf16[128,2048]{1,0:T(8,128)(2,1)S(1)}, bf16[128,2048]{1,0:T(8,128)(2,1)}, u32[]{:S(2)}) copy-start(bf16[128,2048]{1,0:T(8,128)(2,1)} %get-tuple-element.61) | copy-start | bytes 1572868
  484.4 6.9 %copy-start.1 = (f32[64,6144]{1,0:T(8,128)S(1)}, f32[64,6144]{1,0:T(8,128)}, u32[]{:S(2)}) copy-start(f32[64,6144]{1,0:T(8,128)} %get-tuple-element.98) | copy-start | bytes 4718596
  489.7 2.7 copy-start.5
  489.7 3.5 copy-start.3
  491.3 3.0 copy-start.2
Sparse Core Ops, SparseCore 0:
  9.8 63.0 all-gather.1
  330.9 43.3 reduce-scatter.1

commit v7 on v6

--- a/solution.py
+++ b/solution.py
@@ -133,30 +133,47 @@
 
     def begin(self, make=None):
         x, got, send, recv = self.x, self.got, self.send, self.recv
-        make = make or (lambda block: None)
         me = lax.axis_index("seq")
-        self.copies = []
-        if not self.square:
-            for at, step in enumerate(range(1, self.count)):
-                target = lax.rem(me + step, self.count)
-                make(target)
-                self.copies.append(push(x.at[target], got.at[at], send, recv, at, {"seq": target}))
-            make(me)
+        if self.square:
+            _, across, along, far = corners()
+            half = x.shape[1] // 2
+            top, low = pl.ds(0, half), pl.ds(half, half)
+            to_across, to_along = {"seq": across}, {"seq": along}
+            targets = (far, across, along)
+            plan = [
+                (0, x.at[far, top], self.pair.at[0], to_across),
+                (0, x.at[far, low], self.pair.at[1], to_along),
+                (1, x.at[across, top], got.at[0, top], to_across),
+                (2, x.at[along, low], got.at[1, low], to_along),
+            ]
+        else:
+            targets = [lax.rem(me + step, self.count) for step in range(1, self.count)]
+            plan = [
+                (at, x.at[target], got.at[at], {"seq": target})
+                for at, target in enumerate(targets)
+            ]
+        self.copies = [
+            remote(source, target, send.at[at], recv.at[at], peer)
+            for at, (_, source, target, peer) in enumerate(plan)
+        ]
+        if make is None:
+            for copy in self.copies:
+                copy.start()
             return
-        _, across, along, far = corners()
-        half = x.shape[1] // 2
-        top, low = pl.ds(0, half), pl.ds(half, half)
-        to_across, to_along = {"seq": across}, {"seq": along}
-        make(far)
-        self.copies = [
-            push(x.at[far, top], self.pair.at[0], send, recv, 0, to_across),
-            push(x.at[far, low], self.pair.at[1], send, recv, 1, to_along),
-        ]
-        make(across)
-        self.copies.append(push(x.at[across, top], got.at[0, top], send, recv, 2, to_across))
-        make(along)
-        self.copies.append(push(x.at[along, low], got.at[1, low], send, recv, 3, to_along))
-        make(me)
+
+        @pl.loop(0, self.count)
+        def _(at):
+            block = me
+            for step, target in enumerate(targets):
+                block = jnp.where(at == step, target, block)
+            make(at, block)
+            for step in range(len(targets)):
+
+                @pl.when(at == step)
+                def _(step=step):
+                    for copy, item in zip(self.copies, plan):
+                        if item[0] == step:
+                            copy.start()
 
     def relay(self):
         if not self.square:
@@ -469,6 +486,16 @@
         body(pl.ds(pl.multiple_of(at * CHUNK, CHUNK), CHUNK))
 
 
+def fetch(pairs, sems):
+    copies = [
+        pltpu.make_async_copy(source, target, sems.at[at])
+        for at, (source, target) in enumerate(pairs)
+    ]
+    for copy in copies:
+        copy.start()
+    return copies
+
+
 PIECES = 2
 
 
@@ -501,7 +528,7 @@
         return taken
 
     if inside:
-        hidden_ref, down_ref, mlp_ref, back_ref, grads_ref = take(5)
+        far_refs = take(5)
     else:
         out_ref, both_ref = take(2)
     total_ref, all_ref, sums_ref, layer_ref, rows_ref = take(5)
@@ -513,6 +540,11 @@
     outs_refs, both_refs = take(6), take(4)
     if inside:
         out_ref, both_ref = take(2)
+        near_refs = take(5)
+        hidden_ref, down_ref, mlp_ref, back_ref, grads_ref = near_refs
+        (fetch_sem,) = take(1)
+        order = (2, 3, 0, 1, 4)
+        fetched = fetch([(far_refs[at], near_refs[at]) for at in order], fetch_sem)
     outs = LineSum(dps, lambda owner: out_ref.at[owner], *outs_refs)
     both = Plane(seqs, both_ref, *both_refs)
     chips = dps // 2
@@ -539,26 +571,41 @@
 
     def down_rows():
         count = down_rows_ref.shape[0]
-        for first in range(0, count, 256):
-            here = slice(first, min(first + 256, count))
+
+        def one(here):
             down_rows_ref[here, :] = contract_rows(hidden_ref[:, here], grads_ref[...]).astype(
                 down_rows_ref.dtype
             )
 
+        @pl.loop(0, count // 128)
+        def _(at):
+            one(pl.ds(pl.multiple_of(at * 128, 128), 128))
+
+        if count % 128:
+            one(pl.ds(count // 128 * 128, count % 128))
+
     meet_cross(ways)
     line.begin()
     line.lead()
-    served = []
-
-    def make(source):
-        if inside:
-            both_rows(source)
-        if len(served) == 1:
+    if inside:
+        fetched[0].wait()
+        fetched[1].wait()
+
+    def make(at, source):
+        both_rows(source)
+
+        @pl.when(at == 1)
+        def _():
             line.step(0)
-        served.append(source)
-
-    both.begin(make)
+
     if inside:
+        both.begin(make)
+    else:
+        both.begin()
+        line.step(0)
+    if inside:
+        fetched[2].wait()
+        fetched[3].wait()
         out_part()
     outs.begin()
     line.step(1)
@@ -566,6 +613,9 @@
     for at in range(2, chips):
         line.step(at)
     outs.lead()
+    if inside:
+        fetched[4].wait()
+        down_rows()
     line.end()
     sums_ref[...] = jnp.zeros(sums_ref.shape, F32)
     gain = gain_ref[...]
@@ -585,8 +635,6 @@
     gathered.relay()
     for at in range(1, chips):
         outs.step(at)
-    if inside:
-        down_rows()
     both.end()
 
     def two(here):
@@ -628,26 +676,29 @@
         + Plane.scratch(seqs, cut[0], cut[1], BF16)
     )
     if inside:
-        operands += [hidden, down_full, mlp_all, both_grad, grad_all]
+        far = [hidden, down_full, mlp_all, both_grad, grad_all]
         made.append(jax.ShapeDtypeStruct((hidden.shape[1], wide), BF16))
         places.append(vmem)
         scratch += [pltpu.VMEM(pieces, BF16), pltpu.VMEM((seqs,) + cut, BF16)]
+        scratch += [pltpu.VMEM(item.shape, item.dtype) for item in far]
+        scratch += [pltpu.SemaphoreType.DMA((5,))]
     else:
         out_part = dot(hidden, down_full).astype(BF16)
         both = contract_rows(mlp_all, both_grad).astype(BF16)
         down_rows = contract_rows(hidden, grad_all).astype(BF16)
         operands += [out_part.reshape(pieces), both.reshape((seqs,) + cut)]
+        far = []
     results = pl.pallas_call(
         functools.partial(turning, ways, inside),
         out_shape=tuple(made),
-        in_specs=[vmem] * len(operands),
+        in_specs=[vmem] * len(operands) + [anywhere] * len(far),
         out_specs=tuple(places),
         scratch_shapes=scratch,
         cost_estimate=lasting(85),
         compiler_params=pltpu.CompilerParams(
             collective_id=tag, has_side_effects=True, vmem_limit_bytes=63 * 2**20
         ),
-    )(*operands)
+    )(*operands, *far)
     total, gathered, sums, layer, both = results[:5]
     if inside:
         down_rows = results[5]
@@ -687,12 +738,13 @@
 
 
 def reversing(
-    ways, grads_ref, out_ref, qkv_ref, lse_ref, table_ref, w_ref, attn_ref, att_ref, both_ref, *rest
+    ways, grads_ref, out_ref, qkv_ref, lse_ref, table_ref, w_far, attn_far, att_ref, both_ref, *rest
 ):
     dps = ways[1]
     part_ref, rows_ref, bias_ref, outs_ref, swapped_ref = rest[:5]
     swap = SwapDp(dps, both_ref, swapped_ref, *rest[5:8])
-    pg_ref, grad_ref = rest[8:10]
+    pg_ref, grad_ref, w_ref, attn_ref, fetch_sem = rest[8:13]
+    fetched = fetch([(w_far, w_ref), (attn_far, attn_ref)], fetch_sem)
     dp = lax.axis_index("dp")
     meet([{"dp": lax.rem(dp + step, dps)} for step in range(1, dps)])
     length, wide = grads_ref.shape
@@ -773,6 +825,9 @@
         here = pl.ds(pl.multiple_of(at * CHUNK, CHUNK), CHUNK)
         bias_ref[0:1, :] += jnp.sum(pg_ref[here, :].astype(F32), axis=0, keepdims=True)
 
+    for copy in fetched:
+        copy.wait()
+
     @pl.loop(0, wide // step)
     def _(at):
         columns = pl.ds(pl.multiple_of(at * step, step), step)
@@ -803,10 +858,16 @@
             jax.ShapeDtypeStruct((ways[1], 1, group // ways[1], wide), BF16),
             jax.ShapeDtypeStruct(both.shape, BF16),
         ),
-        in_specs=[vmem] * 9,
+        in_specs=[vmem] * 5 + [anywhere] * 2 + [vmem] * 2,
         out_specs=(vmem,) * 4 + (anywhere,),
         scratch_shapes=SwapDp.scratch(ways[1])
-        + [pltpu.VMEM((length, 3 * group), BF16), pltpu.VMEM((length, group), BF16)],
+        + [
+            pltpu.VMEM((length, 3 * group), BF16),
+            pltpu.VMEM((length, group), BF16),
+            pltpu.VMEM(qkv_full.shape, BF16),
+            pltpu.VMEM(attn_all.shape, BF16),
+            pltpu.SemaphoreType.DMA((2,)),
+        ],
         cost_estimate=lasting(45),
         compiler_params=pltpu.CompilerParams(
             collective_id=tag, has_side_effects=True, vmem_limit_bytes=60 * 2**20
@@ -963,12 +1024,12 @@
     out_weight_ref,
     grad_ref,
     table_ref,
-    w_ref,
-    attn_ref,
-    qkv_ref,
-    att_ref,
+    w_far,
+    attn_far,
+    qkv_far,
+    att_far,
     lse_ref,
-    out_ref,
+    out_far,
     vec_ref,
     resid_ref,
     all_ref,
@@ -986,6 +1047,13 @@
         return taken
 
     x_ref, given_ref, bias_ref, cut_ref, swapped_ref, branch_ref, own_ref = take(7)
+    w_ref, attn_ref, qkv_ref, att_ref, out_ref, keep_sem = take(6)
+    kept = []
+
+    def keep(source, target):
+        kept.append(pltpu.make_async_copy(source, target, keep_sem.at[len(kept)]))
+        kept[-1].start()
+
     gathered = PlaneGather(seqs, in_ref, x_ref, *take(3))
     outs = LineGather(dps, out_weight_ref, out_ref, *take(5))
     swap = SwapDp(dps, cut_ref, swapped_ref, *take(3))
@@ -1127,19 +1195,25 @@
         return value
 
     for kind in range(4):
-        for chunk in range(width // 128):
-            vec_ref[kind : kind + 1, pl.ds(chunk * 128, 128)] = row_of(
-                lambda unit, kind=kind, chunk=chunk: given_ref[chunk * per + unit, kind : kind + 1]
+
+        @pl.loop(0, width // 128)
+        def _(chunk, kind=kind):
+            vec_ref[kind : kind + 1, pl.ds(pl.multiple_of(chunk * 128, 128), 128)] = row_of(
+                lambda unit: given_ref[chunk * per + unit, kind : kind + 1]
             )
-    for chunk in range(3 * group // 128):
-        third, inner = chunk * 128 // group, chunk * 128 % group // part
-        first = third * count + seq * dps + inner
-
-        def pick(unit, first=first):
+
+    lot = group // 128
+
+    @pl.loop(0, 3 * lot)
+    def _(chunk):
+        first = chunk // lot * count + seq * dps + lax.rem(chunk, lot) * per
+
+        def pick(unit):
             at = first + unit
             return given_ref[at // 3, pl.ds(4 + lax.rem(at, 3), 1)]
 
-        bias_ref[0:1, pl.ds(chunk * 128, 128)] = row_of(pick)
+        bias_ref[0:1, pl.ds(pl.multiple_of(chunk * 128, 128), 128)] = row_of(pick)
+
     for hop in range(1, chips - 1):
         pass_on(hop)
     outs.begin()
@@ -1157,6 +1231,8 @@
     for owner in range(chips):
         for source in sources:
             share(source, owner, 1 - core).wait_recv()
+    keep(w_ref, w_far)
+    keep(attn_ref, attn_far)
     tile = min(256, group)
 
     def product(at):
@@ -1181,6 +1257,7 @@
     for hop in range(1, chips - 1):
         outs.hop(hop)
     swap.begin()
+    keep(qkv_ref, qkv_far)
     scale = HEAD_DIM ** (-0.5)
     size = min(256, length)
     triangle = lax.broadcasted_iota(jnp.int32, (size, size), 1) <= lax.broadcasted_iota(
@@ -1218,6 +1295,8 @@
             )
 
     outs.end()
+    keep(att_ref, att_far)
+    keep(out_ref, out_far)
     step = min(256, width)
 
     @pl.loop(0, width // step)
@@ -1256,6 +1335,8 @@
     moved.end()
     gates.end()
 
+    for copy in kept:
+        copy.wait()
     for swapped in swaps:
         swapped.wait_send()
     for hop in range(chips - 1):
@@ -1301,7 +1382,7 @@
             made(BF16, seqs, dps, part, cols),
         ),
         in_specs=[vmem] * 8,
-        out_specs=(vmem,) * 8 + (anywhere,) * 3,
+        out_specs=(anywhere,) * 4 + (vmem, anywhere, vmem, vmem) + (anywhere,) * 3,
         scratch_shapes=[
             pltpu.VMEM((seqs, rows, width), BF16),
             pltpu.VMEM((count, 8, 128), F32),
@@ -1310,6 +1391,12 @@
             pltpu.VMEM((dps, part, cols), BF16),
             pltpu.VMEM((seqs, rows, width), BF16),
             pltpu.VMEM((rows, width), BF16),
+            pltpu.VMEM((width, 3 * group), BF16),
+            pltpu.VMEM((length, width), BF16),
+            pltpu.VMEM((length, 3 * group), BF16),
+            pltpu.VMEM((length, group), BF16),
+            pltpu.VMEM((dps, part, width), BF16),
+            dma((5,)),
         ]
         + PlaneGather.scratch(seqs)
         + LineGather.scratch(dps)

time: 503 us -> 492 us (0.978)
  Pallas kernels: 437 us -> 426 us
  transfers between devices with their start and end apart: 2 -> 2, of which waited for: 0 -> 0; matrix products, arithmetic and copies ran while one was open for 4% -> 5% of each run, Pallas kernels for 68% -> 68%
where the time goes in v7:
time: 492 us; the launch traced here: 491 us
  Pallas kernels  426 us (87%)
  matrix products  30.2 us (6%)
  between operations  14.2 us (3%)
  local copies, waits for them, and re-layouts  13.5 us (3%)
  other arithmetic  6.48 us (1%)
    pallas_call x1, Pallas kernels, front_all(): pl.pallas_call(functools.partial(front, ways), out_shape=(made(BF16, widt...  184 us
    pallas_call x1, Pallas kernels, close_all(): pl.pallas_call(functools.partial(closing, ways), out_shape=(jax.ShapeDtyp...  113 us
    pallas_call x1, Pallas kernels, turn_all(): pl.pallas_call(functools.partial(turning, ways, inside), out_shape=tuple(...  93.3 us
    pallas_call x1, Pallas kernels, reverse_all(): pl.pallas_call(functools.partial(reversing, ways), out_shape=(jax.ShapeDt...  35.8 us
    dot_general x2, matrix products, contract_cols(): lax.dot_general(left, right, (((1,), (1,)), ((), ())), preferred_element_...  18.6 us
    dot_general x1, matrix products, dot(): return jnp.dot(left, right, preferred_element_type=F32)  11.7 us
  transfers between devices with their start and end apart: 2, of which 0 were waited for; matrix products, arithmetic and copies ran while one was open for 5% of the time, Pallas kernels for 68%

profile of v7, /device:TPU:0, one launch (start us, length us, event | category | flops | bytes accessed | tf_op | source)
XLA Modules:
  0.0 491.2 jit_solution(5635171097467395337)
XLA Ops:
  7.2 0.0 all-gather.2.cloned.1.call-start
  7.2 0.7 all-gather.2.cloned.1.call-update
  7.9 0.0 reduce-scatter.2.cloned.1.call-start
  8.0 0.7 reshape.255
  8.7 0.7 concatenate.6
  9.5 0.6 pad_convert_fusion.small_ref
  10.1 1.0 fusion.4
  11.1 0.9 pad_maximum_fusion.1.table_ref
  12.0 184.3 %shard_map.211 = (bf16[2048,1536]{1,0:T(8,128)(2,1)}, bf16[512,2048]{1,0:T(8,128)(2,1)}, bf16[512,1536]{1,0:T(8,128)(2,1)}, bf16[512,512]{1,0:T(8,128)(2,1)}, f3...) custom-call(bf16[64,6144]{1,0:T(8,128)(2,1)} %qkv_weight_ref.1, ...), custom_call_target="tpu_custom_call" | custom-call | bytes 540000000 | tf_op jit(solution)/shard_map/pallas_call | solution.py:1369
  196.3 1.5 fusion.13
  197.8 11.7 %fusion.14 = f32[1024,1408]{1,0:T(8,128)} fusion(bf16[1024,2048]{1,0:T(8,128)(2,1)} %bitcast.39, bf16[2048,1408]{1,0:T(8,128)(2,1)} %bitcast.61), kind=kOutput, calls=%fused_computation.40 | convolution fusion | flops 5905580032 | bytes 15728640 | tf_op jit(solution)/shard_map/dot_general | solution.py:31
  209.5 0.0 all-gather.2.cloned.1.call-done.rest_1_
  209.5 0.0 slice-start
  209.5 0.0 slice-start.1
  209.5 10.3 %multiply_convert_fusion.2 = (bf16[1024,704]{1,0:T(8,128)(2,1)S(1)}, bf16[1024,704]{1,0:T(8,128)(2,1)S(1)}, bf16[1024,704]{1,0:T(8,128)(2,1)}) fusion(f32[1024,1408]{1,0:T(8,128)} %fusion.14, bf16[1024,2048]{1,0:T(8,128)(2,1)} %bitcast.41, bf16[704,2048]{1,0:T(8,128)(2,1)} %all-gather.2.cloned.1.call-done.rest_1_), kind=kOutput, calls=%fused_computation.3 | convolution fusion | flops 2963603456 | bytes 17170432 | tf_op jit(solution)/shard_map/dot_general | solution.py:39
  219.8 0.9 pad_maximum_fusion.rest_3_
  220.7 0.0 slice-done
  220.7 0.0 slice-done.1
  220.7 0.0 copy-start
  220.7 8.3 %convolution_convert_fusion = bf16[1024,2048]{1,0:T(8,128)(2,1)} fusion(bf16[1024,1408]{1,0:T(8,128)(2,1)S(1)} %pad_maximum_fusion.rest_3_, bf16[2048,1408]{1,0:T(8,128)(2,1)S(1)} %bitcast.64), kind=kOutput, calls=%fused_computation | convolution fusion | flops 5907677184 | bytes 12845056 | tf_op jit(solution)/shard_map/dot_general | solution.py:39
  229.0 0.0 copy-done
  229.0 0.0 copy-start.7
  229.0 93.3 %shard_map.212 = (f32[128,2048]{1,0:T(8,128)}, bf16[4,128,2048]{2,1,0:T(8,128)(2,1)}, f32[8,2048]{1,0:T(8,128)}, bf16[128,2048]{1,0:T(8,128)(2,1)}, bf16[512,140...) custom-call(bf16[8,2,64,2048]{3,2,1,0:T(8,128)(2,1)} %bitcast.43, f32[128,2048]{1,0:T(8,128)} %get-tuple-element.43.resid_ref, ...), custom_call_target="tpu_custom_call" | custom-call | bytes 255000000 | tf_op jit(solution)/shard_map/pallas_call | solution.py:691
  322.3 0.0 reduce-scatter.2.cloned.1.call-update
  322.4 0.0 copy-done.7
  322.4 0.8 copy.26
  323.2 0.1 broadcast_bitcast_fusion.1
  323.3 0.0 copy-start.8
  323.3 35.8 %shard_map.213 = (bf16[512,2048]{1,0:T(8,128)(2,1)}, bf16[2048,1536]{1,0:T(8,128)(2,1)}, f32[8,1536]{1,0:T(8,128)}, bf16[8,1,64,2048]{3,2,1,0:T(8,128)(2,1)}, bf16[8,64,1408]{2,1,0:T(8,128)(2,1)}) custom-call(bf16[512,2048]{1,0:T(8,128)(2,1)} %bitcast.50, bf16[512,2048]{1,0:T(8,128)(2,1)} %bitcast.49, bf16[512,1536]{1,0:T(8,128)(2,1)} %get-tuple-element.48.qkv_ref, ...), custom_call_target="tpu_custom_call" | custom-call | bytes 135000000 | tf_op jit(solution)/shard_map/pallas_call | solution.py:852
  359.1 0.8 slice_reduce_fusion
  360.0 0.0 copy-done.8
  360.0 0.6 pad_add_fusion.sums_ref
  360.6 0.0 copy-start.4
  360.6 112.7 %shard_map.214 = (f32[64,6144]{1,0:T(8,128)}, bf16[128,2048]{1,0:T(8,128)(2,1)}, f32[8,2048]{1,0:T(8,128)}, f32[64,5632]{1,0:T(8,128)}, f32[64,5632]{1,0:T(8,128)}, /*index=5*/f32[64,2048]{1,0:T(8,128)}) custom-call(bf16[4,8,64,1536]{3,2,1,0:T(8,128)(2,1)} %bitcast.38, bf16[4,128,2048]{2,1,0:T(8,128)(2,1)} %bitcast.48, f32[8,2048]{1,0:T(8,128)} %pad_add_fusion.sums_ref, ...), custom_call_target="tpu_custom_call" | custom-call | bytes 225000000 | tf_op jit(solution)/shard_map/pallas_call | solution.py:975
  473.3 0.0 copy-start.6
  473.3 0.0 copy-start.1
  473.3 1.0 slice.37
  474.4 0.6 dynamic_slice.7
  475.0 0.7 constant_dynamic-slice_fusion
  475.8 0.5 slice_bitcast_fusion
  476.3 0.0 reduce-scatter.2.cloned.1.call-done
  476.3 2.4 convert_element_type.55
  478.7 0.0 copy-start.5
  478.7 0.0 copy-done.4
  478.7 0.0 copy-start.3
  478.7 0.8 copy.36
  479.5 0.0 copy-done.6
  479.5 0.8 copy.37
  480.3 0.0 copy-done.1
  480.3 0.0 copy-start.2
  480.3 1.1 copy.38
  481.4 0.0 copy-done.5
  481.4 0.8 copy.39
  482.2 0.0 copy-done.3
  482.2 1.1 copy.40
  483.3 0.0 copy-done.2
  483.3 1.1 copy.41
  (12 shorter events, 0.1 us)
Async XLA Ops:
  7.2 202.3 %all-gather.2.cloned.1.call-start = ((), (), s32[]{:S(2)}) async-start(), calls=%async_computation.1 | async-start | bytes 3604480 | tf_op jit(solution)/shard_map/all_gather | solution.py:65
  7.9 468.4 %reduce-scatter.2.cloned.1.call-start = ((), (), s32[]{:S(2)}) async-start(), calls=%async_computation.2 | async-start | bytes 3604480 | tf_op jit(solution)/shard_map/reduce_scatter | solution.py:69
  209.5 11.2 %slice-start = ((s8[5767168]{0:T(1024)(128)(4,1)}), s8[4194304]{0:T(1024)(128)(4,1)S(1)}, s32[]{:S(2)}) async-start(s8[5767168]{0:T(1024)(128)(4,1)} %bitcast.62), calls=%async_computation.3 | async-start | bytes 8388608
  209.5 11.2 %slice-start.1 = ((s8[5767168]{0:T(1024)(128)(4,1)}), s8[1572864]{0:T(1024)(128)(4,1)S(1)}, s32[]{:S(2)}) async-start(s8[5767168]{0:T(1024)(128)(4,1)} %bitcast.62), calls=%async_computation.4 | async-start | bytes 3145728
  220.7 8.3 %copy-start = (bf16[1024,1408]{1,0:T(8,128)(2,1)}, bf16[1024,1408]{1,0:T(8,128)(2,1)S(1)}, u32[]{:S(2)}) copy-start(bf16[1024,1408]{1,0:T(8,128)(2,1)S(1)} %pad_maximum_fusion.rest_3_) | copy-start | bytes 8650756
  229.0 93.4 %copy-start.7 = (f32[512,128]{1,0:T(8,128)S(1)}, f32[512,128]{1,0:T(8,128)}, u32[]{:S(2)}) copy-start(f32[512,128]{1,0:T(8,128)} %get-tuple-element.49) | copy-start | bytes 786436
  323.3 36.7 %copy-start.8 = (f32[8,2048]{1,0:T(8,128)S(1)}, f32[8,2048]{1,0:T(8,128)}, u32[]{:S(2)}) copy-start(f32[8,2048]{1,0:T(8,128)} %get-tuple-element.56) | copy-start | bytes 196612
  360.6 118.0 %copy-start.4 = (bf16[128,2048]{1,0:T(8,128)(2,1)S(1)}, bf16[128,2048]{1,0:T(8,128)(2,1)}, u32[]{:S(2)}) copy-start(bf16[128,2048]{1,0:T(8,128)(2,1)} %get-tuple-element.45) | copy-start | bytes 1572868
  473.3 6.1 %copy-start.6 = (bf16[128,2048]{1,0:T(8,128)(2,1)S(1)}, bf16[128,2048]{1,0:T(8,128)(2,1)}, u32[]{:S(2)}) copy-start(bf16[128,2048]{1,0:T(8,128)(2,1)} %get-tuple-element.61) | copy-start | bytes 1572868
  473.3 6.9 %copy-start.1 = (f32[64,6144]{1,0:T(8,128)S(1)}, f32[64,6144]{1,0:T(8,128)}, u32[]{:S(2)}) copy-start(f32[64,6144]{1,0:T(8,128)} %get-tuple-element.98) | copy-start | bytes 4718596
  478.7 2.7 copy-start.5
  478.7 3.5 copy-start.3
  480.3 3.0 copy-start.2
Sparse Core Ops, SparseCore 0:
  9.8 63.0 all-gather.1
  322.5 43.6 reduce-scatter.1
